TPU v7x, 32 devices: a whole 2x2x4 slice. The times are simulated.
32 devices in a mesh: groups: 1, rail: 16 (over z, y, x), node: 2 (over core).
Axes of the slice: x: 2, y: 2, z: 4, core: 2. Of those that a mesh axis runs over, the one named last changes fastest.
Arguments:
- tokens: bfloat16 [512, 7168], P(('groups', 'rail', 'node')), may hold values from -6 to 6
- routes: int32 [512, 2], P(('groups', 'rail', 'node')), may hold values from 0 to 3, all different within a row; in each aligned block of 16 rows (0 to 15, 16 to 31, ...) at most 12 rows name the same one
- route_weight: int32 [512, 2], P(('groups', 'rail', 'node')), may hold values from 1 to 255
- gate_weight: bfloat16 [16, 2, 7168, 256], P('rail', 'node'), may hold values from -0.0625 to 0.0625
- up_weight: bfloat16 [16, 2, 7168, 256], P('rail', 'node'), may hold values from -0.0625 to 0.0625
- down_weight: bfloat16 [16, 2, 256, 7168], P('rail', 'node'), may hold values from -0.125 to 0.125
Outputs:
- moe_out: bfloat16 [512, 7168], P(('groups', 'rail', 'node'))
Inputs may be any that keep to these rules, and one draw needn't show every extreme that they name: `routes`: each row names 2 different experts; among the 16 rows of one device no expert is named by more than 12 rows, and in some blocks of every draw an expert is named by exactly 12.
All inputs are finite; a program needn't handle non-finite values.
Results may differ from a plain program's by a relative error of at most 0.0085.
Values may be sent and summed in bfloat16 or wider, within the bound.
No kernel may reach another device: no remote copies, remote signals or barrier semaphores. Data moves between devices by JAX's collectives and lax.ppermute only.
A program may use at most 128 MiB of HBM per device.

v0:
```python
import jax
import jax.numpy as jnp
from jax import lax
from jax.sharding import PartitionSpec as P

SLICES = 8


def partner_2(block, axis, distance):
    count = lax.axis_size(axis)
    route = []
    for low in range(count):
        high = low | 1 << distance
        if high != low and high < count:
            route += [(low, high), (high, low)]
    return lax.ppermute(block, axis, route)


def shards(tokens, routes, route_weight, gate_weight, up_weight, down_weight):
    row_count, model_width = tokens.shape
    top_count = routes.shape[1]
    rail_size = lax.axis_size("rail")
    node_size = lax.axis_size("node")
    devices = rail_size * node_size
    experts = devices // SLICES
    capacity = min(row_count, 3 * row_count * top_count // (2 * experts))
    split_count = rail_size // SLICES
    piece_width = model_width // SLICES
    levels = SLICES.bit_length() - 1
    listed = routes.reshape(-1)
    onehot = (listed[:, None] == jnp.arange(experts, dtype=jnp.int32)[None, :]).astype(jnp.int32)
    earlier = jnp.cumsum(onehot, axis=0) - onehot
    slot_key = listed * capacity + jnp.sum(earlier * onehot, axis=1)
    chosen = slot_key[:, None] == jnp.arange(experts * capacity, dtype=jnp.int32)[None, :]
    chosen = chosen.reshape(row_count, top_count, experts * capacity)
    dispatch = jnp.sum(chosen.astype(jnp.bfloat16), axis=1)
    share = route_weight.astype(jnp.float32) / 256.0
    combine = jnp.sum(chosen.astype(jnp.float32) * share[:, :, None], axis=1)
    packed = jnp.einsum("te,td->ed", dispatch, tokens, preferred_element_type=jnp.float32).astype(
        jnp.bfloat16
    )
    w_gate = gate_weight[0, 0]
    w_up = up_weight[0, 0]
    w_down = down_weight[0, 0]
    rail_index = lax.axis_index("rail")

    def own_bit(bit):
        return rail_index // 2**bit % 2 == 1

    pieces = packed.reshape(split_count, node_size, capacity, SLICES, piece_width)
    pieces = pieces.transpose(0, 3, 1, 2, 4).reshape(devices, capacity, piece_width)
    assembled = lax.all_to_all(pieces, ("rail", "node"), split_axis=0, concat_axis=0, tiled=True)
    for bit in range(levels):
        partner = partner_2(assembled, "rail", bit)
        assembled = jnp.where(
            own_bit(bit),
            jnp.concatenate([partner, assembled], 2),
            jnp.concatenate([assembled, partner], 2),
        )
    rows = assembled.reshape(-1, model_width)
    gate_vals = jnp.dot(rows, w_gate, preferred_element_type=jnp.float32)
    up_vals = jnp.dot(rows, w_up, preferred_element_type=jnp.float32)
    hidden = (jax.nn.silu(gate_vals) * up_vals).astype(jnp.bfloat16)
    partial_value = jnp.dot(hidden, w_down, preferred_element_type=jnp.float32)
    partials = partial_value.reshape(assembled.shape)
    half = model_width // 2
    upper = own_bit(levels - 1)
    lower_part = partials[:, :, :half]
    upper_part = partials[:, :, half:]
    sending = jnp.where(upper, lower_part, upper_part)
    keeping = jnp.where(upper, upper_part, lower_part)
    received = partner_2(sending, "rail", levels - 1)
    current = keeping + received
    for bit in range(levels - 2, -1, -1):
        half = current.shape[2] // 2
        upper = own_bit(bit)
        lower_part = current[:, :, :half]
        upper_part = current[:, :, half:]
        sending = jnp.where(upper, lower_part, upper_part)
        keeping = jnp.where(upper, upper_part, lower_part)
        received = partner_2(sending, "rail", bit)
        current = keeping + received
    returned = lax.all_to_all(current, ("rail", "node"), split_axis=0, concat_axis=0, tiled=True)
    summed = returned.reshape(split_count, SLICES, node_size, capacity, piece_width)
    summed = summed.transpose(0, 2, 3, 1, 4).reshape(experts * capacity, model_width)
    mixed = jnp.dot(
        combine, summed, precision=lax.Precision.HIGHEST, preferred_element_type=jnp.float32
    )
    return mixed.astype(jnp.bfloat16)


def solution(mesh):
    in_specs = (
        P(("groups", "rail", "node"), None),
        P(("groups", "rail", "node"), None),
        P(("groups", "rail", "node"), None),
        P("rail", "node", None, None),
        P("rail", "node", None, None),
        P("rail", "node", None, None),
    )
    out_specs = P(("groups", "rail", "node"), None)
    return jax.shard_map(shards, mesh=mesh, in_specs=in_specs, out_specs=out_specs, check_vma=False)
```

profile of v0, /device:TPU:0, one launch (start us, length us, event | category | flops | bytes accessed | tf_op | source)
XLA Modules:
  0.0 447.2 jit_solution(17365011079022647936)
XLA Ops:
  0.0 0.0 copy-start
  0.0 0.8 copy.70
  0.8 0.1 eq.48
  0.9 0.1 fusion.8
  1.0 0.1 reduce_window_sum.11
  1.0 0.2 select_reduce_fusion.1
  1.2 0.1 reduce_sum.33
  1.3 0.1 copy.71
  1.4 0.7 multiply_add_fusion
  2.1 0.1 fusion.9
  2.2 0.0 copy-done
  2.2 0.4 convolution_convert_fusion
  2.5 0.1 copy.88
  2.6 0.5 copy.93
  3.2 0.2 copy.87
  3.4 30.5 %all_to_all.10 = bf16[32,12,896]{2,1,0:T(8,128)(2,1)S(1)} all-to-all(bf16[32,12,896]{2,1,0:T(8,128)(2,1)S(1)} %bitcast.32), channel_id=1, replica_groups=mesh['groups'=1,'rail'=16,'node'=2] {'rail','node'}, dimensions={0} | all-to-all | bytes 1376256 | tf_op jit(solution)/shard_map/all_to_all | solution.py:52
  33.9 0.1 copy.74
  34.0 1.5 collective-permute-start
  35.6 15.7 %collective-permute-done = bf16[32,12,896]{2,0,1:T(8,128)(2,1)S(1)} collective-permute-done((bf16[32,12,896]{2,0,1:T(8,128)(2,1)S(1)}, bf16[32,12,896]{2,0,1:T(8,128)(2,1)S(1)}, u32[]{:S(2)}, u32[]{:S(2)}) %collective-permute-start) | collective-permute-done | bytes 688160 | tf_op jit(solution)/shard_map/ppermute | solution.py:16
  51.3 0.2 copy.75
  51.5 0.5 maximum_select_fusion.3
  52.1 1.2 copy-done.3
  53.3 0.4 copy.77
  53.7 1.5 collective-permute-start.1
  55.2 29.8 %collective-permute-done.1 = bf16[32,12,1792]{2,0,1:T(8,128)(2,1)} collective-permute-done((bf16[32,12,1792]{2,0,1:T(8,128)(2,1)S(1)}, bf16[32,12,1792]{2,0,1:T(8,128)(2,1)}, u32[]{:S(2)}, u32[]{:S(2)}) %collective-permute-start.1) | collective-permute-done | bytes 1376288 | tf_op jit(solution)/shard_map/ppermute | solution.py:16
  84.9 2.1 copy.78
  87.0 1.2 maximum_select_fusion.1
  88.2 3.1 copy.80
  91.3 1.6 collective-permute-start.2
  92.9 0.2 concatenate.47
  93.1 1.3 concatenate.46
  94.4 1.5 maximum_select_fusion.4
  95.8 1.3 concatenate.45
  97.1 4.5 %maximum_select_fusion.2 = bf16[384,3584]{1,0:T(8,128)(2,1)} fusion(bf16[384,1792]{1,0:T(8,128)(2,1)} %maximum_select_fusion.4, bf16[384,1792]{1,0:T(8,128)(2,1)} %concatenate.45, pred[]{:T(512)S(6)} %eq.56), kind=kLoop, calls=%fused_computation.12 | loop fusion | flops 12386304 | bytes 5505025 | tf_op jit(solution)/shard_map/jit(_where)/select_n | solution.py:55
  101.6 49.7 %collective-permute-done.2 = bf16[32,12,3584]{2,0,1:T(8,128)(2,1)} collective-permute-done((bf16[32,12,3584]{2,0,1:T(8,128)(2,1)}, bf16[32,12,3584]{2,0,1:T(8,128)(2,1)}, u32[]{:S(2)}, u32[]{:S(2)}) %collective-permute-start.2) | collective-permute-done | bytes 2752544 | tf_op jit(solution)/shard_map/ppermute | solution.py:16
  151.4 5.2 %copy.81 = bf16[32,12,3584]{2,1,0:T(8,128)(2,1)} copy(bf16[32,12,3584]{2,0,1:T(8,128)(2,1)} %collective-permute-done.2) | data formatting | bytes 5505024 | tf_op jit(solution)/shard_map/ppermute | solution.py:16
  156.6 5.4 %concatenate.44 = bf16[384,3584]{1,0:T(8,128)(2,1)} reshape(bf16[32,12,3584]{2,1,0:T(8,128)(2,1)} %copy.81) | data formatting | bytes 5505024 | tf_op jit(solution)/shard_map/concatenate | solution.py:57
  161.9 6.4 %fusion.4 = f32[384,256]{1,0:T(8,128)S(1)} fusion(bf16[1,1,7168,256]{3,2,1,0:T(8,128)(2,1)} %param.9, bf16[384,3584]{1,0:T(8,128)(2,1)} %maximum_select_fusion.2, bf16[384,3584]{1,0:T(8,128)(2,1)} %concatenate.44, pred[]{:T(512)S(6)} %eq.57), kind=kOutput, calls=%fused_computation.10 | convolution fusion | flops 1434058752 | bytes 9568257 | tf_op jit(solution)/shard_map/dot_general | solution.py:61
  168.4 0.0 copy-done.6
  168.4 0.4 copy-done.7
  168.8 1.1 copy-done.9
  169.9 3.1 multiply_convert_fusion
  173.0 3.6 fusion
  176.6 0.8 slice_select_fusion
  177.5 1.8 collective-permute-start.3
  179.3 116.4 %collective-permute-done.3 = f32[32,12,3584]{2,0,1:T(8,128)} collective-permute-done((f32[32,12,3584]{2,0,1:T(8,128)S(1)}, f32[32,12,3584]{2,0,1:T(8,128)}, u32[]{:S(2)}, u32[]{:S(2)}) %collective-permute-start.3) | collective-permute-done | bytes 5505056 | tf_op jit(solution)/shard_map/ppermute | solution.py:16
  295.7 6.6 %select_add_fusion = f32[32,12,3584]{2,0,1:T(8,128)} fusion(f32[32,12,3584]{2,0,1:T(8,128)} %collective-permute-done.3, f32[32,12,7168]{2,0,1:T(8,128)S(1)} %fusion, pred[]{:T(512)S(6)} %eq.57), kind=kLoop, calls=%fused_computation.3 | loop fusion | flops 2752512 | bytes 22020096 | tf_op jit(solution)/shard_map/add | solution.py:73
  302.3 3.1 slice_select_fusion.1
  305.4 0.9 collective-permute-start.4
  306.3 57.3 %collective-permute-done.4 = f32[32,12,1792]{2,0,1:T(8,128)S(1)} collective-permute-done((f32[32,12,1792]{2,0,1:T(8,128)S(1)}, f32[32,12,1792]{2,0,1:T(8,128)S(1)}, u32[]{:S(2)}, u32[]{:S(2)}) %collective-permute-start.4) | collective-permute-done | bytes 2752544 | tf_op jit(solution)/shard_map/ppermute | solution.py:16
  363.7 0.5 select_add_fusion.1
  364.2 0.2 slice_select_fusion.2
  364.4 4.0 collective-permute-start.5
  368.3 26.8 %collective-permute-done.5 = f32[32,12,896]{2,0,1:T(8,128)S(1)} collective-permute-done((f32[32,12,896]{2,0,1:T(8,128)S(1)}, f32[32,12,896]{2,0,1:T(8,128)S(1)}, u32[]{:S(2)}, u32[]{:S(2)}) %collective-permute-start.5) | collective-permute-done | bytes 1376288 | tf_op jit(solution)/shard_map/ppermute | solution.py:16
  395.1 0.2 select_add_fusion.2
  395.3 0.0 copy-start.8
  395.3 2.1 copy.85
  397.4 4.2 all-to-all-start.1
  401.7 0.1 select_reduce_fusion
  401.7 43.0 %all-to-all-done.1 = f32[32,12,896]{2,1,0:T(8,128)S(1)} async-done(((f32[32,12,896]{2,1,0:T(8,128)}), f32[32,12,896]{2,1,0:T(8,128)S(1)}, u32[]{:S(2)}, u32[]{:S(2)}) %all-to-all-start.1) | async-done | bytes 1376288 | tf_op jit(solution)/shard_map/all_to_all | solution.py:83
  444.7 0.8 copy.86
  445.5 0.2 copy.89
  445.8 1.5 convolution_convert_fusion.1
  447.2 0.0 copy-done.1
  (14 shorter events, 0.1 us)
Async XLA Ops:
  0.0 2.2 copy-start
  34.0 17.2 %collective-permute-start = (bf16[32,12,896]{2,0,1:T(8,128)(2,1)S(1)}, bf16[32,12,896]{2,0,1:T(8,128)(2,1)S(1)}, u32[]{:S(2)}, u32[]{:S(2)}) collective-permute-start(bf16[32,12,896]{2,0,1:T(8,128)(2,1)S(1)} %copy.74), channel_id=1, source_target_pairs={{0,2},{2,0},{4,6},{6,4},{8,10},{10,8},{12,14},{14,12},{16,18},{18,... | collective-permute-start | bytes 2064392 | tf_op jit(solution)/shard_map/ppermute | solution.py:16
  51.5 2.2 copy-start.5
  52.0 1.2 copy-start.3
  53.7 31.2 %collective-permute-start.1 = (bf16[32,12,1792]{2,0,1:T(8,128)(2,1)S(1)}, bf16[32,12,1792]{2,0,1:T(8,128)(2,1)}, u32[]{:S(2)}, u32[]{:S(2)}) collective-permute-start(bf16[32,12,1792]{2,0,1:T(8,128)(2,1)S(1)} %copy.77), channel_id=1, source_target_pairs={{0,4},{4,0},{2,6},{6,2},{8,12},{12,8},{10,14},{14,10},{16,20},{20,... | collective-permute-start | bytes 4128776 | tf_op jit(solution)/shard_map/ppermute | solution.py:16
  55.2 31.9 %copy-start.4 = (bf16[32,12,1792]{2,1,0:T(8,128)(2,1)S(1)}, bf16[32,12,1792]{2,1,0:T(8,128)(2,1)}, u32[]{:S(2)}) copy-start(bf16[32,12,1792]{2,1,0:T(8,128)(2,1)} %copy-done.3) | copy-start | bytes 4128772
  91.3 60.1 %collective-permute-start.2 = (bf16[32,12,3584]{2,0,1:T(8,128)(2,1)}, bf16[32,12,3584]{2,0,1:T(8,128)(2,1)}, u32[]{:S(2)}, u32[]{:S(2)}) collective-permute-start(bf16[32,12,3584]{2,0,1:T(8,128)(2,1)} %copy.80), channel_id=1, source_target_pairs={{0,8},{8,0},{2,10},{10,2},{4,12},{12,4},{6,14},{14,6},{16,24},{24,... | collective-permute-start | bytes 8257544 | tf_op jit(solution)/shard_map/ppermute | solution.py:16
  161.9 6.4 %copy-start.6 = (bf16[384,3584]{1,0:T(8,128)(2,1)S(1)}, bf16[384,3584]{1,0:T(8,128)(2,1)}, u32[]{:S(2)}) copy-start(bf16[384,3584]{1,0:T(8,128)(2,1)} %maximum_select_fusion.2) | copy-start | bytes 8257540
  161.9 6.9 %copy-start.7 = (bf16[384,3584]{1,0:T(8,128)(2,1)S(1)}, bf16[384,3584]{1,0:T(8,128)(2,1)}, u32[]{:S(2)}) copy-start(bf16[384,3584]{1,0:T(8,128)(2,1)} %concatenate.44) | copy-start | bytes 8257540
  161.9 7.9 %copy-start.9 = (bf16[1,1,7168,256]{3,2,1,0:T(8,128)(2,1)S(1)}, bf16[1,1,7168,256]{3,2,1,0:T(8,128)(2,1)}, u32[]{:S(2)}) copy-start(bf16[1,1,7168,256]{3,2,1,0:T(8,128)(2,1)} %param.10) | copy-start | bytes 11010052
  177.5 118.2 %collective-permute-start.3 = (f32[32,12,3584]{2,0,1:T(8,128)S(1)}, f32[32,12,3584]{2,0,1:T(8,128)}, u32[]{:S(2)}, u32[]{:S(2)}) collective-permute-start(f32[32,12,3584]{2,0,1:T(8,128)S(1)} %slice_select_fusion), channel_id=1, source_target_pairs={{0,8},{8,0},{2,10},{10,2},{4,12},{12,4},{6,14},{14,6},{16,24},{24,... | collective-permute-start | bytes 16515080 | tf_op jit(solution)/shard_map/ppermute | solution.py:16
  302.3 61.4 %copy-start.2 = (f32[32,12,3584]{2,0,1:T(8,128)S(1)}, f32[32,12,3584]{2,0,1:T(8,128)}, u32[]{:S(2)}) copy-start(f32[32,12,3584]{2,0,1:T(8,128)} %select_add_fusion) | copy-start | bytes 16515076
  305.4 58.2 %collective-permute-start.4 = (f32[32,12,1792]{2,0,1:T(8,128)S(1)}, f32[32,12,1792]{2,0,1:T(8,128)S(1)}, u32[]{:S(2)}, u32[]{:S(2)}) collective-permute-start(f32[32,12,1792]{2,0,1:T(8,128)S(1)} %slice_select_fusion.1), channel_id=1, source_target_pairs={{0,4},{4,0},{2,6},{6,2},{8,12},{12,8},{10,14},{14,10},{16,20},{20,... | collective-permute-start | bytes 8257544 | tf_op jit(solution)/shard_map/ppermute | solution.py:16
  364.4 30.7 %collective-permute-start.5 = (f32[32,12,896]{2,0,1:T(8,128)S(1)}, f32[32,12,896]{2,0,1:T(8,128)S(1)}, u32[]{:S(2)}, u32[]{:S(2)}) collective-permute-start(f32[32,12,896]{2,0,1:T(8,128)S(1)} %slice_select_fusion.2), channel_id=1, source_target_pairs={{0,2},{2,0},{4,6},{6,4},{8,10},{10,8},{12,14},{14,12},{16,18},{18,... | collective-permute-start | bytes 4128776 | tf_op jit(solution)/shard_map/ppermute | solution.py:16
  395.3 6.3 %copy-start.8 = (s32[16,2]{0,1:T(2,128)S(1)}, s32[16,2]{0,1:T(2,128)}, u32[]{:S(2)}) copy-start(s32[16,2]{0,1:T(2,128)} %param.8) | copy-start | bytes 388
  397.4 47.3 %all-to-all-start.1 = ((f32[32,12,896]{2,1,0:T(8,128)}), f32[32,12,896]{2,1,0:T(8,128)S(1)}, u32[]{:S(2)}, u32[]{:S(2)}) async-start(f32[32,12,896]{2,1,0:T(8,128)} %copy.85), calls=%async_computation.1 | async-start | bytes 3670016 | tf_op jit(solution)/shard_map/all_to_all | solution.py:83
  444.7 2.5 copy-start.1
where the time goes:
time: 448 us; the launch traced here: 447 us
  waiting for transfers between devices  339 us (76%)
  blocking collectives  30.5 us (7%)
  local copies, waits for them, and re-layouts  27 us (6%)
  other arithmetic  20.3 us (5%)
  starting transfers between devices  15.5 us (3%)
  matrix products  15 us (3%)
    ppermute x6, waiting for transfers between devices, partner_2(): return lax.ppermute(block, axis, route)  296 us
    all_to_all x1, waiting for transfers between devices, shards(): lax.all_to_all(current, ('rail', 'node'), split_axis=0, concat_axis=0, ti...  43 us
    all_to_all x1, blocking collectives, shards(): lax.all_to_all(pieces, ('rail', 'node'), split_axis=0, concat_axis=0, til...  30.5 us
    ppermute x6, starting transfers between devices, partner_2(): return lax.ppermute(block, axis, route)  11.3 us
  transfers between devices with their start and end apart: 7, of which 7 were waited for; matrix products, arithmetic and copies ran while one was open for 2% of the time, Pallas kernels for 0%

commit v1 on v0

v1 whole, which is shorter than its diff:
```python
import jax
import jax.numpy as jnp
from jax import lax
from jax.sharding import PartitionSpec as P

SLICES = 8
LANES = 128
PLANE = 4


def send(block, target):
    rails, nodes = lax.axis_size("rail"), lax.axis_size("node")
    route = []
    for rail in range(rails):
        for node in range(nodes):
            rail_to, node_to = target(rail, node)
            route.append((rail * nodes + node, rail_to * nodes + node_to))
    return lax.ppermute(block, ("rail", "node"), route)


def first_partner(rail, node):
    return rail ^ (1 if node % 2 == 0 else 2), node


def second_partner(rail, node):
    return rail ^ (2 if node % 2 == 0 else 1), node


def layer_shift(layers, count):
    def target(rail, node):
        return (rail // PLANE + count) % layers * PLANE + rail % PLANE, node

    return target


def node_shift(nodes, count):
    return lambda rail, node: (rail, (node + count) % nodes)


def shards(tokens, routes, route_weight, gate_weight, up_weight, down_weight):
    row_count, model_width = tokens.shape
    nodes = lax.axis_size("node")
    layers = lax.axis_size("rail") // PLANE
    node = lax.axis_index("node")
    first_expert = lax.axis_index("rail") // SLICES * nodes

    weights = []
    for count in range(nodes):
        held = (gate_weight[0, 0], up_weight[0, 0], down_weight[0, 0])
        if count:
            held = tuple(send(w, node_shift(nodes, count)) for w in held)
        weights.append((first_expert + (node - count) % nodes, held))

    lanes = jnp.arange(LANES, dtype=jnp.int32)
    share = route_weight.astype(jnp.float32) / 256.0
    named = routes[:, :, None] == lanes[None, None, :]
    coef = jnp.sum(jnp.where(named, share[:, :, None], 0.0), axis=1).astype(jnp.bfloat16)
    own = jnp.concatenate([tokens, coef], axis=1)

    def experts_of(block):
        rows = block[:, :model_width]
        coefs = block[:, model_width:].astype(jnp.float32)
        total = None
        for expert, (w_gate, w_up, w_down) in weights:
            mine = jnp.sum(jnp.where(lanes[None, :] == expert, coefs, 0.0), axis=1, keepdims=True)
            gate_vals = jnp.dot(rows, w_gate, preferred_element_type=jnp.float32)
            up_vals = jnp.dot(rows, w_up, preferred_element_type=jnp.float32)
            hidden = (jax.nn.silu(gate_vals) * up_vals * mine).astype(jnp.bfloat16)
            part = jnp.dot(hidden, w_down, preferred_element_type=jnp.float32)
            total = part if total is None else total + part
        return total

    shifts = sorted(range(layers), key=lambda count: min(count, layers - count))
    units = [(count, send(own, layer_shift(layers, count)) if count else own) for count in shifts]
    result = None
    for count, unit in units:
        pair = jnp.concatenate([unit, send(unit, first_partner)], axis=0)
        block = jnp.concatenate([pair, send(pair, second_partner)], axis=0)
        out = experts_of(block)
        out = out[: 2 * row_count] + send(out[2 * row_count :].astype(jnp.bfloat16), second_partner)
        out = out[:row_count] + send(out[row_count:].astype(jnp.bfloat16), first_partner)
        if count:
            out = send(out.astype(jnp.bfloat16), layer_shift(layers, -count)).astype(jnp.float32)
        result = out if result is None else result + out
    return result.astype(jnp.bfloat16)


def solution(mesh):
    rows = P(("groups", "rail", "node"), None)
    weights = P("rail", "node", None, None)
    return jax.shard_map(
        shards,
        mesh=mesh,
        in_specs=(rows, rows, rows, weights, weights, weights),
        out_specs=rows,
        check_vma=False,
    )
```

time: 448 us -> 177 us (0.40)
  waiting for transfers between devices: 339 us -> 61.4 us
  matrix products: 15 us -> 70.2 us
  blocking collectives: 30.5 us -> 0 us
  local copies, waits for them, and re-layouts: 27 us -> 7.08 us
  starting transfers between devices: 15.5 us -> 29.2 us
  other arithmetic: 20.3 us -> 8.59 us
    ppermute x6 -> x25, waiting for transfers between devices: 296 us -> 61.4 us  [send(): return lax.ppermute(block, ('rail', 'node'), route)]
    dot_general x5 -> x16, matrix products: 15 us -> 70.2 us  [the longest x8 55.7 us: experts_of(): part = jnp.dot(hidden, w_down, preferred_element_type=jnp.float32)]
    all_to_all x1 -> x0, waiting for transfers between devices: 43 us -> none  [shards(): lax.all_to_all(current, ('rail', 'node'), split_axis=0, concat_axis=0, ti...]
    all_to_all x1 -> x0, blocking collectives: 30.5 us -> none  [shards(): lax.all_to_all(pieces, ('rail', 'node'), split_axis=0, concat_axis=0, til...]
    ppermute x6 -> x25, starting transfers between devices: 11.3 us -> 29.2 us  [send(): return lax.ppermute(block, ('rail', 'node'), route)]
    select_n x7 -> x0, other arithmetic: 11.8 us -> none  [the longest x4 7.7 us: shards(): jnp.where(own_bit(bit), jnp.concatenate([partner, assembled], 2), jnp.con...]
    concatenate x4 -> x3, local copies, waits for them, and re-layouts: 8.07 us -> 0.11 us  [shards(): block = jnp.concatenate([pair, send(pair, second_partner)], axis=0)]
    ppermute x3 -> x0, local copies, waits for them, and re-layouts: 7.53 us -> none  [partner_2(): return lax.ppermute(block, axis, route)]
  transfers between devices with their start and end apart: 7 -> 25, of which waited for: 7 -> 13; matrix products, arithmetic and copies ran while one was open for 2% -> 41% of each run, Pallas kernels for 0% -> 0%
where the time goes in v1:
time: 177 us
  matrix products  70.2 us (40%)
  waiting for transfers between devices  61.4 us (35%)
  starting transfers between devices  29.2 us (16%)
  other arithmetic  8.59 us (5%)
  local copies, waits for them, and re-layouts  7.08 us (4%)
    ppermute x25, waiting for transfers between devices, send(): return lax.ppermute(block, ('rail', 'node'), route)  61.4 us
    dot_general x8, matrix products, experts_of(): part = jnp.dot(hidden, w_down, preferred_element_type=jnp.float32)  55.7 us
    ppermute x25, starting transfers between devices, send(): return lax.ppermute(block, ('rail', 'node'), route)  29.2 us
    dot_general x8, matrix products, experts_of(): gate_vals = jnp.dot(rows, w_gate, preferred_element_type=jnp.float32)  14.6 us
    slice x4, local copies, waits for them, and re-layouts, shards(): out[2 * row_count:].astype(jnp.bfloat16)  6.72 us
    add x4, other arithmetic, shards(): out[:2 * row_count]  3.92 us
  transfers between devices with their start and end apart: 25, of which 13 were waited for; matrix products, arithmetic and copies ran while one was open for 41% of the time, Pallas kernels for 0%

profile of v1, /device:TPU:0, one launch (start us, length us, event | category | flops | bytes accessed | tf_op | source)
XLA Modules:
  0.0 176.8 jit_solution(13901326886131378831)
XLA Ops:
  0.0 0.7 convert_multiply_fusion
  0.7 0.8 select_reduce_fusion
  1.5 1.0 pad_maximum_fusion.5
  2.4 3.0 %collective-permute-start = (bf16[16,7296]{1,0:T(8,128)(2,1)S(1)}, bf16[16,7296]{1,0:T(8,128)(2,1)S(1)}, u32[]{:S(2)}, u32[]{:S(2)}) collective-permute-start(bf16[16,7296]{1,0:T(8,128)(2,1)S(1)} %pad_maximum_fusion.5), channel_id=1, source_target_pairs={{0,2},{1,5},{2,0},{3,7},{4,6},{5,1},{6,4},{7,3},{8,10},{9,13},{10,... | collective-permute-start | bytes 700424 | tf_op jit(solution)/shard_map/ppermute | solution.py:18
  5.5 1.6 collective-permute-start.7
  7.0 2.2 %collective-permute-start.13 = (bf16[16,7296]{1,0:T(8,128)(2,1)S(1)}, bf16[16,7296]{1,0:T(8,128)(2,1)S(1)}, u32[]{:S(2)}, u32[]{:S(2)}) collective-permute-start(bf16[16,7296]{1,0:T(8,128)(2,1)S(1)} %pad_maximum_fusion.5), channel_id=1, source_target_pairs={{0,24},{1,25},{2,26},{3,27},{4,28},{5,29},{6,30},{7,31},{8,0},{9,1... | collective-permute-start | bytes 700424 | tf_op jit(solution)/shard_map/ppermute | solution.py:18
  9.3 0.8 collective-permute-start.19
  10.1 0.6 collective-permute-start.3
  10.7 1.0 pad_maximum_fusion.1
  11.6 4.2 %collective-permute-done.7 = bf16[16,7296]{1,0:T(8,128)(2,1)S(1)} collective-permute-done((bf16[16,7296]{1,0:T(8,128)(2,1)S(1)}, bf16[16,7296]{1,0:T(8,128)(2,1)S(1)}, u32[]{:S(2)}, u32[]{:S(2)}) %collective-permute-start.7) | collective-permute-done | bytes 233504 | tf_op jit(solution)/shard_map/ppermute | solution.py:18
  15.9 3.0 %collective-permute-done.13 = bf16[16,7296]{1,0:T(8,128)(2,1)S(1)} collective-permute-done((bf16[16,7296]{1,0:T(8,128)(2,1)S(1)}, bf16[16,7296]{1,0:T(8,128)(2,1)S(1)}, u32[]{:S(2)}, u32[]{:S(2)}) %collective-permute-start.13) | collective-permute-done | bytes 233504 | tf_op jit(solution)/shard_map/ppermute | solution.py:18
  19.0 0.7 collective-permute-start.1
  19.7 9.8 %collective-permute-done.19 = bf16[16,7296]{1,0:T(8,128)(2,1)S(1)} collective-permute-done((bf16[16,7296]{1,0:T(8,128)(2,1)S(1)}, bf16[16,7296]{1,0:T(8,128)(2,1)S(1)}, u32[]{:S(2)}, u32[]{:S(2)}) %collective-permute-start.19) | collective-permute-done | bytes 233504 | tf_op jit(solution)/shard_map/ppermute | solution.py:18
  29.5 1.5 collective-permute-start.8
  31.0 4.6 %collective-permute-done.8 = bf16[16,7296]{1,0:T(8,128)(2,1)S(1)} collective-permute-done((bf16[16,7296]{1,0:T(8,128)(2,1)S(1)}, bf16[16,7296]{1,0:T(8,128)(2,1)S(1)}, u32[]{:S(2)}, u32[]{:S(2)}) %collective-permute-start.8) | collective-permute-done | bytes 233504 | tf_op jit(solution)/shard_map/ppermute | solution.py:18
  35.6 1.5 collective-permute-start.14
  37.1 4.5 %collective-permute-done.14 = bf16[16,7296]{1,0:T(8,128)(2,1)S(1)} collective-permute-done((bf16[16,7296]{1,0:T(8,128)(2,1)S(1)}, bf16[16,7296]{1,0:T(8,128)(2,1)S(1)}, u32[]{:S(2)}, u32[]{:S(2)}) %collective-permute-start.14) | collective-permute-done | bytes 233504 | tf_op jit(solution)/shard_map/ppermute | solution.py:18
  41.7 1.5 collective-permute-start.20
  43.2 4.8 %collective-permute-done.20 = bf16[16,7296]{1,0:T(8,128)(2,1)S(1)} collective-permute-done((bf16[16,7296]{1,0:T(8,128)(2,1)S(1)}, bf16[16,7296]{1,0:T(8,128)(2,1)S(1)}, u32[]{:S(2)}, u32[]{:S(2)}) %collective-permute-start.20) | collective-permute-done | bytes 233504 | tf_op jit(solution)/shard_map/ppermute | solution.py:18
  48.0 0.6 collective-permute-start.9
  48.7 1.4 collective-permute-start.15
  50.2 0.8 fusion.30
  51.0 5.6 %collective-permute-done.9 = bf16[32,7296]{1,0:T(8,128)(2,1)S(1)} collective-permute-done((bf16[32,7296]{1,0:T(8,128)(2,1)S(1)}, bf16[32,7296]{1,0:T(8,128)(2,1)S(1)}, u32[]{:S(2)}, u32[]{:S(2)}) %collective-permute-start.9) | collective-permute-done | bytes 466976 | tf_op jit(solution)/shard_map/ppermute | solution.py:18
  56.5 0.6 collective-permute-start.21
  57.2 4.3 %collective-permute-done.15 = bf16[32,7296]{1,0:T(8,128)(2,1)S(1)} collective-permute-done((bf16[32,7296]{1,0:T(8,128)(2,1)S(1)}, bf16[32,7296]{1,0:T(8,128)(2,1)S(1)}, u32[]{:S(2)}, u32[]{:S(2)}) %collective-permute-start.15) | collective-permute-done | bytes 466976 | tf_op jit(solution)/shard_map/ppermute | solution.py:18
  61.6 5.0 %collective-permute-done.21 = bf16[32,7296]{1,0:T(8,128)(2,1)S(1)} collective-permute-done((bf16[32,7296]{1,0:T(8,128)(2,1)S(1)}, bf16[32,7296]{1,0:T(8,128)(2,1)S(1)}, u32[]{:S(2)}, u32[]{:S(2)}) %collective-permute-start.21) | collective-permute-done | bytes 466976 | tf_op jit(solution)/shard_map/ppermute | solution.py:18
  66.6 0.2 fusion.40
  66.7 0.7 fusion.22
  67.5 0.8 fusion.14
  68.3 0.8 fusion.6
  69.0 7.0 %fusion.56 = f32[64,7168]{1,0:T(8,128)} fusion(f32[64,256]{1,0:T(8,128)S(1)} %fusion.22, bf16[64,7296]{1,0:T(8,128)(2,1)} %copy-done.1, f32[64]{0:T(128)S(1)} %get-tuple-element.13, bf16[1,1,256,7168]{3,2,1,0:T(8,128)(2,1)} %param.11, bf16[1,1,7168,256]{3,2,1,0:T(8,128)(2,1)} %param.10), kind=kOutput, calls=%fused_computation.90 | convolution fusion | flops 469876736 | bytes 10158336 | tf_op jit(solution)/shard_map/dot_general | solution.py:69
  76.0 6.7 %fusion.65 = f32[64,7168]{1,0:T(8,128)} fusion(f32[64,256]{1,0:T(8,128)S(1)} %fusion.14, bf16[64,7296]{1,0:T(8,128)(2,1)S(1)} %constant_dynamic-update-slice_fusion.3, f32[64]{0:T(128)S(1)} %get-tuple-element.15, bf16[1,1,256,7168]{3,2,1,0:T(8,128)(2,1)} %param.11, bf16[1,1,7168,256]{3,2,1,0:T(8,128)(2,1)} %param.10), kind=kOutput, calls=%fused_computation.91 | convolution fusion | flops 469876736 | bytes 10158592 | tf_op jit(solution)/shard_map/dot_general | solution.py:69
  82.7 6.7 %fusion.74 = f32[64,7168]{1,0:T(8,128)} fusion(f32[64,256]{1,0:T(8,128)S(1)} %fusion.6, bf16[64,7296]{1,0:T(8,128)(2,1)S(1)} %constant_dynamic-update-slice_fusion.6, f32[64]{0:T(128)S(1)} %get-tuple-element.17, bf16[1,1,256,7168]{3,2,1,0:T(8,128)(2,1)} %param.11, bf16[1,1,7168,256]{3,2,1,0:T(8,128)(2,1)} %param.10), kind=kOutput, calls=%fused_computation.92 | convolution fusion | flops 469876736 | bytes 10158592 | tf_op jit(solution)/shard_map/dot_general | solution.py:69
  89.4 6.7 %fusion.47 = f32[64,7168]{1,0:T(8,128)} fusion(f32[64,256]{1,0:T(8,128)S(1)} %fusion.30, bf16[64,7296]{1,0:T(8,128)(2,1)S(1)} %pad_maximum_fusion, f32[64]{0:T(128)S(1)} %get-tuple-element.12, bf16[1,1,256,7168]{3,2,1,0:T(8,128)(2,1)} %param.11, bf16[1,1,7168,256]{3,2,1,0:T(8,128)(2,1)} %param.10), kind=kOutput, calls=%fused_computation.89 | convolution fusion | flops 469876736 | bytes 10158592 | tf_op jit(solution)/shard_map/dot_general | solution.py:69
  96.1 3.0 %fusion.18 = f32[64,256]{1,0:T(8,128)S(1)} fusion(bf16[7168,256]{1,0:T(8,128)(2,1)} %collective-permute-done.2, bf16[64,7296]{1,0:T(8,128)(2,1)} %copy-done.1), kind=kOutput, calls=%fused_computation.31 | convolution fusion | flops 234881024 | bytes 4653056 | tf_op jit(solution)/shard_map/dot_general | solution.py:66
  99.1 7.5 %convolution_add_fusion.2 = f32[64,7168]{1,0:T(8,128)} fusion(f32[64,7168]{1,0:T(8,128)} %fusion.56, bf16[256,7168]{1,0:T(8,128)(2,1)} %collective-permute-done.4, f32[64,256]{1,0:T(8,128)S(1)} %fusion.18, bf16[7168,256]{1,0:T(8,128)(2,1)} %collective-permute-done.3, bf16[64,7296]{1,0:T(8,128)(2,1)} %copy-done.1, f32[64]{0:T(128)S(1)} %get-tuple-element.14), kind=kOutput, calls=%fused_computation.2 | convolution fusion | flops 470335488 | bytes 11993344 | tf_op jit(solution)/shard_map/dot_general | solution.py:69
  106.6 2.0 %slice.229 = bf16[32,7168]{1,0:T(8,128)(2,1)} slice(f32[64,7168]{1,0:T(8,128)} %convolution_add_fusion.2), slice={[32:64], [0:7168]} | slice | bytes 917504 | tf_op jit(solution)/shard_map/slice | solution.py:80
  108.6 0.6 collective-permute-start.10
  109.3 3.0 %fusion.10 = f32[64,256]{1,0:T(8,128)S(1)} fusion(bf16[7168,256]{1,0:T(8,128)(2,1)} %collective-permute-done.2, bf16[64,7296]{1,0:T(8,128)(2,1)S(1)} %constant_dynamic-update-slice_fusion.3), kind=kOutput, calls=%fused_computation.23 | convolution fusion | flops 234881024 | bytes 4653056 | tf_op jit(solution)/shard_map/dot_general | solution.py:66
  112.2 7.2 %convolution_add_fusion.1 = f32[64,7168]{1,0:T(8,128)} fusion(f32[64,7168]{1,0:T(8,128)} %fusion.65, bf16[256,7168]{1,0:T(8,128)(2,1)} %collective-permute-done.4, f32[64,256]{1,0:T(8,128)S(1)} %fusion.10, bf16[7168,256]{1,0:T(8,128)(2,1)} %collective-permute-done.3, bf16[64,7296]{1,0:T(8,128)(2,1)S(1)} %constant_dynamic-update-slice_fusion.3, ...), kind=kOutput, calls=%fused_computation.1 | convolution fusion | flops 470335488 | bytes 11993600 | tf_op jit(solution)/shard_map/dot_general | solution.py:69
  119.4 2.0 %slice.228 = bf16[32,7168]{1,0:T(8,128)(2,1)} slice(f32[64,7168]{1,0:T(8,128)} %convolution_add_fusion.1), slice={[32:64], [0:7168]} | slice | bytes 917504 | tf_op jit(solution)/shard_map/slice | solution.py:80
  121.4 1.4 collective-permute-start.16
  122.8 2.8 %fusion.2 = f32[64,256]{1,0:T(8,128)S(1)} fusion(bf16[7168,256]{1,0:T(8,128)(2,1)} %collective-permute-done.2, bf16[64,7296]{1,0:T(8,128)(2,1)S(1)} %constant_dynamic-update-slice_fusion.6), kind=kOutput, calls=%fused_computation.15 | convolution fusion | flops 234881024 | bytes 4653056 | tf_op jit(solution)/shard_map/dot_general | solution.py:66
  125.6 7.2 %convolution_add_fusion = f32[64,7168]{1,0:T(8,128)} fusion(f32[64,7168]{1,0:T(8,128)} %fusion.74, bf16[256,7168]{1,0:T(8,128)(2,1)} %collective-permute-done.4, f32[64,256]{1,0:T(8,128)S(1)} %fusion.2, bf16[7168,256]{1,0:T(8,128)(2,1)} %collective-permute-done.3, bf16[64,7296]{1,0:T(8,128)(2,1)S(1)} %constant_dynamic-update-slice_fusion.6, ...), kind=kOutput, calls=%fused_computation | convolution fusion | flops 470335488 | bytes 11993600 | tf_op jit(solution)/shard_map/dot_general | solution.py:69
  132.8 1.4 slice.227
  134.1 0.7 collective-permute-start.22
  134.9 2.8 %fusion.26 = f32[64,256]{1,0:T(8,128)S(1)} fusion(bf16[7168,256]{1,0:T(8,128)(2,1)} %collective-permute-done.2, bf16[64,7296]{1,0:T(8,128)(2,1)S(1)} %pad_maximum_fusion), kind=kOutput, calls=%fused_computation.39 | convolution fusion | flops 234881024 | bytes 4653056 | tf_op jit(solution)/shard_map/dot_general | solution.py:66
  137.7 6.8 %convolution_add_fusion.3 = f32[64,7168]{1,0:T(8,128)} fusion(f32[64,7168]{1,0:T(8,128)S(1)} %copy-done.2, bf16[256,7168]{1,0:T(8,128)(2,1)} %collective-permute-done.4, f32[64,256]{1,0:T(8,128)S(1)} %fusion.26, bf16[7168,256]{1,0:T(8,128)(2,1)} %collective-permute-done.3, bf16[64,7296]{1,0:T(8,128)(2,1)S(1)} %pad_maximum_fusion, f32[64]{0:T(128)S(1)} %get-tuple-element.11), kind=kOutput, calls=%fused_computation.3 | convolution fusion | flops 470335488 | bytes 11993600 | tf_op jit(solution)/shard_map/dot_general | solution.py:69
  144.4 1.4 slice.230
  145.8 1.4 collective-permute-start.5
  147.3 1.4 slice_add_fusion.2
  148.7 1.5 collective-permute-start.11
  150.2 1.4 slice_add_fusion.1
  151.6 0.6 collective-permute-start.17
  152.2 1.1 slice_add_fusion
  153.4 1.5 collective-permute-start.23
  154.9 4.4 %collective-permute-done.5 = bf16[32,7168]{1,0:T(8,128)(2,1)S(1)} collective-permute-done((bf16[32,7168]{1,0:T(8,128)(2,1)S(1)}, bf16[32,7168]{1,0:T(8,128)(2,1)S(1)}, u32[]{:S(2)}, u32[]{:S(2)}) %collective-permute-start.5) | collective-permute-done | bytes 458784 | tf_op jit(solution)/shard_map/ppermute | solution.py:18
  159.4 1.4 collective-permute-start.6
  160.8 2.2 %collective-permute-start.12 = (bf16[16,7168]{1,0:T(8,128)(2,1)S(1)}, bf16[16,7168]{1,0:T(8,128)(2,1)S(1)}, u32[]{:S(2)}, u32[]{:S(2)}) collective-permute-start(bf16[16,7168]{1,0:T(8,128)(2,1)S(1)} %fusion.34), channel_id=1, source_target_pairs={{0,24},{1,25},{2,26},{3,27},{4,28},{5,29},{6,30},{7,31},{8,0},{9,1... | collective-permute-start | bytes 688136 | tf_op jit(solution)/shard_map/ppermute | solution.py:18
  163.2 1.5 collective-permute-start.24
  164.7 0.8 collective-permute-done.6
  165.5 5.9 %collective-permute-done.12 = bf16[16,7168]{1,0:T(8,128)(2,1)S(1)} collective-permute-done((bf16[16,7168]{1,0:T(8,128)(2,1)S(1)}, bf16[16,7168]{1,0:T(8,128)(2,1)S(1)}, u32[]{:S(2)}, u32[]{:S(2)}) %collective-permute-start.12) | collective-permute-done | bytes 229408 | tf_op jit(solution)/shard_map/ppermute | solution.py:18
  171.3 4.7 %collective-permute-done.24 = bf16[16,7168]{1,0:T(8,128)(2,1)S(1)} collective-permute-done((bf16[16,7168]{1,0:T(8,128)(2,1)S(1)}, bf16[16,7168]{1,0:T(8,128)(2,1)S(1)}, u32[]{:S(2)}, u32[]{:S(2)}) %collective-permute-start.24) | collective-permute-done | bytes 229408 | tf_op jit(solution)/shard_map/ppermute | solution.py:18
  176.0 0.8 fusion.38
  (49 shorter events, 0.8 us)
Async XLA Ops:
  0.0 50.1 %copy-start.5 = (bf16[16,7168]{1,0:T(8,128)(2,1)S(1)}, bf16[16,7168]{1,0:T(8,128)(2,1)}, u32[]{:S(2)}) copy-start(bf16[16,7168]{1,0:T(8,128)(2,1)} %param.6) | copy-start | bytes 688132
  2.4 7.7 %collective-permute-start = (bf16[16,7296]{1,0:T(8,128)(2,1)S(1)}, bf16[16,7296]{1,0:T(8,128)(2,1)S(1)}, u32[]{:S(2)}, u32[]{:S(2)}) collective-permute-start(bf16[16,7296]{1,0:T(8,128)(2,1)S(1)} %pad_maximum_fusion.5), channel_id=1, source_target_pairs={{0,2},{1,5},{2,0},{3,7},{4,6},{5,1},{6,4},{7,3},{8,10},{9,13},{10,... | collective-permute-start | bytes 700424 | tf_op jit(solution)/shard_map/ppermute | solution.py:18
  5.5 10.4 %collective-permute-start.7 = (bf16[16,7296]{1,0:T(8,128)(2,1)S(1)}, bf16[16,7296]{1,0:T(8,128)(2,1)S(1)}, u32[]{:S(2)}, u32[]{:S(2)}) collective-permute-start(bf16[16,7296]{1,0:T(8,128)(2,1)S(1)} %pad_maximum_fusion.5), channel_id=1, source_target_pairs={{0,8},{1,9},{2,10},{3,11},{4,12},{5,13},{6,14},{7,15},{8,16},{9,17... | collective-permute-start | bytes 700424 | tf_op jit(solution)/shard_map/ppermute | solution.py:18
  7.0 11.9 %collective-permute-start.13 = (bf16[16,7296]{1,0:T(8,128)(2,1)S(1)}, bf16[16,7296]{1,0:T(8,128)(2,1)S(1)}, u32[]{:S(2)}, u32[]{:S(2)}) collective-permute-start(bf16[16,7296]{1,0:T(8,128)(2,1)S(1)} %pad_maximum_fusion.5), channel_id=1, source_target_pairs={{0,24},{1,25},{2,26},{3,27},{4,28},{5,29},{6,30},{7,31},{8,0},{9,1... | collective-permute-start | bytes 700424 | tf_op jit(solution)/shard_map/ppermute | solution.py:18
  9.3 20.2 %collective-permute-start.19 = (bf16[16,7296]{1,0:T(8,128)(2,1)S(1)}, bf16[16,7296]{1,0:T(8,128)(2,1)S(1)}, u32[]{:S(2)}, u32[]{:S(2)}) collective-permute-start(bf16[16,7296]{1,0:T(8,128)(2,1)S(1)} %pad_maximum_fusion.5), channel_id=1, source_target_pairs={{0,16},{1,17},{2,18},{3,19},{4,20},{5,21},{6,22},{7,23},{8,24},{9,... | collective-permute-start | bytes 700424 | tf_op jit(solution)/shard_map/ppermute | solution.py:18
  10.1 86.0 %collective-permute-start.2 = (bf16[7168,256]{1,0:T(8,128)(2,1)}, bf16[7168,256]{1,0:T(8,128)(2,1)}, u32[]{:S(2)}, u32[]{:S(2)}) collective-permute-start(bf16[7168,256]{1,0:T(8,128)(2,1)} %bitcast.43), channel_id=1, source_target_pairs={{0,1},{1,0},{2,3},{3,2},{4,5},{5,4},{6,7},{7,6},{8,9},{9,8},{10,11... | collective-permute-start | bytes 11010056 | tf_op jit(solution)/shard_map/ppermute | solution.py:18
  10.1 89.0 %collective-permute-start.3 = (bf16[7168,256]{1,0:T(8,128)(2,1)}, bf16[7168,256]{1,0:T(8,128)(2,1)}, u32[]{:S(2)}, u32[]{:S(2)}) collective-permute-start(bf16[7168,256]{1,0:T(8,128)(2,1)} %bitcast.44), channel_id=1, source_target_pairs={{0,1},{1,0},{2,3},{3,2},{4,5},{5,4},{6,7},{7,6},{8,9},{9,8},{10,11... | collective-permute-start | bytes 11010056 | tf_op jit(solution)/shard_map/ppermute | solution.py:18
  15.9 34.3 %copy-start = (bf16[1,1,7168,256]{3,2,1,0:T(8,128)(2,1)S(1)}, bf16[1,1,7168,256]{3,2,1,0:T(8,128)(2,1)}, u32[]{:S(2)}) copy-start(bf16[1,1,7168,256]{3,2,1,0:T(8,128)(2,1)} %param.9) | copy-start | bytes 11010052
  15.9 83.3 %collective-permute-start.4 = (bf16[256,7168]{1,0:T(8,128)(2,1)}, bf16[256,7168]{1,0:T(8,128)(2,1)}, u32[]{:S(2)}, u32[]{:S(2)}) collective-permute-start(bf16[256,7168]{1,0:T(8,128)(2,1)} %bitcast.45), channel_id=1, source_target_pairs={{0,1},{1,0},{2,3},{3,2},{4,5},{5,4},{6,7},{7,6},{8,9},{9,8},{10,11... | collective-permute-start | bytes 11010056 | tf_op jit(solution)/shard_map/ppermute | solution.py:18
  19.0 29.7 %collective-permute-start.1 = (bf16[32,7296]{1,0:T(8,128)(2,1)S(1)}, bf16[32,7296]{1,0:T(8,128)(2,1)S(1)}, u32[]{:S(2)}, u32[]{:S(2)}) collective-permute-start(bf16[32,7296]{1,0:T(8,128)(2,1)S(1)} %pad_maximum_fusion.1), channel_id=1, source_target_pairs={{0,4},{1,3},{2,6},{3,1},{4,0},{5,7},{6,2},{7,5},{8,12},{9,11},{10,... | collective-permute-start | bytes 1400840 | tf_op jit(solution)/shard_map/ppermute | solution.py:18
  29.5 6.1 %collective-permute-start.8 = (bf16[16,7296]{1,0:T(8,128)(2,1)S(1)}, bf16[16,7296]{1,0:T(8,128)(2,1)S(1)}, u32[]{:S(2)}, u32[]{:S(2)}) collective-permute-start(bf16[16,7296]{1,0:T(8,128)(2,1)S(1)} %collective-permute-done.7), channel_id=1, source_target_pairs={{0,2},{1,5},{2,0},{3,7},{4,6},{5,1},{6,4},{7,3},{8,10},{9,13},{10,... | collective-permute-start | bytes 700424 | tf_op jit(solution)/shard_map/ppermute | solution.py:18
  35.6 6.1 %collective-permute-start.14 = (bf16[16,7296]{1,0:T(8,128)(2,1)S(1)}, bf16[16,7296]{1,0:T(8,128)(2,1)S(1)}, u32[]{:S(2)}, u32[]{:S(2)}) collective-permute-start(bf16[16,7296]{1,0:T(8,128)(2,1)S(1)} %collective-permute-done.13), channel_id=1, source_target_pairs={{0,2},{1,5},{2,0},{3,7},{4,6},{5,1},{6,4},{7,3},{8,10},{9,13},{10,... | collective-permute-start | bytes 700424 | tf_op jit(solution)/shard_map/ppermute | solution.py:18
  41.7 6.3 %collective-permute-start.20 = (bf16[16,7296]{1,0:T(8,128)(2,1)S(1)}, bf16[16,7296]{1,0:T(8,128)(2,1)S(1)}, u32[]{:S(2)}, u32[]{:S(2)}) collective-permute-start(bf16[16,7296]{1,0:T(8,128)(2,1)S(1)} %collective-permute-done.19), channel_id=1, source_target_pairs={{0,2},{1,5},{2,0},{3,7},{4,6},{5,1},{6,4},{7,3},{8,10},{9,13},{10,... | collective-permute-start | bytes 700424 | tf_op jit(solution)/shard_map/ppermute | solution.py:18
  48.0 8.6 %collective-permute-start.9 = (bf16[32,7296]{1,0:T(8,128)(2,1)S(1)}, bf16[32,7296]{1,0:T(8,128)(2,1)S(1)}, u32[]{:S(2)}, u32[]{:S(2)}) collective-permute-start(bf16[32,7296]{1,0:T(8,128)(2,1)S(1)} %pad_maximum_fusion.2), channel_id=1, source_target_pairs={{0,4},{1,3},{2,6},{3,1},{4,0},{5,7},{6,2},{7,5},{8,12},{9,11},{10,... | collective-permute-start | bytes 1400840 | tf_op jit(solution)/shard_map/ppermute | solution.py:18
  48.7 12.9 %collective-permute-start.15 = (bf16[32,7296]{1,0:T(8,128)(2,1)S(1)}, bf16[32,7296]{1,0:T(8,128)(2,1)S(1)}, u32[]{:S(2)}, u32[]{:S(2)}) collective-permute-start(bf16[32,7296]{1,0:T(8,128)(2,1)S(1)} %pad_maximum_fusion.3), channel_id=1, source_target_pairs={{0,4},{1,3},{2,6},{3,1},{4,0},{5,7},{6,2},{7,5},{8,12},{9,11},{10,... | collective-permute-start | bytes 1400840 | tf_op jit(solution)/shard_map/ppermute | solution.py:18
  56.5 10.0 %collective-permute-start.21 = (bf16[32,7296]{1,0:T(8,128)(2,1)S(1)}, bf16[32,7296]{1,0:T(8,128)(2,1)S(1)}, u32[]{:S(2)}, u32[]{:S(2)}) collective-permute-start(bf16[32,7296]{1,0:T(8,128)(2,1)S(1)} %pad_maximum_fusion.4), channel_id=1, source_target_pairs={{0,4},{1,3},{2,6},{3,1},{4,0},{5,7},{6,2},{7,5},{8,12},{9,11},{10,... | collective-permute-start | bytes 1400840 | tf_op jit(solution)/shard_map/ppermute | solution.py:18
  57.2 10.3 %copy-start.1 = (bf16[64,7296]{1,0:T(8,128)(2,1)}, bf16[64,7296]{1,0:T(8,128)(2,1)S(1)}, u32[]{:S(2)}) copy-start(bf16[64,7296]{1,0:T(8,128)(2,1)S(1)} %constant_dynamic-update-slice_fusion) | copy-start | bytes 2801668
  108.6 38.6 %collective-permute-start.10 = (bf16[32,7168]{1,0:T(8,128)(2,1)}, bf16[32,7168]{1,0:T(8,128)(2,1)}, u32[]{:S(2)}, u32[]{:S(2)}) collective-permute-start(bf16[32,7168]{1,0:T(8,128)(2,1)} %slice.229), channel_id=1, source_target_pairs={{0,4},{1,3},{2,6},{3,1},{4,0},{5,7},{6,2},{7,5},{8,12},{9,11},{10,... | collective-permute-start | bytes 1376264 | tf_op jit(solution)/shard_map/ppermute | solution.py:18
  121.4 28.8 %collective-permute-start.16 = (bf16[32,7168]{1,0:T(8,128)(2,1)}, bf16[32,7168]{1,0:T(8,128)(2,1)}, u32[]{:S(2)}, u32[]{:S(2)}) collective-permute-start(bf16[32,7168]{1,0:T(8,128)(2,1)} %slice.228), channel_id=1, source_target_pairs={{0,4},{1,3},{2,6},{3,1},{4,0},{5,7},{6,2},{7,5},{8,12},{9,11},{10,... | collective-permute-start | bytes 1376264 | tf_op jit(solution)/shard_map/ppermute | solution.py:18
  132.8 4.9 %copy-start.2 = (f32[64,7168]{1,0:T(8,128)S(1)}, f32[64,7168]{1,0:T(8,128)}, u32[]{:S(2)}) copy-start(f32[64,7168]{1,0:T(8,128)} %fusion.47) | copy-start | bytes 5505028
  134.1 18.1 %collective-permute-start.22 = (bf16[32,7168]{1,0:T(8,128)(2,1)S(1)}, bf16[32,7168]{1,0:T(8,128)(2,1)}, u32[]{:S(2)}, u32[]{:S(2)}) collective-permute-start(bf16[32,7168]{1,0:T(8,128)(2,1)S(1)} %slice.227), channel_id=1, source_target_pairs={{0,4},{1,3},{2,6},{3,1},{4,0},{5,7},{6,2},{7,5},{8,12},{9,11},{10,... | collective-permute-start | bytes 1376264 | tf_op jit(solution)/shard_map/ppermute | solution.py:18
  144.4 7.8 %copy-start.3 = (f32[64,7168]{1,0:T(8,128)S(1)}, f32[64,7168]{1,0:T(8,128)}, u32[]{:S(2)}) copy-start(f32[64,7168]{1,0:T(8,128)} %convolution_add_fusion) | copy-start | bytes 5505028
  145.8 13.5 %copy-start.4 = (f32[64,7168]{1,0:T(8,128)S(1)}, f32[64,7168]{1,0:T(8,128)}, u32[]{:S(2)}) copy-start(f32[64,7168]{1,0:T(8,128)} %convolution_add_fusion.3) | copy-start | bytes 5505028
  145.8 13.5 %collective-permute-start.5 = (bf16[32,7168]{1,0:T(8,128)(2,1)S(1)}, bf16[32,7168]{1,0:T(8,128)(2,1)S(1)}, u32[]{:S(2)}, u32[]{:S(2)}) collective-permute-start(bf16[32,7168]{1,0:T(8,128)(2,1)S(1)} %slice.230), channel_id=1, source_target_pairs={{0,4},{1,3},{2,6},{3,1},{4,0},{5,7},{6,2},{7,5},{8,12},{9,11},{10,... | collective-permute-start | bytes 1376264 | tf_op jit(solution)/shard_map/ppermute | solution.py:18
  148.7 12.1 %collective-permute-start.11 = (bf16[16,7168]{1,0:T(8,128)(2,1)S(1)}, bf16[16,7168]{1,0:T(8,128)(2,1)S(1)}, u32[]{:S(2)}, u32[]{:S(2)}) collective-permute-start(bf16[16,7168]{1,0:T(8,128)(2,1)S(1)} %slice.233), channel_id=1, source_target_pairs={{0,2},{1,5},{2,0},{3,7},{4,6},{5,1},{6,4},{7,3},{8,10},{9,13},{10,... | collective-permute-start | bytes 688136 | tf_op jit(solution)/shard_map/ppermute | solution.py:18
  151.6 11.5 %collective-permute-start.17 = (bf16[16,7168]{1,0:T(8,128)(2,1)S(1)}, bf16[16,7168]{1,0:T(8,128)(2,1)S(1)}, u32[]{:S(2)}, u32[]{:S(2)}) collective-permute-start(bf16[16,7168]{1,0:T(8,128)(2,1)S(1)} %slice.232), channel_id=1, source_target_pairs={{0,2},{1,5},{2,0},{3,7},{4,6},{5,1},{6,4},{7,3},{8,10},{9,13},{10,... | collective-permute-start | bytes 688136 | tf_op jit(solution)/shard_map/ppermute | solution.py:18
  153.4 9.8 %collective-permute-start.23 = (bf16[16,7168]{1,0:T(8,128)(2,1)S(1)}, bf16[16,7168]{1,0:T(8,128)(2,1)S(1)}, u32[]{:S(2)}, u32[]{:S(2)}) collective-permute-start(bf16[16,7168]{1,0:T(8,128)(2,1)S(1)} %slice.231), channel_id=1, source_target_pairs={{0,2},{1,5},{2,0},{3,7},{4,6},{5,1},{6,4},{7,3},{8,10},{9,13},{10,... | collective-permute-start | bytes 688136 | tf_op jit(solution)/shard_map/ppermute | solution.py:18
  159.4 6.1 %collective-permute-start.6 = (bf16[16,7168]{1,0:T(8,128)(2,1)S(1)}, bf16[16,7168]{1,0:T(8,128)(2,1)S(1)}, u32[]{:S(2)}, u32[]{:S(2)}) collective-permute-start(bf16[16,7168]{1,0:T(8,128)(2,1)S(1)} %slice.234), channel_id=1, source_target_pairs={{0,2},{1,5},{2,0},{3,7},{4,6},{5,1},{6,4},{7,3},{8,10},{9,13},{10,... | collective-permute-start | bytes 688136 | tf_op jit(solution)/shard_map/ppermute | solution.py:18
  160.8 10.5 %collective-permute-start.12 = (bf16[16,7168]{1,0:T(8,128)(2,1)S(1)}, bf16[16,7168]{1,0:T(8,128)(2,1)S(1)}, u32[]{:S(2)}, u32[]{:S(2)}) collective-permute-start(bf16[16,7168]{1,0:T(8,128)(2,1)S(1)} %fusion.34), channel_id=1, source_target_pairs={{0,24},{1,25},{2,26},{3,27},{4,28},{5,29},{6,30},{7,31},{8,0},{9,1... | collective-permute-start | bytes 688136 | tf_op jit(solution)/shard_map/ppermute | solution.py:18
  163.1 8.2 %collective-permute-start.18 = (bf16[16,7168]{1,0:T(8,128)(2,1)S(1)}, bf16[16,7168]{1,0:T(8,128)(2,1)S(1)}, u32[]{:S(2)}, u32[]{:S(2)}) collective-permute-start(bf16[16,7168]{1,0:T(8,128)(2,1)S(1)} %fusion.33), channel_id=1, source_target_pairs={{0,8},{1,9},{2,10},{3,11},{4,12},{5,13},{6,14},{7,15},{8,16},{9,17... | collective-permute-start | bytes 688136 | tf_op jit(solution)/shard_map/ppermute | solution.py:18
  163.2 12.8 %collective-permute-start.24 = (bf16[16,7168]{1,0:T(8,128)(2,1)S(1)}, bf16[16,7168]{1,0:T(8,128)(2,1)S(1)}, u32[]{:S(2)}, u32[]{:S(2)}) collective-permute-start(bf16[16,7168]{1,0:T(8,128)(2,1)S(1)} %fusion.32), channel_id=1, source_target_pairs={{0,16},{1,17},{2,18},{3,19},{4,20},{5,21},{6,22},{7,23},{8,24},{9,... | collective-permute-start | bytes 688136 | tf_op jit(solution)/shard_map/ppermute | solution.py:18

commit v2 on v1

v2 whole, which is shorter than its diff:
```python
import jax
import jax.numpy as jnp
from jax import lax
from jax.experimental import pallas as pl
from jax.experimental.pallas import tpu as pltpu
from jax.sharding import PartitionSpec as P


SLICES = 8
LANES = 128
PLANE = 4
CHUNK = 1024


def send(block, target):
    rails, nodes = lax.axis_size("rail"), lax.axis_size("node")
    route = []
    for rail in range(rails):
        for node in range(nodes):
            rail_to, node_to = target(rail, node)
            route.append((rail * nodes + node, rail_to * nodes + node_to))
    return lax.ppermute(block, ("rail", "node"), route)


def first_partner(rail, node):
    return rail ^ (1 if node % 2 == 0 else 2), node


def second_partner(rail, node):
    return rail ^ (2 if node % 2 == 0 else 1), node


def layer_shift(layers, count):
    def target(rail, node):
        return (rail // PLANE + count) % layers * PLANE + rail % PLANE, node

    return target


def node_shift(nodes, count):
    return lambda rail, node: (rail, (node + count) % nodes)


def pieces(width):
    return [(start, min(CHUNK, width - start)) for start in range(0, width, CHUNK)]


def experts_kernel(ids, near, far, *refs):
    kept, sent = refs[-2:]
    weights = refs[:-2]
    width = weights[0].shape[0]
    lane = lax.broadcasted_iota(jnp.int32, (1, LANES), 1)
    coefs = jnp.concatenate([near[:, width:], far[:, width:]], axis=0).astype(jnp.float32)
    hidden = []
    for at in range(len(weights) // 3):
        w_gate, w_up, _ = weights[3 * at : 3 * at + 3]
        gate_vals = up_vals = None
        for start, size in pieces(width):
            rows = jnp.concatenate([near[:, start : start + size], far[:, start : start + size]], axis=0)
            gate_part = jnp.dot(rows, w_gate[start : start + size, :], preferred_element_type=jnp.float32)
            up_part = jnp.dot(rows, w_up[start : start + size, :], preferred_element_type=jnp.float32)
            gate_vals = gate_part if gate_vals is None else gate_vals + gate_part
            up_vals = up_part if up_vals is None else up_vals + up_part
        mine = jnp.sum(jnp.where(lane == ids[at], coefs, 0.0), axis=1, keepdims=True)
        silu = gate_vals / (1.0 + jnp.exp(-gate_vals))
        hidden.append((silu * up_vals * mine).astype(jnp.bfloat16))
    count = kept.shape[0]
    for start, size in pieces(width):
        total = None
        for at, value in enumerate(hidden):
            w_down = weights[3 * at + 2]
            part = jnp.dot(value, w_down[:, start : start + size], preferred_element_type=jnp.float32)
            total = part if total is None else total + part
        kept[:, start : start + size] = total[:count]
        sent[:, start : start + size] = total[count:].astype(jnp.bfloat16)


def run_experts(ids, near, far, weights):
    width = weights[0].shape[0]
    rows = near.shape[0]
    flops = 2 * 2 * rows * sum(w.size for w in weights)
    whole = pl.BlockSpec(memory_space=pltpu.VMEM)
    return pl.pallas_call(
        experts_kernel,
        in_specs=[pl.BlockSpec(memory_space=pltpu.SMEM)] + [whole] * (2 + len(weights)),
        out_specs=(whole, whole),
        out_shape=(
            jax.ShapeDtypeStruct((rows, width), jnp.float32),
            jax.ShapeDtypeStruct((rows, width), jnp.bfloat16),
        ),
        cost_estimate=pl.CostEstimate(flops=flops, bytes_accessed=0, transcendentals=0),
        compiler_params=pltpu.CompilerParams(vmem_limit_bytes=40 << 20),
    )(ids, near, far, *weights)


def grouping(layers):
    shifts = sorted(range(1, layers), key=lambda count: min(count, layers - count))
    return [[0]] + [shifts[at : at + 2] for at in range(0, len(shifts), 2)]


def layer(tokens, routes, route_weight, gate_weight, up_weight, down_weight):
    row_count, _ = tokens.shape
    nodes = lax.axis_size("node")
    layers = lax.axis_size("rail") // PLANE
    node = lax.axis_index("node")
    first_expert = lax.axis_index("rail") // SLICES * nodes

    lanes = jnp.arange(LANES, dtype=jnp.int32)
    share = route_weight.astype(jnp.float32) / 256.0
    named = routes[:, :, None] == lanes[None, None, :]
    coef = jnp.sum(jnp.where(named, share[:, :, None], 0.0), axis=1).astype(jnp.bfloat16)
    own = jnp.concatenate([tokens, coef], axis=1)

    weights = []
    for count in range(nodes):
        held = (gate_weight[0, 0], up_weight[0, 0], down_weight[0, 0])
        weights += [send(w, node_shift(nodes, count)) for w in held] if count else held
    ids = jnp.stack([first_expert + (node - count) % nodes for count in range(nodes)])

    groups = grouping(layers)
    moved = {count: send(own, layer_shift(layers, count)) for count in range(1, layers)}
    moved[0] = own
    result = None
    for group in groups:
        unit = jnp.concatenate([moved[count] for count in group], axis=0)
        near = jnp.concatenate([unit, send(unit, first_partner)], axis=0)
        far = send(near, second_partner)
        kept, sent = run_experts(ids, near, far, weights)
        out = kept + send(sent, second_partner)
        half = out.shape[0] // 2
        out = out[:half] + send(out[half:].astype(jnp.bfloat16), first_partner)
        for at, count in enumerate(group):
            part = out[at * row_count : (at + 1) * row_count]
            if count:
                part = send(part.astype(jnp.bfloat16), layer_shift(layers, -count)).astype(jnp.float32)
            result = part if result is None else result + part
    return result.astype(jnp.bfloat16)


def solution(mesh):
    rows = P(("groups", "rail", "node"), None)
    weights = P("rail", "node", None, None)
    return jax.shard_map(
        layer,
        mesh=mesh,
        in_specs=(rows, rows, rows, weights, weights, weights),
        out_specs=rows,
        check_vma=False,
    )
```

time: 177 us -> 122 us (0.69)
  matrix products: 70.2 us -> 0 us
  Pallas kernels: 0 us -> 25.4 us
  starting transfers between devices: 29.2 us -> 22.9 us
  other arithmetic: 8.59 us -> 3.91 us
  waiting for transfers between devices: 61.4 us -> 63.5 us
    dot_general x16 -> x0, matrix products: 70.2 us -> none  [the longest x8 55.7 us: experts_of(): part = jnp.dot(hidden, w_down, preferred_element_type=jnp.float32)]
    pallas_call x0 -> x3, Pallas kernels: none -> 25.4 us  [run_experts(): pl.pallas_call(experts_kernel, in_specs=[pl.BlockSpec(memory_space=pltpu....]
    slice x8 -> x4, local copies, waits for them, and re-layouts: 6.82 us -> 0.13 us  [the longest x3 0.1 us: layer(): out = out[:half] + send(out[half:].astype(jnp.bfloat16), first_partner)]
    ppermute x25 -> x21, starting transfers between devices: 29.2 us -> 22.9 us  [send(): return lax.ppermute(block, ('rail', 'node'), route)]
    unnamed x18 -> x17, local copies, waits for them, and re-layouts: 0.14 us -> 6.07 us
    add x4 -> x3, other arithmetic: 3.92 us -> 0.37 us  [layer(): out = kept + send(sent, second_partner)]
    ppermute x25 -> x21, waiting for transfers between devices: 61.4 us -> 63.5 us  [send(): return lax.ppermute(block, ('rail', 'node'), route)]
  transfers between devices with their start and end apart: 25 -> 21, of which waited for: 13 -> 10; matrix products, arithmetic and copies ran while one was open for 41% -> 1% of each run, Pallas kernels for 0% -> 21%
where the time goes in v2:
time: 122 us
  waiting for transfers between devices  63.5 us (52%)
  Pallas kernels  25.4 us (21%)
  starting transfers between devices  22.9 us (19%)
  local copies, waits for them, and re-layouts  6.26 us (5%)
  other arithmetic  3.91 us (3%)
    ppermute x21, waiting for transfers between devices, send(): return lax.ppermute(block, ('rail', 'node'), route)  63.5 us
    pallas_call x3, Pallas kernels, run_experts(): pl.pallas_call(experts_kernel, in_specs=[pl.BlockSpec(memory_space=pltpu....  25.4 us
    ppermute x21, starting transfers between devices, send(): return lax.ppermute(block, ('rail', 'node'), route)  22.9 us
    unnamed x17, local copies, waits for them, and re-layouts  6.07 us
  transfers between devices with their start and end apart: 21, of which 10 were waited for; matrix products, arithmetic and copies ran while one was open for 1% of the time, Pallas kernels for 21%

profile of v2, /device:TPU:0, one launch (start us, length us, event | category | flops | bytes accessed | tf_op | source)
XLA Modules:
  0.0 122.1 jit_solution(3820787671025313178)
XLA Ops:
  0.0 0.0 copy-start.6
  0.0 0.7 convert_multiply_fusion
  0.7 0.8 select_reduce_fusion
  1.5 1.0 pad_maximum_fusion.2
  2.4 3.1 %collective-permute-start.7 = (bf16[16,7296]{1,0:T(8,128)(2,1)S(1)}, bf16[16,7296]{1,0:T(8,128)(2,1)S(1)}, u32[]{:S(2)}, u32[]{:S(2)}) collective-permute-start(bf16[16,7296]{1,0:T(8,128)(2,1)S(1)} %pad_maximum_fusion.2), channel_id=1, source_target_pairs={{0,8},{1,9},{2,10},{3,11},{4,12},{5,13},{6,14},{7,15},{8,16},{9,17... | collective-permute-start | bytes 700424 | tf_op jit(solution)/shard_map/ppermute | solution.py:22
  5.5 2.1 %collective-permute-start.8 = (bf16[16,7296]{1,0:T(8,128)(2,1)S(1)}, bf16[16,7296]{1,0:T(8,128)(2,1)S(1)}, u32[]{:S(2)}, u32[]{:S(2)}) collective-permute-start(bf16[16,7296]{1,0:T(8,128)(2,1)S(1)} %pad_maximum_fusion.2), channel_id=1, source_target_pairs={{0,24},{1,25},{2,26},{3,27},{4,28},{5,29},{6,30},{7,31},{8,0},{9,1... | collective-permute-start | bytes 700424 | tf_op jit(solution)/shard_map/ppermute | solution.py:22
  7.6 0.9 collective-permute-start.15
  8.6 1.5 %collective-permute-start = (bf16[16,7296]{1,0:T(8,128)(2,1)S(1)}, bf16[16,7296]{1,0:T(8,128)(2,1)S(1)}, u32[]{:S(2)}, u32[]{:S(2)}) collective-permute-start(bf16[16,7296]{1,0:T(8,128)(2,1)S(1)} %pad_maximum_fusion.2), channel_id=1, source_target_pairs={{0,2},{1,5},{2,0},{3,7},{4,6},{5,1},{6,4},{7,3},{8,10},{9,13},{10,... | collective-permute-start | bytes 700424 | tf_op jit(solution)/shard_map/ppermute | solution.py:22
  10.1 0.0 collective-permute-start.2
  10.1 0.0 copy-start
  10.1 4.1 %collective-permute-done.7 = bf16[16,7296]{1,0:T(8,128)(2,1)S(1)} collective-permute-done((bf16[16,7296]{1,0:T(8,128)(2,1)S(1)}, bf16[16,7296]{1,0:T(8,128)(2,1)S(1)}, u32[]{:S(2)}, u32[]{:S(2)}) %collective-permute-start.7) | collective-permute-done | bytes 233504 | tf_op jit(solution)/shard_map/ppermute | solution.py:22
  14.2 0.0 collective-permute-start.3
  14.2 14.1 %collective-permute-done.15 = bf16[16,7296]{1,0:T(8,128)(2,1)S(1)} collective-permute-done((bf16[16,7296]{1,0:T(8,128)(2,1)S(1)}, bf16[16,7296]{1,0:T(8,128)(2,1)S(1)}, u32[]{:S(2)}, u32[]{:S(2)}) %collective-permute-start.15) | collective-permute-done | bytes 233504 | tf_op jit(solution)/shard_map/ppermute | solution.py:22
  28.3 0.0 collective-permute-start.4
  28.3 0.0 collective-permute-done.8
  28.3 1.6 %collective-permute-start.16 = (bf16[16,7296]{1,0:T(8,128)(2,1)S(1)}, bf16[16,7296]{1,0:T(8,128)(2,1)S(1)}, u32[]{:S(2)}, u32[]{:S(2)}) collective-permute-start(bf16[16,7296]{1,0:T(8,128)(2,1)S(1)} %collective-permute-done.15), channel_id=1, source_target_pairs={{0,2},{1,5},{2,0},{3,7},{4,6},{5,1},{6,4},{7,3},{8,10},{9,13},{10,... | collective-permute-start | bytes 700424 | tf_op jit(solution)/shard_map/ppermute | solution.py:22
  29.9 4.5 %collective-permute-done.16 = bf16[16,7296]{1,0:T(8,128)(2,1)S(1)} collective-permute-done((bf16[16,7296]{1,0:T(8,128)(2,1)S(1)}, bf16[16,7296]{1,0:T(8,128)(2,1)S(1)}, u32[]{:S(2)}, u32[]{:S(2)}) %collective-permute-start.16) | collective-permute-done | bytes 233504 | tf_op jit(solution)/shard_map/ppermute | solution.py:22
  34.4 1.5 %collective-permute-start.9 = (bf16[32,7296]{1,0:T(8,128)(2,1)S(1)}, bf16[32,7296]{1,0:T(8,128)(2,1)S(1)}, u32[]{:S(2)}, u32[]{:S(2)}) collective-permute-start(bf16[32,7296]{1,0:T(8,128)(2,1)S(1)} %pad_maximum_fusion.1), channel_id=1, source_target_pairs={{0,2},{1,5},{2,0},{3,7},{4,6},{5,1},{6,4},{7,3},{8,10},{9,13},{10,... | collective-permute-start | bytes 1400840 | tf_op jit(solution)/shard_map/ppermute | solution.py:22
  36.0 7.1 %collective-permute-done.9 = bf16[32,7296]{1,0:T(8,128)(2,1)S(1)} collective-permute-done((bf16[32,7296]{1,0:T(8,128)(2,1)S(1)}, bf16[32,7296]{1,0:T(8,128)(2,1)S(1)}, u32[]{:S(2)}, u32[]{:S(2)}) %collective-permute-start.9) | collective-permute-done | bytes 466976 | tf_op jit(solution)/shard_map/ppermute | solution.py:22
  43.0 1.5 %collective-permute-start.17 = (bf16[32,7296]{1,0:T(8,128)(2,1)S(1)}, bf16[32,7296]{1,0:T(8,128)(2,1)S(1)}, u32[]{:S(2)}, u32[]{:S(2)}) collective-permute-start(bf16[32,7296]{1,0:T(8,128)(2,1)S(1)} %constant_dynamic-update-slice_fusion.3.near), channel_id=1, source_target_pairs={{0,4},{1,3},{2,6},{3,1},{4,0},{5,7},{6,2},{7,5},{8,12},{9,11},{10,... | collective-permute-start | bytes 1400840 | tf_op jit(solution)/shard_map/ppermute | solution.py:22
  44.6 0.0 collective-permute-done
  44.6 0.6 collective-permute-start.10
  45.2 0.0 copy-done.6
  45.2 6.4 %collective-permute-done.17.far = bf16[32,7296]{1,0:T(8,128)(2,1)S(1)} collective-permute-done((bf16[32,7296]{1,0:T(8,128)(2,1)S(1)}, bf16[32,7296]{1,0:T(8,128)(2,1)S(1)}, u32[]{:S(2)}, u32[]{:S(2)}) %collective-permute-start.17) | collective-permute-done | bytes 466976 | tf_op jit(solution)/shard_map/ppermute | solution.py:22
  51.6 1.5 %collective-permute-start.1 = (bf16[32,7296]{1,0:T(8,128)(2,1)S(1)}, bf16[32,7296]{1,0:T(8,128)(2,1)S(1)}, u32[]{:S(2)}, u32[]{:S(2)}) collective-permute-start(bf16[32,7296]{1,0:T(8,128)(2,1)S(1)} %pad_maximum_fusion.near), channel_id=1, source_target_pairs={{0,4},{1,3},{2,6},{3,1},{4,0},{5,7},{6,2},{7,5},{8,12},{9,11},{10,... | collective-permute-start | bytes 1400840 | tf_op jit(solution)/shard_map/ppermute | solution.py:22
  53.1 0.1 pad_add_fusion.ids
  53.2 0.0 collective-permute-done.2.refs_3_
  53.2 0.0 collective-permute-done.3.refs_4_
  53.2 1.9 %copy-done.5 = bf16[7168,256]{1,0:T(8,128)(2,1)} copy-done((bf16[7168,256]{1,0:T(8,128)(2,1)}, bf16[7168,256]{1,0:T(8,128)(2,1)S(1)}, u32[]{:S(2)}) %copy-start.5) | copy-done | bytes 3670040
  55.1 0.0 collective-permute-done.4.refs_5_
  55.1 0.0 copy-done
  55.1 2.0 %copy-done.1 = bf16[1,1,7168,256]{3,2,1,0:T(8,128)(2,1)S(1)} copy-done((bf16[1,1,7168,256]{3,2,1,0:T(8,128)(2,1)S(1)}, bf16[1,1,7168,256]{3,2,1,0:T(8,128)(2,1)}, u32[]{:S(2)}) %copy-start.1) | copy-done | bytes 3670040
  57.2 2.0 %copy-done.3 = bf16[1,1,256,7168]{3,2,1,0:T(8,128)(2,1)S(1)} copy-done((bf16[1,1,256,7168]{3,2,1,0:T(8,128)(2,1)S(1)}, bf16[1,1,256,7168]{3,2,1,0:T(8,128)(2,1)}, u32[]{:S(2)}) %copy-start.3) | copy-done | bytes 3670040
  59.2 8.4 %shard_map.66 = (f32[32,7168]{1,0:T(8,128)S(1)}, bf16[32,7168]{1,0:T(8,128)(2,1)S(1)}) custom-call(s32[2]{0:T(128)S(1)} %pad_add_fusion.ids, bf16[32,7296]{1,0:T(8,128)(2,1)S(1)} %constant_dynamic-update-slice_fusion.3.near, bf16[32,7296]{1,0:T(8,128)(2,1)S(1)} %collective-permute-done.17.far, bf16[7168,256]{1,0:T(8,128)(2,1)S(1)} %bitcast.6, ...), custom_call_target="tpu_custom_call" | custom-call | flops 1409286144 | tf_op jit(solution)/shard_map/pallas_call | solution.py:83
  67.6 0.0 copy-start.4
  67.6 0.6 collective-permute-start.18
  68.2 0.0 collective-permute-done.10.far
  68.2 0.0 copy-done.2
  68.2 8.8 %shard_map.65 = (f32[64,7168]{1,0:T(8,128)S(1)}, bf16[64,7168]{1,0:T(8,128)(2,1)S(1)}) custom-call(s32[2]{0:T(128)S(1)} %pad_add_fusion.ids, bf16[64,7296]{1,0:T(8,128)(2,1)S(1)} %constant_dynamic-update-slice_fusion.near, bf16[64,7296]{1,0:T(8,128)(2,1)S(1)} %collective-permute-done.10.far, bf16[7168,256]{1,0:T(8,128)(2,1)S(1)} %bitcast.7, ...), custom_call_target="tpu_custom_call" | custom-call | flops 2818572288 | tf_op jit(solution)/shard_map/pallas_call | solution.py:83
  76.9 1.3 %collective-permute-start.11 = (bf16[64,7168]{1,0:T(8,128)(2,1)S(1)}, bf16[64,7168]{1,0:T(8,128)(2,1)S(1)}, u32[]{:S(2)}, u32[]{:S(2)}) collective-permute-start(bf16[64,7168]{1,0:T(8,128)(2,1)S(1)} %get-tuple-element.14), channel_id=1, source_target_pairs={{0,4},{1,3},{2,6},{3,1},{4,0},{5,7},{6,2},{7,5},{8,12},{9,11},{10,... | collective-permute-start | bytes 2752520 | tf_op jit(solution)/shard_map/ppermute | solution.py:22
  78.2 0.0 collective-permute-done.1.far
  78.2 0.0 copy-done.4
  78.2 8.3 %shard_map.64 = (f32[32,7168]{1,0:T(8,128)S(1)}, bf16[32,7168]{1,0:T(8,128)(2,1)S(1)}) custom-call(s32[2]{0:T(128)S(1)} %pad_add_fusion.ids, bf16[32,7296]{1,0:T(8,128)(2,1)S(1)} %pad_maximum_fusion.near, bf16[32,7296]{1,0:T(8,128)(2,1)S(1)} %collective-permute-done.1.far, bf16[7168,256]{1,0:T(8,128)(2,1)S(1)} %bitcast.8, bf16[7168,256]{1,0:T(8,128)(2,1)S(1)} %bitcast.12, ...), custom_call_target="tpu_custom_call" | custom-call | flops 1409286144 | tf_op jit(solution)/shard_map/pallas_call | solution.py:83
  86.5 0.9 collective-permute-start.5
  87.4 0.0 collective-permute-done.18
  87.4 0.1 convert_add_fusion.1
  87.5 1.5 %collective-permute-start.19 = (bf16[16,7168]{1,0:T(8,128)(2,1)S(1)}, bf16[16,7168]{1,0:T(8,128)(2,1)S(1)}, u32[]{:S(2)}, u32[]{:S(2)}) collective-permute-start(bf16[16,7168]{1,0:T(8,128)(2,1)S(1)} %slice.64), channel_id=1, source_target_pairs={{0,2},{1,5},{2,0},{3,7},{4,6},{5,1},{6,4},{7,3},{8,10},{9,13},{10,... | collective-permute-start | bytes 688136 | tf_op jit(solution)/shard_map/ppermute | solution.py:22
  89.0 11.5 %collective-permute-done.5 = bf16[32,7168]{1,0:T(8,128)(2,1)S(1)} collective-permute-done((bf16[32,7168]{1,0:T(8,128)(2,1)S(1)}, bf16[32,7168]{1,0:T(8,128)(2,1)S(1)}, u32[]{:S(2)}, u32[]{:S(2)}) %collective-permute-start.5) | collective-permute-done | bytes 458784 | tf_op jit(solution)/shard_map/ppermute | solution.py:22
  100.5 0.1 convert_add_fusion.2
  100.6 1.9 %collective-permute-start.6 = (bf16[16,7168]{1,0:T(8,128)(2,1)S(1)}, bf16[16,7168]{1,0:T(8,128)(2,1)S(1)}, u32[]{:S(2)}, u32[]{:S(2)}) collective-permute-start(bf16[16,7168]{1,0:T(8,128)(2,1)S(1)} %slice.65), channel_id=1, source_target_pairs={{0,2},{1,5},{2,0},{3,7},{4,6},{5,1},{6,4},{7,3},{8,10},{9,13},{10,... | collective-permute-start | bytes 688136 | tf_op jit(solution)/shard_map/ppermute | solution.py:22
  102.5 0.0 collective-permute-done.11
  102.5 0.2 convert_add_fusion
  102.7 0.3 collective-permute-start.12
  103.0 0.0 collective-permute-done.19
  103.1 0.1 collective-permute-start.20
  103.1 8.5 %collective-permute-done.12 = bf16[32,7168]{1,0:T(8,128)(2,1)S(1)} collective-permute-done((bf16[32,7168]{1,0:T(8,128)(2,1)S(1)}, bf16[32,7168]{1,0:T(8,128)(2,1)S(1)}, u32[]{:S(2)}, u32[]{:S(2)}) %collective-permute-start.12) | collective-permute-done | bytes 458784 | tf_op jit(solution)/shard_map/ppermute | solution.py:22
  111.6 0.1 fusion
  111.8 1.7 %collective-permute-start.13 = (bf16[16,7168]{1,0:T(8,128)(2,1)S(1)}, bf16[16,7168]{1,0:T(8,128)(2,1)S(1)}, u32[]{:S(2)}, u32[]{:S(2)}) collective-permute-start(bf16[16,7168]{1,0:T(8,128)(2,1)S(1)} %get-tuple-element.17), channel_id=1, source_target_pairs={{0,24},{1,25},{2,26},{3,27},{4,28},{5,29},{6,30},{7,31},{8,0},{9,1... | collective-permute-start | bytes 688136 | tf_op jit(solution)/shard_map/ppermute | solution.py:22
  113.4 0.4 collective-permute-start.14
  113.9 0.0 collective-permute-done.6
  113.9 2.2 %collective-permute-done.20 = bf16[16,7168]{1,0:T(8,128)(2,1)S(1)} collective-permute-done((bf16[16,7168]{1,0:T(8,128)(2,1)S(1)}, bf16[16,7168]{1,0:T(8,128)(2,1)S(1)}, u32[]{:S(2)}, u32[]{:S(2)}) %collective-permute-start.20) | collective-permute-done | bytes 229408 | tf_op jit(solution)/shard_map/ppermute | solution.py:22
  116.1 2.2 %collective-permute-done.13 = bf16[16,7168]{1,0:T(8,128)(2,1)S(1)} collective-permute-done((bf16[16,7168]{1,0:T(8,128)(2,1)S(1)}, bf16[16,7168]{1,0:T(8,128)(2,1)S(1)}, u32[]{:S(2)}, u32[]{:S(2)}) %collective-permute-start.13) | collective-permute-done | bytes 229408 | tf_op jit(solution)/shard_map/ppermute | solution.py:22
  118.3 3.0 %collective-permute-done.14 = bf16[16,7168]{1,0:T(8,128)(2,1)S(1)} collective-permute-done((bf16[16,7168]{1,0:T(8,128)(2,1)S(1)}, bf16[16,7168]{1,0:T(8,128)(2,1)S(1)}, u32[]{:S(2)}, u32[]{:S(2)}) %collective-permute-start.14) | collective-permute-done | bytes 229408 | tf_op jit(solution)/shard_map/ppermute | solution.py:22
  121.3 0.8 fusion.5
  (16 shorter events, 0.4 us)
Async XLA Ops:
  0.0 45.2 %copy-start.6 = (bf16[16,7168]{1,0:T(8,128)(2,1)S(1)}, bf16[16,7168]{1,0:T(8,128)(2,1)}, u32[]{:S(2)}) copy-start(bf16[16,7168]{1,0:T(8,128)(2,1)} %param.6) | copy-start | bytes 688132
  2.4 11.7 %collective-permute-start.7 = (bf16[16,7296]{1,0:T(8,128)(2,1)S(1)}, bf16[16,7296]{1,0:T(8,128)(2,1)S(1)}, u32[]{:S(2)}, u32[]{:S(2)}) collective-permute-start(bf16[16,7296]{1,0:T(8,128)(2,1)S(1)} %pad_maximum_fusion.2), channel_id=1, source_target_pairs={{0,8},{1,9},{2,10},{3,11},{4,12},{5,13},{6,14},{7,15},{8,16},{9,17... | collective-permute-start | bytes 700424 | tf_op jit(solution)/shard_map/ppermute | solution.py:22
  5.5 22.8 %collective-permute-start.8 = (bf16[16,7296]{1,0:T(8,128)(2,1)S(1)}, bf16[16,7296]{1,0:T(8,128)(2,1)S(1)}, u32[]{:S(2)}, u32[]{:S(2)}) collective-permute-start(bf16[16,7296]{1,0:T(8,128)(2,1)S(1)} %pad_maximum_fusion.2), channel_id=1, source_target_pairs={{0,24},{1,25},{2,26},{3,27},{4,28},{5,29},{6,30},{7,31},{8,0},{9,1... | collective-permute-start | bytes 700424 | tf_op jit(solution)/shard_map/ppermute | solution.py:22
  7.6 20.6 %collective-permute-start.15 = (bf16[16,7296]{1,0:T(8,128)(2,1)S(1)}, bf16[16,7296]{1,0:T(8,128)(2,1)S(1)}, u32[]{:S(2)}, u32[]{:S(2)}) collective-permute-start(bf16[16,7296]{1,0:T(8,128)(2,1)S(1)} %pad_maximum_fusion.2), channel_id=1, source_target_pairs={{0,16},{1,17},{2,18},{3,19},{4,20},{5,21},{6,22},{7,23},{8,24},{9,... | collective-permute-start | bytes 700424 | tf_op jit(solution)/shard_map/ppermute | solution.py:22
  8.6 36.0 %collective-permute-start = (bf16[16,7296]{1,0:T(8,128)(2,1)S(1)}, bf16[16,7296]{1,0:T(8,128)(2,1)S(1)}, u32[]{:S(2)}, u32[]{:S(2)}) collective-permute-start(bf16[16,7296]{1,0:T(8,128)(2,1)S(1)} %pad_maximum_fusion.2), channel_id=1, source_target_pairs={{0,2},{1,5},{2,0},{3,7},{4,6},{5,1},{6,4},{7,3},{8,10},{9,13},{10,... | collective-permute-start | bytes 700424 | tf_op jit(solution)/shard_map/ppermute | solution.py:22
  10.1 43.1 %collective-permute-start.2 = (bf16[7168,256]{1,0:T(8,128)(2,1)}, bf16[7168,256]{1,0:T(8,128)(2,1)}, u32[]{:S(2)}, u32[]{:S(2)}) collective-permute-start(bf16[7168,256]{1,0:T(8,128)(2,1)} %bitcast.5), channel_id=1, source_target_pairs={{0,1},{1,0},{2,3},{3,2},{4,5},{5,4},{6,7},{7,6},{8,9},{9,8},{10,11... | collective-permute-start | bytes 11010056 | tf_op jit(solution)/shard_map/ppermute | solution.py:22
  10.1 45.0 %copy-start = (bf16[1,1,7168,256]{3,2,1,0:T(8,128)(2,1)S(1)}, bf16[1,1,7168,256]{3,2,1,0:T(8,128)(2,1)}, u32[]{:S(2)}) copy-start(bf16[1,1,7168,256]{3,2,1,0:T(8,128)(2,1)} %param.9) | copy-start | bytes 11010052
  14.2 39.0 %collective-permute-start.3 = (bf16[7168,256]{1,0:T(8,128)(2,1)}, bf16[7168,256]{1,0:T(8,128)(2,1)S(1)}, u32[]{:S(2)}, u32[]{:S(2)}) collective-permute-start(bf16[7168,256]{1,0:T(8,128)(2,1)} %bitcast.9), channel_id=1, source_target_pairs={{0,1},{1,0},{2,3},{3,2},{4,5},{5,4},{6,7},{7,6},{8,9},{9,8},{10,11... | collective-permute-start | bytes 11010056 | tf_op jit(solution)/shard_map/ppermute | solution.py:22
  28.3 26.8 %collective-permute-start.4 = (bf16[256,7168]{1,0:T(8,128)(2,1)}, bf16[256,7168]{1,0:T(8,128)(2,1)}, u32[]{:S(2)}, u32[]{:S(2)}) collective-permute-start(bf16[256,7168]{1,0:T(8,128)(2,1)} %bitcast.13), channel_id=1, source_target_pairs={{0,1},{1,0},{2,3},{3,2},{4,5},{5,4},{6,7},{7,6},{8,9},{9,8},{10,11... | collective-permute-start | bytes 11010056 | tf_op jit(solution)/shard_map/ppermute | solution.py:22
  28.3 6.1 %collective-permute-start.16 = (bf16[16,7296]{1,0:T(8,128)(2,1)S(1)}, bf16[16,7296]{1,0:T(8,128)(2,1)S(1)}, u32[]{:S(2)}, u32[]{:S(2)}) collective-permute-start(bf16[16,7296]{1,0:T(8,128)(2,1)S(1)} %collective-permute-done.15), channel_id=1, source_target_pairs={{0,2},{1,5},{2,0},{3,7},{4,6},{5,1},{6,4},{7,3},{8,10},{9,13},{10,... | collective-permute-start | bytes 700424 | tf_op jit(solution)/shard_map/ppermute | solution.py:22
  34.4 8.6 %collective-permute-start.9 = (bf16[32,7296]{1,0:T(8,128)(2,1)S(1)}, bf16[32,7296]{1,0:T(8,128)(2,1)S(1)}, u32[]{:S(2)}, u32[]{:S(2)}) collective-permute-start(bf16[32,7296]{1,0:T(8,128)(2,1)S(1)} %pad_maximum_fusion.1), channel_id=1, source_target_pairs={{0,2},{1,5},{2,0},{3,7},{4,6},{5,1},{6,4},{7,3},{8,10},{9,13},{10,... | collective-permute-start | bytes 1400840 | tf_op jit(solution)/shard_map/ppermute | solution.py:22
  43.0 8.6 %collective-permute-start.17 = (bf16[32,7296]{1,0:T(8,128)(2,1)S(1)}, bf16[32,7296]{1,0:T(8,128)(2,1)S(1)}, u32[]{:S(2)}, u32[]{:S(2)}) collective-permute-start(bf16[32,7296]{1,0:T(8,128)(2,1)S(1)} %constant_dynamic-update-slice_fusion.3.near), channel_id=1, source_target_pairs={{0,4},{1,3},{2,6},{3,1},{4,0},{5,7},{6,2},{7,5},{8,12},{9,11},{10,... | collective-permute-start | bytes 1400840 | tf_op jit(solution)/shard_map/ppermute | solution.py:22
  44.6 23.6 %collective-permute-start.10 = (bf16[64,7296]{1,0:T(8,128)(2,1)S(1)}, bf16[64,7296]{1,0:T(8,128)(2,1)S(1)}, u32[]{:S(2)}, u32[]{:S(2)}) collective-permute-start(bf16[64,7296]{1,0:T(8,128)(2,1)S(1)} %constant_dynamic-update-slice_fusion.near), channel_id=1, source_target_pairs={{0,4},{1,3},{2,6},{3,1},{4,0},{5,7},{6,2},{7,5},{8,12},{9,11},{10,... | collective-permute-start | bytes 2801672 | tf_op jit(solution)/shard_map/ppermute | solution.py:22
  51.6 26.6 %collective-permute-start.1 = (bf16[32,7296]{1,0:T(8,128)(2,1)S(1)}, bf16[32,7296]{1,0:T(8,128)(2,1)S(1)}, u32[]{:S(2)}, u32[]{:S(2)}) collective-permute-start(bf16[32,7296]{1,0:T(8,128)(2,1)S(1)} %pad_maximum_fusion.near), channel_id=1, source_target_pairs={{0,4},{1,3},{2,6},{3,1},{4,0},{5,7},{6,2},{7,5},{8,12},{9,11},{10,... | collective-permute-start | bytes 1400840 | tf_op jit(solution)/shard_map/ppermute | solution.py:22
  53.2 1.9 %copy-start.5 = (bf16[7168,256]{1,0:T(8,128)(2,1)}, bf16[7168,256]{1,0:T(8,128)(2,1)S(1)}, u32[]{:S(2)}) copy-start(bf16[7168,256]{1,0:T(8,128)(2,1)S(1)} %collective-permute-done.3.refs_4_) | copy-start | bytes 11010052
  55.1 2.0 %copy-start.1 = (bf16[1,1,7168,256]{3,2,1,0:T(8,128)(2,1)S(1)}, bf16[1,1,7168,256]{3,2,1,0:T(8,128)(2,1)}, u32[]{:S(2)}) copy-start(bf16[1,1,7168,256]{3,2,1,0:T(8,128)(2,1)} %param.10) | copy-start | bytes 11010052
  57.2 2.0 %copy-start.3 = (bf16[1,1,256,7168]{3,2,1,0:T(8,128)(2,1)S(1)}, bf16[1,1,256,7168]{3,2,1,0:T(8,128)(2,1)}, u32[]{:S(2)}) copy-start(bf16[1,1,256,7168]{3,2,1,0:T(8,128)(2,1)} %param.11) | copy-start | bytes 11010052
  59.2 9.0 %copy-start.2 = (bf16[1,1,7168,256]{3,2,1,0:T(8,128)(2,1)S(1)}, bf16[1,1,7168,256]{3,2,1,0:T(8,128)(2,1)}, u32[]{:S(2)}) copy-start(bf16[1,1,7168,256]{3,2,1,0:T(8,128)(2,1)} %param.10) | copy-start | bytes 11010052
  67.6 10.7 %copy-start.4 = (bf16[1,1,256,7168]{3,2,1,0:T(8,128)(2,1)S(1)}, bf16[1,1,256,7168]{3,2,1,0:T(8,128)(2,1)}, u32[]{:S(2)}) copy-start(bf16[1,1,256,7168]{3,2,1,0:T(8,128)(2,1)} %param.11) | copy-start | bytes 11010052
  67.6 19.8 %collective-permute-start.18 = (bf16[32,7168]{1,0:T(8,128)(2,1)S(1)}, bf16[32,7168]{1,0:T(8,128)(2,1)S(1)}, u32[]{:S(2)}, u32[]{:S(2)}) collective-permute-start(bf16[32,7168]{1,0:T(8,128)(2,1)S(1)} %get-tuple-element.16), channel_id=1, source_target_pairs={{0,4},{1,3},{2,6},{3,1},{4,0},{5,7},{6,2},{7,5},{8,12},{9,11},{10,... | collective-permute-start | bytes 1376264 | tf_op jit(solution)/shard_map/ppermute | solution.py:22
  76.9 25.6 %collective-permute-start.11 = (bf16[64,7168]{1,0:T(8,128)(2,1)S(1)}, bf16[64,7168]{1,0:T(8,128)(2,1)S(1)}, u32[]{:S(2)}, u32[]{:S(2)}) collective-permute-start(bf16[64,7168]{1,0:T(8,128)(2,1)S(1)} %get-tuple-element.14), channel_id=1, source_target_pairs={{0,4},{1,3},{2,6},{3,1},{4,0},{5,7},{6,2},{7,5},{8,12},{9,11},{10,... | collective-permute-start | bytes 2752520 | tf_op jit(solution)/shard_map/ppermute | solution.py:22
  86.5 14.0 %collective-permute-start.5 = (bf16[32,7168]{1,0:T(8,128)(2,1)S(1)}, bf16[32,7168]{1,0:T(8,128)(2,1)S(1)}, u32[]{:S(2)}, u32[]{:S(2)}) collective-permute-start(bf16[32,7168]{1,0:T(8,128)(2,1)S(1)} %get-tuple-element.12), channel_id=1, source_target_pairs={{0,4},{1,3},{2,6},{3,1},{4,0},{5,7},{6,2},{7,5},{8,12},{9,11},{10,... | collective-permute-start | bytes 1376264 | tf_op jit(solution)/shard_map/ppermute | solution.py:22
  87.5 15.5 %collective-permute-start.19 = (bf16[16,7168]{1,0:T(8,128)(2,1)S(1)}, bf16[16,7168]{1,0:T(8,128)(2,1)S(1)}, u32[]{:S(2)}, u32[]{:S(2)}) collective-permute-start(bf16[16,7168]{1,0:T(8,128)(2,1)S(1)} %slice.64), channel_id=1, source_target_pairs={{0,2},{1,5},{2,0},{3,7},{4,6},{5,1},{6,4},{7,3},{8,10},{9,13},{10,... | collective-permute-start | bytes 688136 | tf_op jit(solution)/shard_map/ppermute | solution.py:22
  100.6 13.2 %collective-permute-start.6 = (bf16[16,7168]{1,0:T(8,128)(2,1)S(1)}, bf16[16,7168]{1,0:T(8,128)(2,1)S(1)}, u32[]{:S(2)}, u32[]{:S(2)}) collective-permute-start(bf16[16,7168]{1,0:T(8,128)(2,1)S(1)} %slice.65), channel_id=1, source_target_pairs={{0,2},{1,5},{2,0},{3,7},{4,6},{5,1},{6,4},{7,3},{8,10},{9,13},{10,... | collective-permute-start | bytes 688136 | tf_op jit(solution)/shard_map/ppermute | solution.py:22
  102.7 8.9 %collective-permute-start.12 = (bf16[32,7168]{1,0:T(8,128)(2,1)S(1)}, bf16[32,7168]{1,0:T(8,128)(2,1)S(1)}, u32[]{:S(2)}, u32[]{:S(2)}) collective-permute-start(bf16[32,7168]{1,0:T(8,128)(2,1)S(1)} %slice.63), channel_id=1, source_target_pairs={{0,2},{1,5},{2,0},{3,7},{4,6},{5,1},{6,4},{7,3},{8,10},{9,13},{10,... | collective-permute-start | bytes 1376264 | tf_op jit(solution)/shard_map/ppermute | solution.py:22
  103.1 13.0 %collective-permute-start.20 = (bf16[16,7168]{1,0:T(8,128)(2,1)S(1)}, bf16[16,7168]{1,0:T(8,128)(2,1)S(1)}, u32[]{:S(2)}, u32[]{:S(2)}) collective-permute-start(bf16[16,7168]{1,0:T(8,128)(2,1)S(1)} %fusion.1), channel_id=1, source_target_pairs={{0,16},{1,17},{2,18},{3,19},{4,20},{5,21},{6,22},{7,23},{8,24},{9,... | collective-permute-start | bytes 688136 | tf_op jit(solution)/shard_map/ppermute | solution.py:22
  111.8 6.5 %collective-permute-start.13 = (bf16[16,7168]{1,0:T(8,128)(2,1)S(1)}, bf16[16,7168]{1,0:T(8,128)(2,1)S(1)}, u32[]{:S(2)}, u32[]{:S(2)}) collective-permute-start(bf16[16,7168]{1,0:T(8,128)(2,1)S(1)} %get-tuple-element.17), channel_id=1, source_target_pairs={{0,24},{1,25},{2,26},{3,27},{4,28},{5,29},{6,30},{7,31},{8,0},{9,1... | collective-permute-start | bytes 688136 | tf_op jit(solution)/shard_map/ppermute | solution.py:22
  113.4 7.8 %collective-permute-start.14 = (bf16[16,7168]{1,0:T(8,128)(2,1)S(1)}, bf16[16,7168]{1,0:T(8,128)(2,1)S(1)}, u32[]{:S(2)}, u32[]{:S(2)}) collective-permute-start(bf16[16,7168]{1,0:T(8,128)(2,1)S(1)} %get-tuple-element.18), channel_id=1, source_target_pairs={{0,8},{1,9},{2,10},{3,11},{4,12},{5,13},{6,14},{7,15},{8,16},{9,17... | collective-permute-start | bytes 688136 | tf_op jit(solution)/shard_map/ppermute | solution.py:22

commit v3 on v2

v3 whole, which is shorter than its diff:
```python
import functools

import jax
import jax.numpy as jnp
from jax import lax
from jax.experimental import pallas as pl
from jax.experimental.pallas import tpu as pltpu
from jax.sharding import PartitionSpec as P


SLICES = 8
LANES = 128
PLANE = 4
CHUNK = 1024


def send(block, target):
    rails, nodes = lax.axis_size("rail"), lax.axis_size("node")
    route = []
    for rail in range(rails):
        for node in range(nodes):
            rail_to, node_to = target(rail, node)
            route.append((rail * nodes + node, rail_to * nodes + node_to))
    return lax.ppermute(block, ("rail", "node"), route)


def first_partner(rail, node):
    return rail ^ (1 if node % 2 == 0 else 2), node


def second_partner(rail, node):
    return rail ^ (2 if node % 2 == 0 else 1), node


def layer_shift(layers, count):
    def target(rail, node):
        return (rail // PLANE + count) % layers * PLANE + rail % PLANE, node

    return target


def node_shift(nodes, count):
    return lambda rail, node: (rail, (node + count) % nodes)


def pieces(width):
    return [(start, min(CHUNK, width - start)) for start in range(0, width, CHUNK)]


def pack_kernel(tokens, routes, route_weight, packed):
    width = tokens.shape[1]
    lane = lax.broadcasted_iota(jnp.int32, (tokens.shape[0], LANES), 1)
    share = route_weight[...].astype(jnp.float32) / 256.0
    coef = jnp.zeros(lane.shape, jnp.float32)
    for at in range(routes.shape[1]):
        coef += jnp.where(lane == routes[:, at : at + 1], share[:, at : at + 1], 0.0)
    packed[:, :width] = tokens[...]
    packed[:, width:] = coef.astype(jnp.bfloat16)


def pack(tokens, routes, route_weight):
    rows, width = tokens.shape
    whole = pl.BlockSpec(memory_space=pltpu.VMEM)
    return pl.pallas_call(
        pack_kernel,
        in_specs=[whole] * 3,
        out_specs=whole,
        out_shape=jax.ShapeDtypeStruct((rows, width + LANES), jnp.bfloat16),
        compiler_params=pltpu.CompilerParams(vmem_limit_bytes=2 << 20),
    )(tokens, routes, route_weight)


def experts_kernel(ids, *refs, units, held):
    blocks, weights, outs = refs[: 2 * units], refs[2 * units : -2 * units], refs[-2 * units :]
    width = weights[0].shape[0]
    count = blocks[0].shape[0]
    lane = lax.broadcasted_iota(jnp.int32, (1, LANES), 1)
    coefs = jnp.concatenate([block[:, width:] for block in blocks], axis=0).astype(jnp.float32)
    hidden = []
    for at in range(held):
        w_gate, w_up, _ = weights[3 * at : 3 * at + 3]
        gate_vals = up_vals = None
        for start, size in pieces(width):
            rows = jnp.concatenate([block[:, start : start + size] for block in blocks], axis=0)
            gate_part = jnp.dot(rows, w_gate[start : start + size, :], preferred_element_type=jnp.float32)
            up_part = jnp.dot(rows, w_up[start : start + size, :], preferred_element_type=jnp.float32)
            gate_vals = gate_part if gate_vals is None else gate_vals + gate_part
            up_vals = up_part if up_vals is None else up_vals + up_part
        mine = jnp.sum(jnp.where(lane == ids[at], coefs, 0.0), axis=1, keepdims=True)
        silu = gate_vals / (1.0 + jnp.exp(-gate_vals))
        hidden.append((silu * up_vals * mine).astype(jnp.bfloat16))
    for start, size in pieces(width):
        total = None
        for at, value in enumerate(hidden):
            w_down = weights[3 * at + 2]
            part = jnp.dot(value, w_down[:, start : start + size], preferred_element_type=jnp.float32)
            total = part if total is None else total + part
        for at, out in enumerate(outs):
            out[:, start : start + size] = total[at * count : (at + 1) * count].astype(out.dtype)


def stage_kernel(*refs):
    held = (len(refs) - 1) // 2
    copies = [pltpu.make_async_copy(refs[at], refs[held + at], refs[2 * held].at[at]) for at in range(held)]
    for copy in copies:
        copy.start()
    for copy in copies:
        copy.wait()


def stage(weights):
    return pl.pallas_call(
        stage_kernel,
        in_specs=[pl.BlockSpec(memory_space=pltpu.HBM)] * len(weights),
        out_specs=tuple(pl.BlockSpec(memory_space=pltpu.VMEM) for _ in weights),
        out_shape=tuple(pltpu.VMEM(w.shape, w.dtype) for w in weights),
        scratch_shapes=[pltpu.SemaphoreType.DMA((len(weights),))],
        compiler_params=pltpu.CompilerParams(vmem_limit_bytes=1 << 20),
    )(*[pltpu.with_memory_space_constraint(w, pltpu.HBM) for w in weights])


def run_experts(ids, blocks, weights):
    width = weights[0].shape[0]
    rows = blocks[0].shape[0]
    flops = 2 * rows * len(blocks) * sum(w.size for w in weights)
    whole = pl.BlockSpec(memory_space=pltpu.VMEM)
    return pl.pallas_call(
        functools.partial(experts_kernel, units=len(blocks) // 2, held=len(weights) // 3),
        in_specs=[pl.BlockSpec(memory_space=pltpu.SMEM)] + [whole] * (len(blocks) + len(weights)),
        out_specs=(whole,) * len(blocks),
        out_shape=tuple(
            jax.ShapeDtypeStruct((rows, width), jnp.bfloat16 if at % 2 else jnp.float32) for at in range(len(blocks))
        ),
        cost_estimate=pl.CostEstimate(flops=flops, bytes_accessed=0, transcendentals=0),
        compiler_params=pltpu.CompilerParams(vmem_limit_bytes=8 << 20),
    )(ids, *blocks, *weights)


def shifts_of(layers):
    return sorted(range(1, layers), key=lambda count: min(count, layers - count))


def layer(tokens, routes, route_weight, gate_weight, up_weight, down_weight):
    row_count, _ = tokens.shape
    nodes = lax.axis_size("node")
    layers = lax.axis_size("rail") // PLANE
    node = lax.axis_index("node")
    first_expert = lax.axis_index("rail") // SLICES * nodes

    own = pack(tokens, routes, route_weight)

    weights = []
    for count in range(nodes):
        held = (gate_weight[0, 0], up_weight[0, 0], down_weight[0, 0])
        weights += [send(w, node_shift(nodes, count)) for w in held] if count else held
        weights[3 * count :] = stage(weights[3 * count :])
    ids = jnp.stack([first_expert + (node - count) % nodes for count in range(nodes)])

    shifts = shifts_of(layers)
    moved, blocks = {0: own}, {}
    for count in shifts:
        step = 1 if count <= layers // 2 else -1
        moved[count] = send(moved[(count - step) % layers], layer_shift(layers, step))
    for count, unit in moved.items():
        beside = send(unit, first_partner)
        near = jnp.concatenate([unit, beside], axis=0)
        blocks[count] = (near, send(near, second_partner))
    sums = {}
    for count in shifts:
        together = [count, 0] if count == shifts[0] else [count]
        outs = run_experts(ids, [block for unit in together for block in blocks[unit]], weights)
        for at, unit in enumerate(together):
            sums[unit] = outs[2 * at : 2 * at + 2]
    result = None
    for count in shifts + [0]:
        kept, sent = sums[count]
        back = send(sent, second_partner)
        out = kept + back
        back = send(out[row_count:].astype(jnp.bfloat16), first_partner)
        out = out[:row_count] + back
        if count:
            out = send(out.astype(jnp.bfloat16), layer_shift(layers, -count)).astype(jnp.float32)
        result = out if result is None else result + out
    return result.astype(jnp.bfloat16)


def solution(mesh):
    rows = P(("groups", "rail", "node"), None)
    weights = P("rail", "node", None, None)
    return jax.shard_map(
        layer,
        mesh=mesh,
        in_specs=(rows, rows, rows, weights, weights, weights),
        out_specs=rows,
        check_vma=False,
    )
```

time: 122 us -> 118 us (0.967)
  Pallas kernels: 25.4 us -> 22.2 us
  local copies, waits for them, and re-layouts: 6.26 us -> 8.97 us
  other arithmetic: 3.91 us -> 1.4 us
    pallas_call x3 -> x6, Pallas kernels: 25.4 us -> 22.2 us  [the longest x3 12.9 us: run_experts(): pl.pallas_call(functools.partial(experts_kernel, units=len(blocks) // 2,...]
    unnamed x17 -> x19, local copies, waits for them, and re-layouts: 6.07 us -> 8.8 us
    ppermute x21 -> x25, starting transfers between devices: 22.9 us -> 21.9 us  [send(): return lax.ppermute(block, ('rail', 'node'), route)]
    ppermute x21 -> x25, waiting for transfers between devices: 63.5 us -> 63.4 us  [send(): return lax.ppermute(block, ('rail', 'node'), route)]
  transfers between devices with their start and end apart: 21 -> 25, of which waited for: 10 -> 12; matrix products, arithmetic and copies ran while one was open for 1% -> 1% of each run, Pallas kernels for 21% -> 19%
where the time goes in v3:
time: 118 us
  waiting for transfers between devices  63.4 us (54%)
  Pallas kernels  22.2 us (19%)
  starting transfers between devices  21.9 us (19%)
  local copies, waits for them, and re-layouts  8.97 us (8%)
  other arithmetic  1.4 us (1%)
    ppermute x25, waiting for transfers between devices, send(): return lax.ppermute(block, ('rail', 'node'), route)  63.4 us
    ppermute x25, starting transfers between devices, send(): return lax.ppermute(block, ('rail', 'node'), route)  21.9 us
    pallas_call x3, Pallas kernels, run_experts(): pl.pallas_call(functools.partial(experts_kernel, units=len(blocks) // 2,...  12.9 us
    pallas_call x2, Pallas kernels, stage(): pl.pallas_call(stage_kernel, in_specs=[pl.BlockSpec(memory_space=pltpu.HB...  9.16 us
    unnamed x19, local copies, waits for them, and re-layouts  8.8 us
  transfers between devices with their start and end apart: 25, of which 12 were waited for; matrix products, arithmetic and copies ran while one was open for 1% of the time, Pallas kernels for 19%

profile of v3, /device:TPU:0, one launch (start us, length us, event | category | flops | bytes accessed | tf_op | source)
XLA Modules:
  0.0 118.1 jit_solution(10971495499564910001)
XLA Ops:
  0.0 0.8 copy.7.routes
  0.8 0.8 copy.8.route_weight
  1.5 0.9 copy-done.6
  2.5 0.1 shard_map.64
  2.5 3.0 %collective-permute-start.3 = (bf16[16,7296]{1,0:T(8,128)(2,1)S(1)}, bf16[16,7296]{1,0:T(8,128)(2,1)S(1)}, u32[]{:S(2)}, u32[]{:S(2)}) collective-permute-start(bf16[16,7296]{1,0:T(8,128)(2,1)S(1)} %shard_map.64), channel_id=1, source_target_pairs={{0,2},{1,5},{2,0},{3,7},{4,6},{5,1},{6,4},{7,3},{8,10},{9,13},{10,... | collective-permute-start | bytes 700424 | tf_op jit(solution)/shard_map/ppermute | solution.py:24
  5.5 1.6 %collective-permute-start = (bf16[16,7296]{1,0:T(8,128)(2,1)S(1)}, bf16[16,7296]{1,0:T(8,128)(2,1)S(1)}, u32[]{:S(2)}, u32[]{:S(2)}) collective-permute-start(bf16[16,7296]{1,0:T(8,128)(2,1)S(1)} %shard_map.64), channel_id=1, source_target_pairs={{0,8},{1,9},{2,10},{3,11},{4,12},{5,13},{6,14},{7,15},{8,16},{9,17... | collective-permute-start | bytes 700424 | tf_op jit(solution)/shard_map/ppermute | solution.py:24
  7.1 0.0 collective-permute-start.5
  7.1 0.5 collective-permute-start.6
  7.6 4.2 %shard_map.65 = (bf16[7168,256]{1,0:T(8,128)(2,1)S(1)}, bf16[7168,256]{1,0:T(8,128)(2,1)S(1)}, bf16[256,7168]{1,0:T(8,128)(2,1)S(1)}) custom-call(bf16[7168,256]{1,0:T(8,128)(2,1)} %bitcast.6, bf16[7168,256]{1,0:T(8,128)(2,1)} %bitcast.8, bf16[256,7168]{1,0:T(8,128)(2,1)} %bitcast.10), custom_call_target="tpu_custom_call" | custom-call | tf_op jit(solution)/shard_map/pallas_call | solution.py:112
  11.9 1.8 %copy-done = bf16[7168,256]{1,0:T(8,128)(2,1)} copy-done((bf16[7168,256]{1,0:T(8,128)(2,1)}, bf16[7168,256]{1,0:T(8,128)(2,1)S(1)}, u32[]{:S(2)}) %copy-start) | copy-done | bytes 3670040
  13.6 1.8 %copy-done.2 = bf16[7168,256]{1,0:T(8,128)(2,1)} copy-done((bf16[7168,256]{1,0:T(8,128)(2,1)}, bf16[7168,256]{1,0:T(8,128)(2,1)S(1)}, u32[]{:S(2)}) %copy-start.2) | copy-done | bytes 3670040
  15.4 1.9 %copy-done.4 = bf16[256,7168]{1,0:T(8,128)(2,1)} copy-done((bf16[256,7168]{1,0:T(8,128)(2,1)}, bf16[256,7168]{1,0:T(8,128)(2,1)S(1)}, u32[]{:S(2)}) %copy-start.4) | copy-done | bytes 3670040
  17.4 0.1 pad_add_fusion.ids
  17.4 0.0 collective-permute-done.3
  17.4 2.2 %collective-permute-start.11 = (bf16[16,7296]{1,0:T(8,128)(2,1)S(1)}, bf16[16,7296]{1,0:T(8,128)(2,1)S(1)}, u32[]{:S(2)}, u32[]{:S(2)}) collective-permute-start(bf16[16,7296]{1,0:T(8,128)(2,1)S(1)} %shard_map.64), channel_id=1, source_target_pairs={{0,24},{1,25},{2,26},{3,27},{4,28},{5,29},{6,30},{7,31},{8,0},{9,1... | collective-permute-start | bytes 700424 | tf_op jit(solution)/shard_map/ppermute | solution.py:24
  19.7 1.6 %collective-permute-start.4 = (bf16[32,7296]{1,0:T(8,128)(2,1)S(1)}, bf16[32,7296]{1,0:T(8,128)(2,1)S(1)}, u32[]{:S(2)}, u32[]{:S(2)}) collective-permute-start(bf16[32,7296]{1,0:T(8,128)(2,1)S(1)} %pad_maximum_fusion.refs_2_), channel_id=1, source_target_pairs={{0,4},{1,3},{2,6},{3,1},{4,0},{5,7},{6,2},{7,5},{8,12},{9,11},{10,... | collective-permute-start | bytes 1400840 | tf_op jit(solution)/shard_map/ppermute | solution.py:24
  21.4 4.2 %collective-permute-done.11 = bf16[16,7296]{1,0:T(8,128)(2,1)S(1)} collective-permute-done((bf16[16,7296]{1,0:T(8,128)(2,1)S(1)}, bf16[16,7296]{1,0:T(8,128)(2,1)S(1)}, u32[]{:S(2)}, u32[]{:S(2)}) %collective-permute-start.11) | collective-permute-done | bytes 233504 | tf_op jit(solution)/shard_map/ppermute | solution.py:24
  25.6 1.6 %collective-permute-start.17 = (bf16[16,7296]{1,0:T(8,128)(2,1)S(1)}, bf16[16,7296]{1,0:T(8,128)(2,1)S(1)}, u32[]{:S(2)}, u32[]{:S(2)}) collective-permute-start(bf16[16,7296]{1,0:T(8,128)(2,1)S(1)} %collective-permute-done), channel_id=1, source_target_pairs={{0,8},{1,9},{2,10},{3,11},{4,12},{5,13},{6,14},{7,15},{8,16},{9,17... | collective-permute-start | bytes 700424 | tf_op jit(solution)/shard_map/ppermute | solution.py:24
  27.1 8.0 %collective-permute-done.17 = bf16[16,7296]{1,0:T(8,128)(2,1)S(1)} collective-permute-done((bf16[16,7296]{1,0:T(8,128)(2,1)S(1)}, bf16[16,7296]{1,0:T(8,128)(2,1)S(1)}, u32[]{:S(2)}, u32[]{:S(2)}) %collective-permute-start.17) | collective-permute-done | bytes 233504 | tf_op jit(solution)/shard_map/ppermute | solution.py:24
  35.1 6.0 %collective-permute-done.1 = bf16[16,7296]{1,0:T(8,128)(2,1)S(1)} collective-permute-done((bf16[16,7296]{1,0:T(8,128)(2,1)S(1)}, bf16[16,7296]{1,0:T(8,128)(2,1)S(1)}, u32[]{:S(2)}, u32[]{:S(2)}) %collective-permute-start.1) | collective-permute-done | bytes 233504 | tf_op jit(solution)/shard_map/ppermute | solution.py:24
  41.2 0.0 collective-permute-start.12
  41.2 6.0 %collective-permute-done.12 = bf16[16,7296]{1,0:T(8,128)(2,1)S(1)} collective-permute-done((bf16[16,7296]{1,0:T(8,128)(2,1)S(1)}, bf16[16,7296]{1,0:T(8,128)(2,1)S(1)}, u32[]{:S(2)}, u32[]{:S(2)}) %collective-permute-start.12) | collective-permute-done | bytes 233504 | tf_op jit(solution)/shard_map/ppermute | solution.py:24
  47.2 0.0 collective-permute-start.18
  47.3 7.5 %collective-permute-done.18 = bf16[16,7296]{1,0:T(8,128)(2,1)S(1)} collective-permute-done((bf16[16,7296]{1,0:T(8,128)(2,1)S(1)}, bf16[16,7296]{1,0:T(8,128)(2,1)S(1)}, u32[]{:S(2)}, u32[]{:S(2)}) %collective-permute-start.18) | collective-permute-done | bytes 233504 | tf_op jit(solution)/shard_map/ppermute | solution.py:24
  54.8 1.5 %collective-permute-start.2 = (bf16[32,7296]{1,0:T(8,128)(2,1)S(1)}, bf16[32,7296]{1,0:T(8,128)(2,1)S(1)}, u32[]{:S(2)}, u32[]{:S(2)}) collective-permute-start(bf16[32,7296]{1,0:T(8,128)(2,1)S(1)} %constant_dynamic-update-slice_fusion.refs_0_), channel_id=1, source_target_pairs={{0,4},{1,3},{2,6},{3,1},{4,0},{5,7},{6,2},{7,5},{8,12},{9,11},{10,... | collective-permute-start | bytes 1400840 | tf_op jit(solution)/shard_map/ppermute | solution.py:24
  56.3 0.5 collective-permute-start.13
  56.9 0.0 collective-permute-done.6.refs_1_
  56.9 1.6 %collective-permute-start.19 = (bf16[32,7296]{1,0:T(8,128)(2,1)S(1)}, bf16[32,7296]{1,0:T(8,128)(2,1)S(1)}, u32[]{:S(2)}, u32[]{:S(2)}) collective-permute-start(bf16[32,7296]{1,0:T(8,128)(2,1)S(1)} %constant_dynamic-update-slice_fusion.4.refs_0_), channel_id=1, source_target_pairs={{0,4},{1,3},{2,6},{3,1},{4,0},{5,7},{6,2},{7,5},{8,12},{9,11},{10,... | collective-permute-start | bytes 1400840 | tf_op jit(solution)/shard_map/ppermute | solution.py:24
  58.5 4.9 %shard_map.66 = (bf16[7168,256]{1,0:T(8,128)(2,1)S(1)}, bf16[7168,256]{1,0:T(8,128)(2,1)S(1)}, bf16[256,7168]{1,0:T(8,128)(2,1)S(1)}) custom-call(bf16[7168,256]{1,0:T(8,128)(2,1)} %collective-permute-done.5.refs_0_, bf16[7168,256]{1,0:T(8,128)(2,1)} %collective-permute-done.6.refs_1_, bf16[256,7168]{1,0:T(8,128)(2,1)} %collective-permute-done.7.refs_2_), custom_call_target="tpu_custom_call" | custom-call | tf_op jit(solution)/shard_map/pallas_call | solution.py:112
  63.4 0.0 collective-permute-done.4.refs_3_
  63.4 0.0 collective-permute-done.2.refs_1_
  63.4 0.8 copy-done.5
  64.2 3.8 %shard_map.67 = (f32[32,7168]{1,0:T(8,128)S(1)}, bf16[32,7168]{1,0:T(8,128)(2,1)S(1)}, f32[32,7168]{1,0:T(8,128)S(1)}, bf16[32,7168]{1,0:T(8,128)(2,1)S(1)}) custom-call(s32[2]{0:T(128)S(1)} %pad_add_fusion.ids, bf16[32,7296]{1,0:T(8,128)(2,1)S(1)} %constant_dynamic-update-slice_fusion.refs_0_, bf16[32,7296]{1,0:T(8,128)(2,1)S(1)} %collective-permute-done.2.refs_1_, ...), custom_call_target="tpu_custom_call" | custom-call | flops 2818572288 | tf_op jit(solution)/shard_map/pallas_call | solution.py:127
  68.0 1.6 %collective-permute-start.8 = (bf16[32,7168]{1,0:T(8,128)(2,1)S(1)}, bf16[32,7168]{1,0:T(8,128)(2,1)S(1)}, u32[]{:S(2)}, u32[]{:S(2)}) collective-permute-start(bf16[32,7168]{1,0:T(8,128)(2,1)S(1)} %get-tuple-element.26), channel_id=1, source_target_pairs={{0,4},{1,3},{2,6},{3,1},{4,0},{5,7},{6,2},{7,5},{8,12},{9,11},{10,... | collective-permute-start | bytes 1376264 | tf_op jit(solution)/shard_map/ppermute | solution.py:24
  69.6 0.0 collective-permute-done.13.refs_1_
  69.6 4.5 %shard_map.68 = (f32[32,7168]{1,0:T(8,128)S(1)}, bf16[32,7168]{1,0:T(8,128)(2,1)S(1)}) custom-call(s32[2]{0:T(128)S(1)} %pad_add_fusion.ids, bf16[32,7296]{1,0:T(8,128)(2,1)S(1)} %constant_dynamic-update-slice_fusion.2.refs_0_, bf16[32,7296]{1,0:T(8,128)(2,1)S(1)} %collective-permute-done.13.refs_1_, bf16[7168,256]{1,0:T(8,128)(2,1)S(1)} %copy-done.1, ...), custom_call_target="tpu_custom_call" | custom-call | flops 1409286144 | tf_op jit(solution)/shard_map/pallas_call | solution.py:127
  74.1 0.6 collective-permute-start.14
  74.7 0.0 collective-permute-done.19.refs_1_
  74.7 4.6 %shard_map.69 = (f32[32,7168]{1,0:T(8,128)S(1)}, bf16[32,7168]{1,0:T(8,128)(2,1)S(1)}) custom-call(s32[2]{0:T(128)S(1)} %pad_add_fusion.ids, bf16[32,7296]{1,0:T(8,128)(2,1)S(1)} %constant_dynamic-update-slice_fusion.4.refs_0_, bf16[32,7296]{1,0:T(8,128)(2,1)S(1)} %collective-permute-done.19.refs_1_, bf16[7168,256]{1,0:T(8,128)(2,1)S(1)} %copy-done.1, ...), custom_call_target="tpu_custom_call" | custom-call | flops 1409286144 | tf_op jit(solution)/shard_map/pallas_call | solution.py:127
  79.3 1.6 %collective-permute-start.20 = (bf16[32,7168]{1,0:T(8,128)(2,1)S(1)}, bf16[32,7168]{1,0:T(8,128)(2,1)S(1)}, u32[]{:S(2)}, u32[]{:S(2)}) collective-permute-start(bf16[32,7168]{1,0:T(8,128)(2,1)S(1)} %get-tuple-element.30), channel_id=1, source_target_pairs={{0,4},{1,3},{2,6},{3,1},{4,0},{5,7},{6,2},{7,5},{8,12},{9,11},{10,... | collective-permute-start | bytes 1376264 | tf_op jit(solution)/shard_map/ppermute | solution.py:24
  80.9 0.5 collective-permute-start.23
  81.4 0.1 convert_add_fusion.3
  81.5 0.4 collective-permute-start.9
  81.9 7.1 %collective-permute-done.14 = bf16[32,7168]{1,0:T(8,128)(2,1)S(1)} collective-permute-done((bf16[32,7168]{1,0:T(8,128)(2,1)S(1)}, bf16[32,7168]{1,0:T(8,128)(2,1)S(1)}, u32[]{:S(2)}, u32[]{:S(2)}) %collective-permute-start.14) | collective-permute-done | bytes 458784 | tf_op jit(solution)/shard_map/ppermute | solution.py:24
  89.0 0.1 convert_add_fusion.2
  89.1 0.1 collective-permute-start.15
  89.2 8.4 %collective-permute-done.20 = bf16[32,7168]{1,0:T(8,128)(2,1)S(1)} collective-permute-done((bf16[32,7168]{1,0:T(8,128)(2,1)S(1)}, bf16[32,7168]{1,0:T(8,128)(2,1)S(1)}, u32[]{:S(2)}, u32[]{:S(2)}) %collective-permute-start.20) | collective-permute-done | bytes 458784 | tf_op jit(solution)/shard_map/ppermute | solution.py:24
  97.6 0.1 convert_add_fusion.1
  97.7 0.1 collective-permute-start.21
  97.8 5.0 %collective-permute-done.23 = bf16[32,7168]{1,0:T(8,128)(2,1)S(1)} collective-permute-done((bf16[32,7168]{1,0:T(8,128)(2,1)S(1)}, bf16[32,7168]{1,0:T(8,128)(2,1)S(1)}, u32[]{:S(2)}, u32[]{:S(2)}) %collective-permute-start.23) | collective-permute-done | bytes 458784 | tf_op jit(solution)/shard_map/ppermute | solution.py:24
  102.8 0.1 convert_add_fusion
  103.0 0.1 collective-permute-start.24
  103.1 0.0 collective-permute-done.9
  103.1 2.1 %collective-permute-start.10 = (bf16[16,7168]{1,0:T(8,128)(2,1)S(1)}, bf16[16,7168]{1,0:T(8,128)(2,1)S(1)}, u32[]{:S(2)}, u32[]{:S(2)}) collective-permute-start(bf16[16,7168]{1,0:T(8,128)(2,1)S(1)} %fusion.4), channel_id=1, source_target_pairs={{0,24},{1,25},{2,26},{3,27},{4,28},{5,29},{6,30},{7,31},{8,0},{9,1... | collective-permute-start | bytes 688136 | tf_op jit(solution)/shard_map/ppermute | solution.py:24
  105.2 0.0 collective-permute-done.15
  105.2 0.1 collective-permute-start.16
  105.3 0.0 collective-permute-done.21
  105.3 0.1 fusion.2
  105.4 0.8 collective-permute-start.22
  106.2 2.9 %collective-permute-done.24 = bf16[16,7168]{1,0:T(8,128)(2,1)S(1)} collective-permute-done((bf16[16,7168]{1,0:T(8,128)(2,1)S(1)}, bf16[16,7168]{1,0:T(8,128)(2,1)S(1)}, u32[]{:S(2)}, u32[]{:S(2)}) %collective-permute-start.24) | collective-permute-done | bytes 229408 | tf_op jit(solution)/shard_map/ppermute | solution.py:24
  109.1 0.1 collective-permute-done.10
  109.2 4.0 %collective-permute-done.16 = bf16[16,7168]{1,0:T(8,128)(2,1)S(1)} collective-permute-done((bf16[16,7168]{1,0:T(8,128)(2,1)S(1)}, bf16[16,7168]{1,0:T(8,128)(2,1)S(1)}, u32[]{:S(2)}, u32[]{:S(2)}) %collective-permute-start.16) | collective-permute-done | bytes 229408 | tf_op jit(solution)/shard_map/ppermute | solution.py:24
  113.2 4.1 %collective-permute-done.22 = bf16[16,7168]{1,0:T(8,128)(2,1)S(1)} collective-permute-done((bf16[16,7168]{1,0:T(8,128)(2,1)S(1)}, bf16[16,7168]{1,0:T(8,128)(2,1)S(1)}, u32[]{:S(2)}, u32[]{:S(2)}) %collective-permute-start.22) | collective-permute-done | bytes 229408 | tf_op jit(solution)/shard_map/ppermute | solution.py:24
  117.3 0.8 fusion.1
  (28 shorter events, 0.4 us)
Async XLA Ops:
  1.5 0.9 copy-start.6
  2.5 14.9 %collective-permute-start.3 = (bf16[16,7296]{1,0:T(8,128)(2,1)S(1)}, bf16[16,7296]{1,0:T(8,128)(2,1)S(1)}, u32[]{:S(2)}, u32[]{:S(2)}) collective-permute-start(bf16[16,7296]{1,0:T(8,128)(2,1)S(1)} %shard_map.64), channel_id=1, source_target_pairs={{0,2},{1,5},{2,0},{3,7},{4,6},{5,1},{6,4},{7,3},{8,10},{9,13},{10,... | collective-permute-start | bytes 700424 | tf_op jit(solution)/shard_map/ppermute | solution.py:24
  5.5 14.2 %collective-permute-start = (bf16[16,7296]{1,0:T(8,128)(2,1)S(1)}, bf16[16,7296]{1,0:T(8,128)(2,1)S(1)}, u32[]{:S(2)}, u32[]{:S(2)}) collective-permute-start(bf16[16,7296]{1,0:T(8,128)(2,1)S(1)} %shard_map.64), channel_id=1, source_target_pairs={{0,8},{1,9},{2,10},{3,11},{4,12},{5,13},{6,14},{7,15},{8,16},{9,17... | collective-permute-start | bytes 700424 | tf_op jit(solution)/shard_map/ppermute | solution.py:24
  7.1 49.2 %collective-permute-start.5 = (bf16[7168,256]{1,0:T(8,128)(2,1)}, bf16[7168,256]{1,0:T(8,128)(2,1)}, u32[]{:S(2)}, u32[]{:S(2)}) collective-permute-start(bf16[7168,256]{1,0:T(8,128)(2,1)} %bitcast.5), channel_id=1, source_target_pairs={{0,1},{1,0},{2,3},{3,2},{4,5},{5,4},{6,7},{7,6},{8,9},{9,8},{10,11... | collective-permute-start | bytes 11010056 | tf_op jit(solution)/shard_map/ppermute | solution.py:24
  7.1 49.8 %collective-permute-start.6 = (bf16[7168,256]{1,0:T(8,128)(2,1)}, bf16[7168,256]{1,0:T(8,128)(2,1)}, u32[]{:S(2)}, u32[]{:S(2)}) collective-permute-start(bf16[7168,256]{1,0:T(8,128)(2,1)} %bitcast.7), channel_id=1, source_target_pairs={{0,1},{1,0},{2,3},{3,2},{4,5},{5,4},{6,7},{7,6},{8,9},{9,8},{10,11... | collective-permute-start | bytes 11010056 | tf_op jit(solution)/shard_map/ppermute | solution.py:24
  7.6 50.9 %collective-permute-start.7 = (bf16[256,7168]{1,0:T(8,128)(2,1)}, bf16[256,7168]{1,0:T(8,128)(2,1)}, u32[]{:S(2)}, u32[]{:S(2)}) collective-permute-start(bf16[256,7168]{1,0:T(8,128)(2,1)} %bitcast.9), channel_id=1, source_target_pairs={{0,1},{1,0},{2,3},{3,2},{4,5},{5,4},{6,7},{7,6},{8,9},{9,8},{10,11... | collective-permute-start | bytes 11010056 | tf_op jit(solution)/shard_map/ppermute | solution.py:24
  11.8 1.8 %copy-start = (bf16[7168,256]{1,0:T(8,128)(2,1)}, bf16[7168,256]{1,0:T(8,128)(2,1)S(1)}, u32[]{:S(2)}) copy-start(bf16[7168,256]{1,0:T(8,128)(2,1)S(1)} %get-tuple-element.19.refs_4_.refs_2_) | copy-start | bytes 11010052
  13.6 1.8 %copy-start.2 = (bf16[7168,256]{1,0:T(8,128)(2,1)}, bf16[7168,256]{1,0:T(8,128)(2,1)S(1)}, u32[]{:S(2)}) copy-start(bf16[7168,256]{1,0:T(8,128)(2,1)S(1)} %get-tuple-element.20.refs_5_.refs_3_) | copy-start | bytes 11010052
  15.4 1.9 %copy-start.4 = (bf16[256,7168]{1,0:T(8,128)(2,1)}, bf16[256,7168]{1,0:T(8,128)(2,1)S(1)}, u32[]{:S(2)}) copy-start(bf16[256,7168]{1,0:T(8,128)(2,1)S(1)} %get-tuple-element.21.refs_6_.refs_4_) | copy-start | bytes 11010052
  17.4 8.1 %collective-permute-start.11 = (bf16[16,7296]{1,0:T(8,128)(2,1)S(1)}, bf16[16,7296]{1,0:T(8,128)(2,1)S(1)}, u32[]{:S(2)}, u32[]{:S(2)}) collective-permute-start(bf16[16,7296]{1,0:T(8,128)(2,1)S(1)} %shard_map.64), channel_id=1, source_target_pairs={{0,24},{1,25},{2,26},{3,27},{4,28},{5,29},{6,30},{7,31},{8,0},{9,1... | collective-permute-start | bytes 700424 | tf_op jit(solution)/shard_map/ppermute | solution.py:24
  19.7 43.7 %collective-permute-start.4 = (bf16[32,7296]{1,0:T(8,128)(2,1)S(1)}, bf16[32,7296]{1,0:T(8,128)(2,1)S(1)}, u32[]{:S(2)}, u32[]{:S(2)}) collective-permute-start(bf16[32,7296]{1,0:T(8,128)(2,1)S(1)} %pad_maximum_fusion.refs_2_), channel_id=1, source_target_pairs={{0,4},{1,3},{2,6},{3,1},{4,0},{5,7},{6,2},{7,5},{8,12},{9,11},{10,... | collective-permute-start | bytes 1400840 | tf_op jit(solution)/shard_map/ppermute | solution.py:24
  25.6 9.5 %collective-permute-start.17 = (bf16[16,7296]{1,0:T(8,128)(2,1)S(1)}, bf16[16,7296]{1,0:T(8,128)(2,1)S(1)}, u32[]{:S(2)}, u32[]{:S(2)}) collective-permute-start(bf16[16,7296]{1,0:T(8,128)(2,1)S(1)} %collective-permute-done), channel_id=1, source_target_pairs={{0,8},{1,9},{2,10},{3,11},{4,12},{5,13},{6,14},{7,15},{8,16},{9,17... | collective-permute-start | bytes 700424 | tf_op jit(solution)/shard_map/ppermute | solution.py:24
  35.1 6.1 %collective-permute-start.1 = (bf16[16,7296]{1,0:T(8,128)(2,1)S(1)}, bf16[16,7296]{1,0:T(8,128)(2,1)S(1)}, u32[]{:S(2)}, u32[]{:S(2)}) collective-permute-start(bf16[16,7296]{1,0:T(8,128)(2,1)S(1)} %collective-permute-done), channel_id=1, source_target_pairs={{0,2},{1,5},{2,0},{3,7},{4,6},{5,1},{6,4},{7,3},{8,10},{9,13},{10,... | collective-permute-start | bytes 700424 | tf_op jit(solution)/shard_map/ppermute | solution.py:24
  41.2 6.1 %collective-permute-start.12 = (bf16[16,7296]{1,0:T(8,128)(2,1)S(1)}, bf16[16,7296]{1,0:T(8,128)(2,1)S(1)}, u32[]{:S(2)}, u32[]{:S(2)}) collective-permute-start(bf16[16,7296]{1,0:T(8,128)(2,1)S(1)} %collective-permute-done.11), channel_id=1, source_target_pairs={{0,2},{1,5},{2,0},{3,7},{4,6},{5,1},{6,4},{7,3},{8,10},{9,13},{10,... | collective-permute-start | bytes 700424 | tf_op jit(solution)/shard_map/ppermute | solution.py:24
  47.2 7.6 %collective-permute-start.18 = (bf16[16,7296]{1,0:T(8,128)(2,1)S(1)}, bf16[16,7296]{1,0:T(8,128)(2,1)S(1)}, u32[]{:S(2)}, u32[]{:S(2)}) collective-permute-start(bf16[16,7296]{1,0:T(8,128)(2,1)S(1)} %collective-permute-done.17), channel_id=1, source_target_pairs={{0,2},{1,5},{2,0},{3,7},{4,6},{5,1},{6,4},{7,3},{8,10},{9,13},{10,... | collective-permute-start | bytes 700424 | tf_op jit(solution)/shard_map/ppermute | solution.py:24
  54.8 8.6 %collective-permute-start.2 = (bf16[32,7296]{1,0:T(8,128)(2,1)S(1)}, bf16[32,7296]{1,0:T(8,128)(2,1)S(1)}, u32[]{:S(2)}, u32[]{:S(2)}) collective-permute-start(bf16[32,7296]{1,0:T(8,128)(2,1)S(1)} %constant_dynamic-update-slice_fusion.refs_0_), channel_id=1, source_target_pairs={{0,4},{1,3},{2,6},{3,1},{4,0},{5,7},{6,2},{7,5},{8,12},{9,11},{10,... | collective-permute-start | bytes 1400840 | tf_op jit(solution)/shard_map/ppermute | solution.py:24
  56.3 13.3 %collective-permute-start.13 = (bf16[32,7296]{1,0:T(8,128)(2,1)S(1)}, bf16[32,7296]{1,0:T(8,128)(2,1)S(1)}, u32[]{:S(2)}, u32[]{:S(2)}) collective-permute-start(bf16[32,7296]{1,0:T(8,128)(2,1)S(1)} %constant_dynamic-update-slice_fusion.2.refs_0_), channel_id=1, source_target_pairs={{0,4},{1,3},{2,6},{3,1},{4,0},{5,7},{6,2},{7,5},{8,12},{9,11},{10,... | collective-permute-start | bytes 1400840 | tf_op jit(solution)/shard_map/ppermute | solution.py:24
  56.8 6.6 %copy-start.1 = (bf16[7168,256]{1,0:T(8,128)(2,1)S(1)}, bf16[7168,256]{1,0:T(8,128)(2,1)}, u32[]{:S(2)}) copy-start(bf16[7168,256]{1,0:T(8,128)(2,1)} %copy-done) | copy-start | bytes 11010052
  56.8 6.6 %copy-start.3 = (bf16[7168,256]{1,0:T(8,128)(2,1)S(1)}, bf16[7168,256]{1,0:T(8,128)(2,1)}, u32[]{:S(2)}) copy-start(bf16[7168,256]{1,0:T(8,128)(2,1)} %copy-done.2) | copy-start | bytes 11010052
  56.9 7.4 %copy-start.5 = (bf16[256,7168]{1,0:T(8,128)(2,1)S(1)}, bf16[256,7168]{1,0:T(8,128)(2,1)}, u32[]{:S(2)}) copy-start(bf16[256,7168]{1,0:T(8,128)(2,1)} %copy-done.4) | copy-start | bytes 11010052
  56.9 17.8 %collective-permute-start.19 = (bf16[32,7296]{1,0:T(8,128)(2,1)S(1)}, bf16[32,7296]{1,0:T(8,128)(2,1)S(1)}, u32[]{:S(2)}, u32[]{:S(2)}) collective-permute-start(bf16[32,7296]{1,0:T(8,128)(2,1)S(1)} %constant_dynamic-update-slice_fusion.4.refs_0_), channel_id=1, source_target_pairs={{0,4},{1,3},{2,6},{3,1},{4,0},{5,7},{6,2},{7,5},{8,12},{9,11},{10,... | collective-permute-start | bytes 1400840 | tf_op jit(solution)/shard_map/ppermute | solution.py:24
  68.0 13.4 %collective-permute-start.8 = (bf16[32,7168]{1,0:T(8,128)(2,1)S(1)}, bf16[32,7168]{1,0:T(8,128)(2,1)S(1)}, u32[]{:S(2)}, u32[]{:S(2)}) collective-permute-start(bf16[32,7168]{1,0:T(8,128)(2,1)S(1)} %get-tuple-element.26), channel_id=1, source_target_pairs={{0,4},{1,3},{2,6},{3,1},{4,0},{5,7},{6,2},{7,5},{8,12},{9,11},{10,... | collective-permute-start | bytes 1376264 | tf_op jit(solution)/shard_map/ppermute | solution.py:24
  74.1 14.9 %collective-permute-start.14 = (bf16[32,7168]{1,0:T(8,128)(2,1)S(1)}, bf16[32,7168]{1,0:T(8,128)(2,1)S(1)}, u32[]{:S(2)}, u32[]{:S(2)}) collective-permute-start(bf16[32,7168]{1,0:T(8,128)(2,1)S(1)} %get-tuple-element.28), channel_id=1, source_target_pairs={{0,4},{1,3},{2,6},{3,1},{4,0},{5,7},{6,2},{7,5},{8,12},{9,11},{10,... | collective-permute-start | bytes 1376264 | tf_op jit(solution)/shard_map/ppermute | solution.py:24
  79.3 18.3 %collective-permute-start.20 = (bf16[32,7168]{1,0:T(8,128)(2,1)S(1)}, bf16[32,7168]{1,0:T(8,128)(2,1)S(1)}, u32[]{:S(2)}, u32[]{:S(2)}) collective-permute-start(bf16[32,7168]{1,0:T(8,128)(2,1)S(1)} %get-tuple-element.30), channel_id=1, source_target_pairs={{0,4},{1,3},{2,6},{3,1},{4,0},{5,7},{6,2},{7,5},{8,12},{9,11},{10,... | collective-permute-start | bytes 1376264 | tf_op jit(solution)/shard_map/ppermute | solution.py:24
  80.9 21.9 %collective-permute-start.23 = (bf16[32,7168]{1,0:T(8,128)(2,1)S(1)}, bf16[32,7168]{1,0:T(8,128)(2,1)S(1)}, u32[]{:S(2)}, u32[]{:S(2)}) collective-permute-start(bf16[32,7168]{1,0:T(8,128)(2,1)S(1)} %get-tuple-element.32), channel_id=1, source_target_pairs={{0,4},{1,3},{2,6},{3,1},{4,0},{5,7},{6,2},{7,5},{8,12},{9,11},{10,... | collective-permute-start | bytes 1376264 | tf_op jit(solution)/shard_map/ppermute | solution.py:24
  81.5 21.5 %collective-permute-start.9 = (bf16[16,7168]{1,0:T(8,128)(2,1)S(1)}, bf16[16,7168]{1,0:T(8,128)(2,1)S(1)}, u32[]{:S(2)}, u32[]{:S(2)}) collective-permute-start(bf16[16,7168]{1,0:T(8,128)(2,1)S(1)} %slice.65), channel_id=1, source_target_pairs={{0,2},{1,5},{2,0},{3,7},{4,6},{5,1},{6,4},{7,3},{8,10},{9,13},{10,... | collective-permute-start | bytes 688136 | tf_op jit(solution)/shard_map/ppermute | solution.py:24
  89.1 16.0 %collective-permute-start.15 = (bf16[16,7168]{1,0:T(8,128)(2,1)S(1)}, bf16[16,7168]{1,0:T(8,128)(2,1)S(1)}, u32[]{:S(2)}, u32[]{:S(2)}) collective-permute-start(bf16[16,7168]{1,0:T(8,128)(2,1)S(1)} %slice.64), channel_id=1, source_target_pairs={{0,2},{1,5},{2,0},{3,7},{4,6},{5,1},{6,4},{7,3},{8,10},{9,13},{10,... | collective-permute-start | bytes 688136 | tf_op jit(solution)/shard_map/ppermute | solution.py:24
  97.7 7.5 %collective-permute-start.21 = (bf16[16,7168]{1,0:T(8,128)(2,1)S(1)}, bf16[16,7168]{1,0:T(8,128)(2,1)S(1)}, u32[]{:S(2)}, u32[]{:S(2)}) collective-permute-start(bf16[16,7168]{1,0:T(8,128)(2,1)S(1)} %slice.63), channel_id=1, source_target_pairs={{0,2},{1,5},{2,0},{3,7},{4,6},{5,1},{6,4},{7,3},{8,10},{9,13},{10,... | collective-permute-start | bytes 688136 | tf_op jit(solution)/shard_map/ppermute | solution.py:24
  103.0 6.1 %collective-permute-start.24 = (bf16[16,7168]{1,0:T(8,128)(2,1)S(1)}, bf16[16,7168]{1,0:T(8,128)(2,1)S(1)}, u32[]{:S(2)}, u32[]{:S(2)}) collective-permute-start(bf16[16,7168]{1,0:T(8,128)(2,1)S(1)} %slice.62), channel_id=1, source_target_pairs={{0,2},{1,5},{2,0},{3,7},{4,6},{5,1},{6,4},{7,3},{8,10},{9,13},{10,... | collective-permute-start | bytes 688136 | tf_op jit(solution)/shard_map/ppermute | solution.py:24
  103.1 6.1 %collective-permute-start.10 = (bf16[16,7168]{1,0:T(8,128)(2,1)S(1)}, bf16[16,7168]{1,0:T(8,128)(2,1)S(1)}, u32[]{:S(2)}, u32[]{:S(2)}) collective-permute-start(bf16[16,7168]{1,0:T(8,128)(2,1)S(1)} %fusion.4), channel_id=1, source_target_pairs={{0,24},{1,25},{2,26},{3,27},{4,28},{5,29},{6,30},{7,31},{8,0},{9,1... | collective-permute-start | bytes 688136 | tf_op jit(solution)/shard_map/ppermute | solution.py:24
  105.2 8.0 %collective-permute-start.16 = (bf16[16,7168]{1,0:T(8,128)(2,1)S(1)}, bf16[16,7168]{1,0:T(8,128)(2,1)S(1)}, u32[]{:S(2)}, u32[]{:S(2)}) collective-permute-start(bf16[16,7168]{1,0:T(8,128)(2,1)S(1)} %fusion.3), channel_id=1, source_target_pairs={{0,8},{1,9},{2,10},{3,11},{4,12},{5,13},{6,14},{7,15},{8,16},{9,17... | collective-permute-start | bytes 688136 | tf_op jit(solution)/shard_map/ppermute | solution.py:24
  105.4 11.9 %collective-permute-start.22 = (bf16[16,7168]{1,0:T(8,128)(2,1)S(1)}, bf16[16,7168]{1,0:T(8,128)(2,1)S(1)}, u32[]{:S(2)}, u32[]{:S(2)}) collective-permute-start(bf16[16,7168]{1,0:T(8,128)(2,1)S(1)} %fusion.2), channel_id=1, source_target_pairs={{0,16},{1,17},{2,18},{3,19},{4,20},{5,21},{6,22},{7,23},{8,24},{9,... | collective-permute-start | bytes 688136 | tf_op jit(solution)/shard_map/ppermute | solution.py:24

commit v4 on v3

--- a/solution.py
+++ b/solution.py
@@ -47,27 +47,37 @@
     return [(start, min(CHUNK, width - start)) for start in range(0, width, CHUNK)]
 
 
-def pack_kernel(tokens, routes, route_weight, packed):
+def pack_kernel(tokens, routes, route_weight, packed, named, shares, arrived):
     width = tokens.shape[1]
-    lane = lax.broadcasted_iota(jnp.int32, (tokens.shape[0], LANES), 1)
-    share = route_weight[...].astype(jnp.float32) / 256.0
-    coef = jnp.zeros(lane.shape, jnp.float32)
-    for at in range(routes.shape[1]):
-        coef += jnp.where(lane == routes[:, at : at + 1], share[:, at : at + 1], 0.0)
-    packed[:, :width] = tokens[...]
-    packed[:, width:] = coef.astype(jnp.bfloat16)
+    copies = [
+        pltpu.make_async_copy(routes, named, arrived.at[0]),
+        pltpu.make_async_copy(route_weight, shares, arrived.at[1]),
+        pltpu.make_async_copy(tokens, packed.at[:, pl.ds(0, width)], arrived.at[2]),
+    ]
+    for copy in copies:
+        copy.start()
+    copies[0].wait()
+    copies[1].wait()
+    expert = lax.broadcasted_iota(jnp.int32, (LANES, tokens.shape[0]), 0)
+    share = shares[...].astype(jnp.float32) / 256.0
+    coef = jnp.zeros(expert.shape, jnp.float32)
+    for at in range(routes.shape[0]):
+        coef += jnp.where(expert == named[at : at + 1, :], share[at : at + 1, :], 0.0)
+    packed[:, width:] = coef.T.astype(jnp.bfloat16)
+    copies[2].wait()
 
 
 def pack(tokens, routes, route_weight):
     rows, width = tokens.shape
-    whole = pl.BlockSpec(memory_space=pltpu.VMEM)
+    arrays = [pltpu.with_memory_space_constraint(a, pltpu.HBM) for a in (tokens, routes.T, route_weight.T)]
     return pl.pallas_call(
         pack_kernel,
-        in_specs=[whole] * 3,
-        out_specs=whole,
-        out_shape=jax.ShapeDtypeStruct((rows, width + LANES), jnp.bfloat16),
+        in_specs=[pl.BlockSpec(memory_space=pltpu.HBM)] * 3,
+        out_specs=pl.BlockSpec(memory_space=pltpu.VMEM),
+        out_shape=pltpu.VMEM((rows, width + LANES), jnp.bfloat16),
+        scratch_shapes=[pltpu.VMEM(a.shape, a.dtype) for a in arrays[1:]] + [pltpu.SemaphoreType.DMA((3,))],
         compiler_params=pltpu.CompilerParams(vmem_limit_bytes=2 << 20),
-    )(tokens, routes, route_weight)
+    )(*arrays)
 
 
 def experts_kernel(ids, *refs, units, held):
@@ -75,13 +85,14 @@
     width = weights[0].shape[0]
     count = blocks[0].shape[0]
     lane = lax.broadcasted_iota(jnp.int32, (1, LANES), 1)
-    coefs = jnp.concatenate([block[:, width:] for block in blocks], axis=0).astype(jnp.float32)
+    repeat = max(1, LANES // (2 * units * count))
+    coefs = jnp.concatenate([block[:, width:] for block in blocks] * repeat, axis=0).astype(jnp.float32)
     hidden = []
     for at in range(held):
         w_gate, w_up, _ = weights[3 * at : 3 * at + 3]
         gate_vals = up_vals = None
         for start, size in pieces(width):
-            rows = jnp.concatenate([block[:, start : start + size] for block in blocks], axis=0)
+            rows = jnp.concatenate([block[:, start : start + size] for block in blocks] * repeat, axis=0)
             gate_part = jnp.dot(rows, w_gate[start : start + size, :], preferred_element_type=jnp.float32)
             up_part = jnp.dot(rows, w_up[start : start + size, :], preferred_element_type=jnp.float32)
             gate_vals = gate_part if gate_vals is None else gate_vals + gate_part
@@ -140,6 +151,11 @@
     return sorted(range(1, layers), key=lambda count: min(count, layers - count))
 
 
+def calls_of(layers):
+    shifts = shifts_of(layers)
+    return [[shifts[0], 0]] + [shifts[at : at + 2][::-1] for at in range(1, len(shifts), 2)]
+
+
 def layer(tokens, routes, route_weight, gate_weight, up_weight, down_weight):
     row_count, _ = tokens.shape
     nodes = lax.axis_size("node")
@@ -166,20 +182,20 @@
         near = jnp.concatenate([unit, beside], axis=0)
         blocks[count] = (near, send(near, second_partner))
     sums = {}
-    for count in shifts:
-        together = [count, 0] if count == shifts[0] else [count]
+    for together in calls_of(layers):
         outs = run_experts(ids, [block for unit in together for block in blocks[unit]], weights)
         for at, unit in enumerate(together):
             sums[unit] = outs[2 * at : 2 * at + 2]
     result = None
-    for count in shifts + [0]:
+    for count in [unit for call in calls_of(layers) for unit in call if unit] + [0]:
         kept, sent = sums[count]
         back = send(sent, second_partner)
         out = kept + back
         back = send(out[row_count:].astype(jnp.bfloat16), first_partner)
         out = out[:row_count] + back
+        out = out.astype(jnp.bfloat16) if count else out
         if count:
-            out = send(out.astype(jnp.bfloat16), layer_shift(layers, -count)).astype(jnp.float32)
+            out = send(out, layer_shift(layers, -count)).astype(jnp.float32)
         result = out if result is None else result + out
     return result.astype(jnp.bfloat16)
 

time: 118 us -> 113 us (0.958)
  starting transfers between devices: 21.9 us -> 30.2 us
  local copies, waits for them, and re-layouts: 8.97 us -> 2.13 us
  Pallas kernels: 22.2 us -> 17 us
  waiting for transfers between devices: 63.4 us -> 61.5 us
    ppermute x25, starting transfers between devices: 21.9 us -> 30.2 us  [send(): return lax.ppermute(block, ('rail', 'node'), route)]
    unnamed x19 -> x5, local copies, waits for them, and re-layouts: 8.8 us -> 1.96 us
    pallas_call x3 -> x2, Pallas kernels: 12.9 us -> 7.54 us  [run_experts(): pl.pallas_call(functools.partial(experts_kernel, units=len(blocks) // 2,...]
    ppermute x25, waiting for transfers between devices: 63.4 us -> 61.5 us  [send(): return lax.ppermute(block, ('rail', 'node'), route)]
  transfers between devices with their start and end apart: 25 -> 25, of which waited for: 12 -> 14; matrix products, arithmetic and copies ran while one was open for 1% -> 1% of each run, Pallas kernels for 19% -> 14%
where the time goes in v4:
time: 113 us; the launch traced here: 112 us
  waiting for transfers between devices  61.5 us (54%)
  starting transfers between devices  30.2 us (27%)
  Pallas kernels  17 us (15%)
  local copies, waits for them, and re-layouts  2.13 us (2%)
  other arithmetic  1.38 us (1%)
    ppermute x25, waiting for transfers between devices, send(): return lax.ppermute(block, ('rail', 'node'), route)  61.5 us
    ppermute x25, starting transfers between devices, send(): return lax.ppermute(block, ('rail', 'node'), route)  30.2 us
    pallas_call x2, Pallas kernels, stage(): pl.pallas_call(stage_kernel, in_specs=[pl.BlockSpec(memory_space=pltpu.HB...  8.45 us
    pallas_call x2, Pallas kernels, run_experts(): pl.pallas_call(functools.partial(experts_kernel, units=len(blocks) // 2,...  7.54 us
  transfers between devices with their start and end apart: 25, of which 14 were waited for; matrix products, arithmetic and copies ran while one was open for 1% of the time, Pallas kernels for 14%

profile of v4, /device:TPU:0, one launch (start us, length us, event | category | flops | bytes accessed | tf_op | source)
XLA Modules:
  0.0 112.5 jit_solution(5599396586053403383)
XLA Ops:
  0.0 1.0 shard_map.64
  1.0 3.0 %collective-permute-start.3 = (bf16[16,7296]{1,0:T(8,128)(2,1)S(1)}, bf16[16,7296]{1,0:T(8,128)(2,1)S(1)}, u32[]{:S(2)}, u32[]{:S(2)}) collective-permute-start(bf16[16,7296]{1,0:T(8,128)(2,1)S(1)} %shard_map.64), channel_id=1, source_target_pairs={{0,2},{1,5},{2,0},{3,7},{4,6},{5,1},{6,4},{7,3},{8,10},{9,13},{10,... | collective-permute-start | bytes 700424 | tf_op jit(solution)/shard_map/ppermute | solution.py:24
  4.0 1.6 %collective-permute-start = (bf16[16,7296]{1,0:T(8,128)(2,1)S(1)}, bf16[16,7296]{1,0:T(8,128)(2,1)S(1)}, u32[]{:S(2)}, u32[]{:S(2)}) collective-permute-start(bf16[16,7296]{1,0:T(8,128)(2,1)S(1)} %shard_map.64), channel_id=1, source_target_pairs={{0,8},{1,9},{2,10},{3,11},{4,12},{5,13},{6,14},{7,15},{8,16},{9,17... | collective-permute-start | bytes 700424 | tf_op jit(solution)/shard_map/ppermute | solution.py:24
  5.6 2.2 %collective-permute-start.14 = (bf16[16,7296]{1,0:T(8,128)(2,1)S(1)}, bf16[16,7296]{1,0:T(8,128)(2,1)S(1)}, u32[]{:S(2)}, u32[]{:S(2)}) collective-permute-start(bf16[16,7296]{1,0:T(8,128)(2,1)S(1)} %shard_map.64), channel_id=1, source_target_pairs={{0,24},{1,25},{2,26},{3,27},{4,28},{5,29},{6,30},{7,31},{8,0},{9,1... | collective-permute-start | bytes 700424 | tf_op jit(solution)/shard_map/ppermute | solution.py:24
  7.9 0.0 collective-permute-start.5
  7.9 0.5 collective-permute-start.6
  8.4 0.0 collective-permute-done.3
  8.4 0.0 collective-permute-start.7
  8.4 6.0 %collective-permute-done = bf16[16,7296]{1,0:T(8,128)(2,1)S(1)} collective-permute-done((bf16[16,7296]{1,0:T(8,128)(2,1)S(1)}, bf16[16,7296]{1,0:T(8,128)(2,1)S(1)}, u32[]{:S(2)}, u32[]{:S(2)}) %collective-permute-start) | collective-permute-done | bytes 233504 | tf_op jit(solution)/shard_map/ppermute | solution.py:24
  14.4 1.5 %collective-permute-start.4 = (bf16[32,7296]{1,0:T(8,128)(2,1)S(1)}, bf16[32,7296]{1,0:T(8,128)(2,1)S(1)}, u32[]{:S(2)}, u32[]{:S(2)}) collective-permute-start(bf16[32,7296]{1,0:T(8,128)(2,1)S(1)} %pad_maximum_fusion.refs_2_), channel_id=1, source_target_pairs={{0,4},{1,3},{2,6},{3,1},{4,0},{5,7},{6,2},{7,5},{8,12},{9,11},{10,... | collective-permute-start | bytes 1400840 | tf_op jit(solution)/shard_map/ppermute | solution.py:24
  15.9 1.6 %collective-permute-done.14 = bf16[16,7296]{1,0:T(8,128)(2,1)S(1)} collective-permute-done((bf16[16,7296]{1,0:T(8,128)(2,1)S(1)}, bf16[16,7296]{1,0:T(8,128)(2,1)S(1)}, u32[]{:S(2)}, u32[]{:S(2)}) %collective-permute-start.14) | collective-permute-done | bytes 233504 | tf_op jit(solution)/shard_map/ppermute | solution.py:24
  17.5 1.1 %collective-permute-start.11 = (bf16[16,7296]{1,0:T(8,128)(2,1)S(1)}, bf16[16,7296]{1,0:T(8,128)(2,1)S(1)}, u32[]{:S(2)}, u32[]{:S(2)}) collective-permute-start(bf16[16,7296]{1,0:T(8,128)(2,1)S(1)} %collective-permute-done), channel_id=1, source_target_pairs={{0,8},{1,9},{2,10},{3,11},{4,12},{5,13},{6,14},{7,15},{8,16},{9,17... | collective-permute-start | bytes 700424 | tf_op jit(solution)/shard_map/ppermute | solution.py:24
  18.7 7.7 %collective-permute-done.11 = bf16[16,7296]{1,0:T(8,128)(2,1)S(1)} collective-permute-done((bf16[16,7296]{1,0:T(8,128)(2,1)S(1)}, bf16[16,7296]{1,0:T(8,128)(2,1)S(1)}, u32[]{:S(2)}, u32[]{:S(2)}) %collective-permute-start.11) | collective-permute-done | bytes 233504 | tf_op jit(solution)/shard_map/ppermute | solution.py:24
  26.4 1.5 %collective-permute-start.1 = (bf16[16,7296]{1,0:T(8,128)(2,1)S(1)}, bf16[16,7296]{1,0:T(8,128)(2,1)S(1)}, u32[]{:S(2)}, u32[]{:S(2)}) collective-permute-start(bf16[16,7296]{1,0:T(8,128)(2,1)S(1)} %collective-permute-done), channel_id=1, source_target_pairs={{0,2},{1,5},{2,0},{3,7},{4,6},{5,1},{6,4},{7,3},{8,10},{9,13},{10,... | collective-permute-start | bytes 700424 | tf_op jit(solution)/shard_map/ppermute | solution.py:24
  27.9 4.6 %collective-permute-done.1 = bf16[16,7296]{1,0:T(8,128)(2,1)S(1)} collective-permute-done((bf16[16,7296]{1,0:T(8,128)(2,1)S(1)}, bf16[16,7296]{1,0:T(8,128)(2,1)S(1)}, u32[]{:S(2)}, u32[]{:S(2)}) %collective-permute-start.1) | collective-permute-done | bytes 233504 | tf_op jit(solution)/shard_map/ppermute | solution.py:24
  32.4 1.5 %collective-permute-start.15 = (bf16[16,7296]{1,0:T(8,128)(2,1)S(1)}, bf16[16,7296]{1,0:T(8,128)(2,1)S(1)}, u32[]{:S(2)}, u32[]{:S(2)}) collective-permute-start(bf16[16,7296]{1,0:T(8,128)(2,1)S(1)} %collective-permute-done.14), channel_id=1, source_target_pairs={{0,2},{1,5},{2,0},{3,7},{4,6},{5,1},{6,4},{7,3},{8,10},{9,13},{10,... | collective-permute-start | bytes 700424 | tf_op jit(solution)/shard_map/ppermute | solution.py:24
  33.9 4.6 %collective-permute-done.15 = bf16[16,7296]{1,0:T(8,128)(2,1)S(1)} collective-permute-done((bf16[16,7296]{1,0:T(8,128)(2,1)S(1)}, bf16[16,7296]{1,0:T(8,128)(2,1)S(1)}, u32[]{:S(2)}, u32[]{:S(2)}) %collective-permute-start.15) | collective-permute-done | bytes 233504 | tf_op jit(solution)/shard_map/ppermute | solution.py:24
  38.5 1.5 %collective-permute-start.12 = (bf16[16,7296]{1,0:T(8,128)(2,1)S(1)}, bf16[16,7296]{1,0:T(8,128)(2,1)S(1)}, u32[]{:S(2)}, u32[]{:S(2)}) collective-permute-start(bf16[16,7296]{1,0:T(8,128)(2,1)S(1)} %collective-permute-done.11), channel_id=1, source_target_pairs={{0,2},{1,5},{2,0},{3,7},{4,6},{5,1},{6,4},{7,3},{8,10},{9,13},{10,... | collective-permute-start | bytes 700424 | tf_op jit(solution)/shard_map/ppermute | solution.py:24
  40.0 6.5 %collective-permute-done.12 = bf16[16,7296]{1,0:T(8,128)(2,1)S(1)} collective-permute-done((bf16[16,7296]{1,0:T(8,128)(2,1)S(1)}, bf16[16,7296]{1,0:T(8,128)(2,1)S(1)}, u32[]{:S(2)}, u32[]{:S(2)}) %collective-permute-start.12) | collective-permute-done | bytes 233504 | tf_op jit(solution)/shard_map/ppermute | solution.py:24
  46.5 0.6 collective-permute-start.2
  47.1 0.0 collective-permute-done.5.refs_0_
  47.2 1.5 %collective-permute-start.16 = (bf16[32,7296]{1,0:T(8,128)(2,1)S(1)}, bf16[32,7296]{1,0:T(8,128)(2,1)S(1)}, u32[]{:S(2)}, u32[]{:S(2)}) collective-permute-start(bf16[32,7296]{1,0:T(8,128)(2,1)S(1)} %constant_dynamic-update-slice_fusion.4.refs_2_), channel_id=1, source_target_pairs={{0,4},{1,3},{2,6},{3,1},{4,0},{5,7},{6,2},{7,5},{8,12},{9,11},{10,... | collective-permute-start | bytes 1400840 | tf_op jit(solution)/shard_map/ppermute | solution.py:24
  48.6 0.0 collective-permute-done.6.refs_1_
  48.7 0.6 collective-permute-start.13
  49.3 0.1 pad_add_fusion.ids
  49.3 4.2 %shard_map.65 = (bf16[7168,256]{1,0:T(8,128)(2,1)S(1)}, bf16[7168,256]{1,0:T(8,128)(2,1)S(1)}, bf16[256,7168]{1,0:T(8,128)(2,1)S(1)}) custom-call(bf16[7168,256]{1,0:T(8,128)(2,1)} %bitcast.8, bf16[7168,256]{1,0:T(8,128)(2,1)} %bitcast.10, bf16[256,7168]{1,0:T(8,128)(2,1)} %bitcast.12), custom_call_target="tpu_custom_call" | custom-call | tf_op jit(solution)/shard_map/pallas_call | solution.py:123
  53.6 0.0 collective-permute-done.7.refs_2_
  53.6 0.0 copy-start
  53.6 1.9 %copy-done = bf16[256,7168]{1,0:T(8,128)(2,1)} copy-done((bf16[256,7168]{1,0:T(8,128)(2,1)}, bf16[256,7168]{1,0:T(8,128)(2,1)S(1)}, u32[]{:S(2)}) %copy-start) | copy-done | bytes 3670040
  55.5 4.2 %shard_map.66 = (bf16[7168,256]{1,0:T(8,128)(2,1)S(1)}, bf16[7168,256]{1,0:T(8,128)(2,1)S(1)}, bf16[256,7168]{1,0:T(8,128)(2,1)S(1)}) custom-call(bf16[7168,256]{1,0:T(8,128)(2,1)} %collective-permute-done.5.refs_0_, bf16[7168,256]{1,0:T(8,128)(2,1)} %collective-permute-done.6.refs_1_, bf16[256,7168]{1,0:T(8,128)(2,1)} %copy-done), custom_call_target="tpu_custom_call" | custom-call | tf_op jit(solution)/shard_map/pallas_call | solution.py:123
  59.7 0.0 collective-permute-done.4.refs_3_
  59.7 0.0 collective-permute-done.2.refs_1_
  59.7 3.8 %shard_map.67 = (f32[32,7168]{1,0:T(8,128)S(1)}, bf16[32,7168]{1,0:T(8,128)(2,1)S(1)}, f32[32,7168]{1,0:T(8,128)S(1)}, bf16[32,7168]{1,0:T(8,128)(2,1)S(1)}) custom-call(s32[2]{0:T(128)S(1)} %pad_add_fusion.ids, bf16[32,7296]{1,0:T(8,128)(2,1)S(1)} %constant_dynamic-update-slice_fusion.refs_0_, bf16[32,7296]{1,0:T(8,128)(2,1)S(1)} %collective-permute-done.2.refs_1_, ...), custom_call_target="tpu_custom_call" | custom-call | flops 2818572288 | tf_op jit(solution)/shard_map/pallas_call | solution.py:138
  63.5 1.5 %collective-permute-start.8 = (bf16[32,7168]{1,0:T(8,128)(2,1)S(1)}, bf16[32,7168]{1,0:T(8,128)(2,1)S(1)}, u32[]{:S(2)}, u32[]{:S(2)}) collective-permute-start(bf16[32,7168]{1,0:T(8,128)(2,1)S(1)} %get-tuple-element.26), channel_id=1, source_target_pairs={{0,4},{1,3},{2,6},{3,1},{4,0},{5,7},{6,2},{7,5},{8,12},{9,11},{10,... | collective-permute-start | bytes 1376264 | tf_op jit(solution)/shard_map/ppermute | solution.py:24
  65.0 0.0 collective-permute-done.16.refs_3_
  65.0 0.1 collective-permute-done.13.refs_1_
  65.1 3.8 %shard_map.68 = (f32[32,7168]{1,0:T(8,128)S(1)}, bf16[32,7168]{1,0:T(8,128)(2,1)S(1)}, f32[32,7168]{1,0:T(8,128)S(1)}, bf16[32,7168]{1,0:T(8,128)(2,1)S(1)}) custom-call(s32[2]{0:T(128)S(1)} %pad_add_fusion.ids, bf16[32,7296]{1,0:T(8,128)(2,1)S(1)} %constant_dynamic-update-slice_fusion.2.refs_0_, bf16[32,7296]{1,0:T(8,128)(2,1)S(1)} %collective-permute-done.13.refs_1_, ...), custom_call_target="tpu_custom_call" | custom-call | flops 2818572288 | tf_op jit(solution)/shard_map/pallas_call | solution.py:138
  68.9 0.7 collective-permute-start.17
  69.5 1.4 %collective-permute-start.20 = (bf16[32,7168]{1,0:T(8,128)(2,1)S(1)}, bf16[32,7168]{1,0:T(8,128)(2,1)S(1)}, u32[]{:S(2)}, u32[]{:S(2)}) collective-permute-start(bf16[32,7168]{1,0:T(8,128)(2,1)S(1)} %get-tuple-element.30), channel_id=1, source_target_pairs={{0,4},{1,3},{2,6},{3,1},{4,0},{5,7},{6,2},{7,5},{8,12},{9,11},{10,... | collective-permute-start | bytes 1376264 | tf_op jit(solution)/shard_map/ppermute | solution.py:24
  71.0 0.6 collective-permute-start.23
  71.6 3.6 %collective-permute-done.8 = bf16[32,7168]{1,0:T(8,128)(2,1)S(1)} collective-permute-done((bf16[32,7168]{1,0:T(8,128)(2,1)S(1)}, bf16[32,7168]{1,0:T(8,128)(2,1)S(1)}, u32[]{:S(2)}, u32[]{:S(2)}) %collective-permute-start.8) | collective-permute-done | bytes 458784 | tf_op jit(solution)/shard_map/ppermute | solution.py:24
  75.1 0.1 convert_add_fusion.3
  75.2 1.5 %collective-permute-start.9 = (bf16[16,7168]{1,0:T(8,128)(2,1)S(1)}, bf16[16,7168]{1,0:T(8,128)(2,1)S(1)}, u32[]{:S(2)}, u32[]{:S(2)}) collective-permute-start(bf16[16,7168]{1,0:T(8,128)(2,1)S(1)} %slice.65), channel_id=1, source_target_pairs={{0,2},{1,5},{2,0},{3,7},{4,6},{5,1},{6,4},{7,3},{8,10},{9,13},{10,... | collective-permute-start | bytes 688136 | tf_op jit(solution)/shard_map/ppermute | solution.py:24
  76.8 7.6 %collective-permute-done.17 = bf16[32,7168]{1,0:T(8,128)(2,1)S(1)} collective-permute-done((bf16[32,7168]{1,0:T(8,128)(2,1)S(1)}, bf16[32,7168]{1,0:T(8,128)(2,1)S(1)}, u32[]{:S(2)}, u32[]{:S(2)}) %collective-permute-start.17) | collective-permute-done | bytes 458784 | tf_op jit(solution)/shard_map/ppermute | solution.py:24
  84.4 0.1 convert_add_fusion.2
  84.5 1.6 %collective-permute-start.18 = (bf16[16,7168]{1,0:T(8,128)(2,1)S(1)}, bf16[16,7168]{1,0:T(8,128)(2,1)S(1)}, u32[]{:S(2)}, u32[]{:S(2)}) collective-permute-start(bf16[16,7168]{1,0:T(8,128)(2,1)S(1)} %slice.64), channel_id=1, source_target_pairs={{0,2},{1,5},{2,0},{3,7},{4,6},{5,1},{6,4},{7,3},{8,10},{9,13},{10,... | collective-permute-start | bytes 688136 | tf_op jit(solution)/shard_map/ppermute | solution.py:24
  86.0 5.7 %collective-permute-done.20 = bf16[32,7168]{1,0:T(8,128)(2,1)S(1)} collective-permute-done((bf16[32,7168]{1,0:T(8,128)(2,1)S(1)}, bf16[32,7168]{1,0:T(8,128)(2,1)S(1)}, u32[]{:S(2)}, u32[]{:S(2)}) %collective-permute-start.20) | collective-permute-done | bytes 458784 | tf_op jit(solution)/shard_map/ppermute | solution.py:24
  91.7 0.1 convert_add_fusion.1
  91.8 1.6 %collective-permute-start.21 = (bf16[16,7168]{1,0:T(8,128)(2,1)S(1)}, bf16[16,7168]{1,0:T(8,128)(2,1)S(1)}, u32[]{:S(2)}, u32[]{:S(2)}) collective-permute-start(bf16[16,7168]{1,0:T(8,128)(2,1)S(1)} %slice.63), channel_id=1, source_target_pairs={{0,2},{1,5},{2,0},{3,7},{4,6},{5,1},{6,4},{7,3},{8,10},{9,13},{10,... | collective-permute-start | bytes 688136 | tf_op jit(solution)/shard_map/ppermute | solution.py:24
  93.4 3.2 %collective-permute-done.23 = bf16[32,7168]{1,0:T(8,128)(2,1)S(1)} collective-permute-done((bf16[32,7168]{1,0:T(8,128)(2,1)S(1)}, bf16[32,7168]{1,0:T(8,128)(2,1)S(1)}, u32[]{:S(2)}, u32[]{:S(2)}) %collective-permute-start.23) | collective-permute-done | bytes 458784 | tf_op jit(solution)/shard_map/ppermute | solution.py:24
  96.6 0.1 convert_add_fusion
  96.8 1.6 %collective-permute-start.24 = (bf16[16,7168]{1,0:T(8,128)(2,1)S(1)}, bf16[16,7168]{1,0:T(8,128)(2,1)S(1)}, u32[]{:S(2)}, u32[]{:S(2)}) collective-permute-start(bf16[16,7168]{1,0:T(8,128)(2,1)S(1)} %slice.62), channel_id=1, source_target_pairs={{0,2},{1,5},{2,0},{3,7},{4,6},{5,1},{6,4},{7,3},{8,10},{9,13},{10,... | collective-permute-start | bytes 688136 | tf_op jit(solution)/shard_map/ppermute | solution.py:24
  98.3 0.0 collective-permute-done.9
  98.4 1.3 %collective-permute-start.10 = (bf16[16,7168]{1,0:T(8,128)(2,1)S(1)}, bf16[16,7168]{1,0:T(8,128)(2,1)S(1)}, u32[]{:S(2)}, u32[]{:S(2)}) collective-permute-start(bf16[16,7168]{1,0:T(8,128)(2,1)S(1)} %fusion.4), channel_id=1, source_target_pairs={{0,24},{1,25},{2,26},{3,27},{4,28},{5,29},{6,30},{7,31},{8,0},{9,1... | collective-permute-start | bytes 688136 | tf_op jit(solution)/shard_map/ppermute | solution.py:24
  99.7 0.0 collective-permute-done.18
  99.7 0.1 collective-permute-start.19
  99.8 0.0 collective-permute-done.21
  99.9 1.3 %collective-permute-start.22 = (bf16[16,7168]{1,0:T(8,128)(2,1)S(1)}, bf16[16,7168]{1,0:T(8,128)(2,1)S(1)}, u32[]{:S(2)}, u32[]{:S(2)}) collective-permute-start(bf16[16,7168]{1,0:T(8,128)(2,1)S(1)} %fusion.2), channel_id=1, source_target_pairs={{0,8},{1,9},{2,10},{3,11},{4,12},{5,13},{6,14},{7,15},{8,16},{9,17... | collective-permute-start | bytes 688136 | tf_op jit(solution)/shard_map/ppermute | solution.py:24
  101.2 1.7 %collective-permute-done.24 = bf16[16,7168]{1,0:T(8,128)(2,1)S(1)} collective-permute-done((bf16[16,7168]{1,0:T(8,128)(2,1)S(1)}, bf16[16,7168]{1,0:T(8,128)(2,1)S(1)}, u32[]{:S(2)}, u32[]{:S(2)}) %collective-permute-start.24) | collective-permute-done | bytes 229408 | tf_op jit(solution)/shard_map/ppermute | solution.py:24
  102.8 1.9 %collective-permute-done.10 = bf16[16,7168]{1,0:T(8,128)(2,1)S(1)} collective-permute-done((bf16[16,7168]{1,0:T(8,128)(2,1)S(1)}, bf16[16,7168]{1,0:T(8,128)(2,1)S(1)}, u32[]{:S(2)}, u32[]{:S(2)}) %collective-permute-start.10) | collective-permute-done | bytes 229408 | tf_op jit(solution)/shard_map/ppermute | solution.py:24
  104.7 6.9 %collective-permute-done.19 = bf16[16,7168]{1,0:T(8,128)(2,1)S(1)} collective-permute-done((bf16[16,7168]{1,0:T(8,128)(2,1)S(1)}, bf16[16,7168]{1,0:T(8,128)(2,1)S(1)}, u32[]{:S(2)}, u32[]{:S(2)}) %collective-permute-start.19) | collective-permute-done | bytes 229408 | tf_op jit(solution)/shard_map/ppermute | solution.py:24
  111.6 0.0 collective-permute-done.22
  111.6 0.8 fusion.1
  (14 shorter events, 0.4 us)
Async XLA Ops:
  1.0 7.4 %collective-permute-start.3 = (bf16[16,7296]{1,0:T(8,128)(2,1)S(1)}, bf16[16,7296]{1,0:T(8,128)(2,1)S(1)}, u32[]{:S(2)}, u32[]{:S(2)}) collective-permute-start(bf16[16,7296]{1,0:T(8,128)(2,1)S(1)} %shard_map.64), channel_id=1, source_target_pairs={{0,2},{1,5},{2,0},{3,7},{4,6},{5,1},{6,4},{7,3},{8,10},{9,13},{10,... | collective-permute-start | bytes 700424 | tf_op jit(solution)/shard_map/ppermute | solution.py:24
  4.0 10.4 %collective-permute-start = (bf16[16,7296]{1,0:T(8,128)(2,1)S(1)}, bf16[16,7296]{1,0:T(8,128)(2,1)S(1)}, u32[]{:S(2)}, u32[]{:S(2)}) collective-permute-start(bf16[16,7296]{1,0:T(8,128)(2,1)S(1)} %shard_map.64), channel_id=1, source_target_pairs={{0,8},{1,9},{2,10},{3,11},{4,12},{5,13},{6,14},{7,15},{8,16},{9,17... | collective-permute-start | bytes 700424 | tf_op jit(solution)/shard_map/ppermute | solution.py:24
  5.6 11.9 %collective-permute-start.14 = (bf16[16,7296]{1,0:T(8,128)(2,1)S(1)}, bf16[16,7296]{1,0:T(8,128)(2,1)S(1)}, u32[]{:S(2)}, u32[]{:S(2)}) collective-permute-start(bf16[16,7296]{1,0:T(8,128)(2,1)S(1)} %shard_map.64), channel_id=1, source_target_pairs={{0,24},{1,25},{2,26},{3,27},{4,28},{5,29},{6,30},{7,31},{8,0},{9,1... | collective-permute-start | bytes 700424 | tf_op jit(solution)/shard_map/ppermute | solution.py:24
  7.9 39.3 %collective-permute-start.5 = (bf16[7168,256]{1,0:T(8,128)(2,1)}, bf16[7168,256]{1,0:T(8,128)(2,1)}, u32[]{:S(2)}, u32[]{:S(2)}) collective-permute-start(bf16[7168,256]{1,0:T(8,128)(2,1)} %bitcast.7), channel_id=1, source_target_pairs={{0,1},{1,0},{2,3},{3,2},{4,5},{5,4},{6,7},{7,6},{8,9},{9,8},{10,11... | collective-permute-start | bytes 11010056 | tf_op jit(solution)/shard_map/ppermute | solution.py:24
  7.9 40.8 %collective-permute-start.6 = (bf16[7168,256]{1,0:T(8,128)(2,1)}, bf16[7168,256]{1,0:T(8,128)(2,1)}, u32[]{:S(2)}, u32[]{:S(2)}) collective-permute-start(bf16[7168,256]{1,0:T(8,128)(2,1)} %bitcast.9), channel_id=1, source_target_pairs={{0,1},{1,0},{2,3},{3,2},{4,5},{5,4},{6,7},{7,6},{8,9},{9,8},{10,11... | collective-permute-start | bytes 11010056 | tf_op jit(solution)/shard_map/ppermute | solution.py:24
  8.4 45.2 %collective-permute-start.7 = (bf16[256,7168]{1,0:T(8,128)(2,1)}, bf16[256,7168]{1,0:T(8,128)(2,1)S(1)}, u32[]{:S(2)}, u32[]{:S(2)}) collective-permute-start(bf16[256,7168]{1,0:T(8,128)(2,1)} %bitcast.11), channel_id=1, source_target_pairs={{0,1},{1,0},{2,3},{3,2},{4,5},{5,4},{6,7},{7,6},{8,9},{9,8},{10,11... | collective-permute-start | bytes 11010056 | tf_op jit(solution)/shard_map/ppermute | solution.py:24
  14.4 45.3 %collective-permute-start.4 = (bf16[32,7296]{1,0:T(8,128)(2,1)S(1)}, bf16[32,7296]{1,0:T(8,128)(2,1)S(1)}, u32[]{:S(2)}, u32[]{:S(2)}) collective-permute-start(bf16[32,7296]{1,0:T(8,128)(2,1)S(1)} %pad_maximum_fusion.refs_2_), channel_id=1, source_target_pairs={{0,4},{1,3},{2,6},{3,1},{4,0},{5,7},{6,2},{7,5},{8,12},{9,11},{10,... | collective-permute-start | bytes 1400840 | tf_op jit(solution)/shard_map/ppermute | solution.py:24
  17.5 8.8 %collective-permute-start.11 = (bf16[16,7296]{1,0:T(8,128)(2,1)S(1)}, bf16[16,7296]{1,0:T(8,128)(2,1)S(1)}, u32[]{:S(2)}, u32[]{:S(2)}) collective-permute-start(bf16[16,7296]{1,0:T(8,128)(2,1)S(1)} %collective-permute-done), channel_id=1, source_target_pairs={{0,8},{1,9},{2,10},{3,11},{4,12},{5,13},{6,14},{7,15},{8,16},{9,17... | collective-permute-start | bytes 700424 | tf_op jit(solution)/shard_map/ppermute | solution.py:24
  26.4 6.1 %collective-permute-start.1 = (bf16[16,7296]{1,0:T(8,128)(2,1)S(1)}, bf16[16,7296]{1,0:T(8,128)(2,1)S(1)}, u32[]{:S(2)}, u32[]{:S(2)}) collective-permute-start(bf16[16,7296]{1,0:T(8,128)(2,1)S(1)} %collective-permute-done), channel_id=1, source_target_pairs={{0,2},{1,5},{2,0},{3,7},{4,6},{5,1},{6,4},{7,3},{8,10},{9,13},{10,... | collective-permute-start | bytes 700424 | tf_op jit(solution)/shard_map/ppermute | solution.py:24
  32.4 6.1 %collective-permute-start.15 = (bf16[16,7296]{1,0:T(8,128)(2,1)S(1)}, bf16[16,7296]{1,0:T(8,128)(2,1)S(1)}, u32[]{:S(2)}, u32[]{:S(2)}) collective-permute-start(bf16[16,7296]{1,0:T(8,128)(2,1)S(1)} %collective-permute-done.14), channel_id=1, source_target_pairs={{0,2},{1,5},{2,0},{3,7},{4,6},{5,1},{6,4},{7,3},{8,10},{9,13},{10,... | collective-permute-start | bytes 700424 | tf_op jit(solution)/shard_map/ppermute | solution.py:24
  38.5 8.0 %collective-permute-start.12 = (bf16[16,7296]{1,0:T(8,128)(2,1)S(1)}, bf16[16,7296]{1,0:T(8,128)(2,1)S(1)}, u32[]{:S(2)}, u32[]{:S(2)}) collective-permute-start(bf16[16,7296]{1,0:T(8,128)(2,1)S(1)} %collective-permute-done.11), channel_id=1, source_target_pairs={{0,2},{1,5},{2,0},{3,7},{4,6},{5,1},{6,4},{7,3},{8,10},{9,13},{10,... | collective-permute-start | bytes 700424 | tf_op jit(solution)/shard_map/ppermute | solution.py:24
  46.5 13.2 %collective-permute-start.2 = (bf16[32,7296]{1,0:T(8,128)(2,1)S(1)}, bf16[32,7296]{1,0:T(8,128)(2,1)S(1)}, u32[]{:S(2)}, u32[]{:S(2)}) collective-permute-start(bf16[32,7296]{1,0:T(8,128)(2,1)S(1)} %constant_dynamic-update-slice_fusion.refs_0_), channel_id=1, source_target_pairs={{0,4},{1,3},{2,6},{3,1},{4,0},{5,7},{6,2},{7,5},{8,12},{9,11},{10,... | collective-permute-start | bytes 1400840 | tf_op jit(solution)/shard_map/ppermute | solution.py:24
  47.2 17.9 %collective-permute-start.16 = (bf16[32,7296]{1,0:T(8,128)(2,1)S(1)}, bf16[32,7296]{1,0:T(8,128)(2,1)S(1)}, u32[]{:S(2)}, u32[]{:S(2)}) collective-permute-start(bf16[32,7296]{1,0:T(8,128)(2,1)S(1)} %constant_dynamic-update-slice_fusion.4.refs_2_), channel_id=1, source_target_pairs={{0,4},{1,3},{2,6},{3,1},{4,0},{5,7},{6,2},{7,5},{8,12},{9,11},{10,... | collective-permute-start | bytes 1400840 | tf_op jit(solution)/shard_map/ppermute | solution.py:24
  48.7 16.4 %collective-permute-start.13 = (bf16[32,7296]{1,0:T(8,128)(2,1)S(1)}, bf16[32,7296]{1,0:T(8,128)(2,1)S(1)}, u32[]{:S(2)}, u32[]{:S(2)}) collective-permute-start(bf16[32,7296]{1,0:T(8,128)(2,1)S(1)} %constant_dynamic-update-slice_fusion.2.refs_0_), channel_id=1, source_target_pairs={{0,4},{1,3},{2,6},{3,1},{4,0},{5,7},{6,2},{7,5},{8,12},{9,11},{10,... | collective-permute-start | bytes 1400840 | tf_op jit(solution)/shard_map/ppermute | solution.py:24
  53.6 1.9 %copy-start = (bf16[256,7168]{1,0:T(8,128)(2,1)}, bf16[256,7168]{1,0:T(8,128)(2,1)S(1)}, u32[]{:S(2)}) copy-start(bf16[256,7168]{1,0:T(8,128)(2,1)S(1)} %collective-permute-done.7.refs_2_) | copy-start | bytes 11010052
  63.5 11.6 %collective-permute-start.8 = (bf16[32,7168]{1,0:T(8,128)(2,1)S(1)}, bf16[32,7168]{1,0:T(8,128)(2,1)S(1)}, u32[]{:S(2)}, u32[]{:S(2)}) collective-permute-start(bf16[32,7168]{1,0:T(8,128)(2,1)S(1)} %get-tuple-element.26), channel_id=1, source_target_pairs={{0,4},{1,3},{2,6},{3,1},{4,0},{5,7},{6,2},{7,5},{8,12},{9,11},{10,... | collective-permute-start | bytes 1376264 | tf_op jit(solution)/shard_map/ppermute | solution.py:24
  68.9 15.5 %collective-permute-start.17 = (bf16[32,7168]{1,0:T(8,128)(2,1)S(1)}, bf16[32,7168]{1,0:T(8,128)(2,1)S(1)}, u32[]{:S(2)}, u32[]{:S(2)}) collective-permute-start(bf16[32,7168]{1,0:T(8,128)(2,1)S(1)} %get-tuple-element.28), channel_id=1, source_target_pairs={{0,4},{1,3},{2,6},{3,1},{4,0},{5,7},{6,2},{7,5},{8,12},{9,11},{10,... | collective-permute-start | bytes 1376264 | tf_op jit(solution)/shard_map/ppermute | solution.py:24
  69.5 22.2 %collective-permute-start.20 = (bf16[32,7168]{1,0:T(8,128)(2,1)S(1)}, bf16[32,7168]{1,0:T(8,128)(2,1)S(1)}, u32[]{:S(2)}, u32[]{:S(2)}) collective-permute-start(bf16[32,7168]{1,0:T(8,128)(2,1)S(1)} %get-tuple-element.30), channel_id=1, source_target_pairs={{0,4},{1,3},{2,6},{3,1},{4,0},{5,7},{6,2},{7,5},{8,12},{9,11},{10,... | collective-permute-start | bytes 1376264 | tf_op jit(solution)/shard_map/ppermute | solution.py:24
  71.0 25.7 %collective-permute-start.23 = (bf16[32,7168]{1,0:T(8,128)(2,1)S(1)}, bf16[32,7168]{1,0:T(8,128)(2,1)S(1)}, u32[]{:S(2)}, u32[]{:S(2)}) collective-permute-start(bf16[32,7168]{1,0:T(8,128)(2,1)S(1)} %get-tuple-element.32), channel_id=1, source_target_pairs={{0,4},{1,3},{2,6},{3,1},{4,0},{5,7},{6,2},{7,5},{8,12},{9,11},{10,... | collective-permute-start | bytes 1376264 | tf_op jit(solution)/shard_map/ppermute | solution.py:24
  75.2 23.1 %collective-permute-start.9 = (bf16[16,7168]{1,0:T(8,128)(2,1)S(1)}, bf16[16,7168]{1,0:T(8,128)(2,1)S(1)}, u32[]{:S(2)}, u32[]{:S(2)}) collective-permute-start(bf16[16,7168]{1,0:T(8,128)(2,1)S(1)} %slice.65), channel_id=1, source_target_pairs={{0,2},{1,5},{2,0},{3,7},{4,6},{5,1},{6,4},{7,3},{8,10},{9,13},{10,... | collective-permute-start | bytes 688136 | tf_op jit(solution)/shard_map/ppermute | solution.py:24
  84.5 15.2 %collective-permute-start.18 = (bf16[16,7168]{1,0:T(8,128)(2,1)S(1)}, bf16[16,7168]{1,0:T(8,128)(2,1)S(1)}, u32[]{:S(2)}, u32[]{:S(2)}) collective-permute-start(bf16[16,7168]{1,0:T(8,128)(2,1)S(1)} %slice.64), channel_id=1, source_target_pairs={{0,2},{1,5},{2,0},{3,7},{4,6},{5,1},{6,4},{7,3},{8,10},{9,13},{10,... | collective-permute-start | bytes 688136 | tf_op jit(solution)/shard_map/ppermute | solution.py:24
  91.8 8.0 %collective-permute-start.21 = (bf16[16,7168]{1,0:T(8,128)(2,1)S(1)}, bf16[16,7168]{1,0:T(8,128)(2,1)S(1)}, u32[]{:S(2)}, u32[]{:S(2)}) collective-permute-start(bf16[16,7168]{1,0:T(8,128)(2,1)S(1)} %slice.63), channel_id=1, source_target_pairs={{0,2},{1,5},{2,0},{3,7},{4,6},{5,1},{6,4},{7,3},{8,10},{9,13},{10,... | collective-permute-start | bytes 688136 | tf_op jit(solution)/shard_map/ppermute | solution.py:24
  96.8 6.1 %collective-permute-start.24 = (bf16[16,7168]{1,0:T(8,128)(2,1)S(1)}, bf16[16,7168]{1,0:T(8,128)(2,1)S(1)}, u32[]{:S(2)}, u32[]{:S(2)}) collective-permute-start(bf16[16,7168]{1,0:T(8,128)(2,1)S(1)} %slice.62), channel_id=1, source_target_pairs={{0,2},{1,5},{2,0},{3,7},{4,6},{5,1},{6,4},{7,3},{8,10},{9,13},{10,... | collective-permute-start | bytes 688136 | tf_op jit(solution)/shard_map/ppermute | solution.py:24
  98.4 6.4 %collective-permute-start.10 = (bf16[16,7168]{1,0:T(8,128)(2,1)S(1)}, bf16[16,7168]{1,0:T(8,128)(2,1)S(1)}, u32[]{:S(2)}, u32[]{:S(2)}) collective-permute-start(bf16[16,7168]{1,0:T(8,128)(2,1)S(1)} %fusion.4), channel_id=1, source_target_pairs={{0,24},{1,25},{2,26},{3,27},{4,28},{5,29},{6,30},{7,31},{8,0},{9,1... | collective-permute-start | bytes 688136 | tf_op jit(solution)/shard_map/ppermute | solution.py:24
  99.7 11.9 %collective-permute-start.19 = (bf16[16,7168]{1,0:T(8,128)(2,1)S(1)}, bf16[16,7168]{1,0:T(8,128)(2,1)S(1)}, u32[]{:S(2)}, u32[]{:S(2)}) collective-permute-start(bf16[16,7168]{1,0:T(8,128)(2,1)S(1)} %fusion.3), channel_id=1, source_target_pairs={{0,16},{1,17},{2,18},{3,19},{4,20},{5,21},{6,22},{7,23},{8,24},{9,... | collective-permute-start | bytes 688136 | tf_op jit(solution)/shard_map/ppermute | solution.py:24
  99.9 11.8 %collective-permute-start.22 = (bf16[16,7168]{1,0:T(8,128)(2,1)S(1)}, bf16[16,7168]{1,0:T(8,128)(2,1)S(1)}, u32[]{:S(2)}, u32[]{:S(2)}) collective-permute-start(bf16[16,7168]{1,0:T(8,128)(2,1)S(1)} %fusion.2), channel_id=1, source_target_pairs={{0,8},{1,9},{2,10},{3,11},{4,12},{5,13},{6,14},{7,15},{8,16},{9,17... | collective-permute-start | bytes 688136 | tf_op jit(solution)/shard_map/ppermute | solution.py:24

commit v5 on v4

--- a/solution.py
+++ b/solution.py
@@ -12,6 +12,7 @@
 LANES = 128
 PLANE = 4
 CHUNK = 1024
+SIDE_IN = False
 
 
 def send(block, target):
@@ -43,16 +44,23 @@
     return lambda rail, node: (rail, (node + count) % nodes)
 
 
-def pieces(width):
-    return [(start, min(CHUNK, width - start)) for start in range(0, width, CHUNK)]
+def pieces(first, end):
+    return [(start, min(CHUNK, end - start)) for start in range(first, end, CHUNK)]
+
+
+def side_of(width):
+    return width // LANES // 7 * LANES
 
 
 def pack_kernel(tokens, routes, route_weight, packed, named, shares, arrived):
     width = tokens.shape[1]
+    main = width - side_of(width)
+    side = pl.ds(main, width - main)
     copies = [
         pltpu.make_async_copy(routes, named, arrived.at[0]),
         pltpu.make_async_copy(route_weight, shares, arrived.at[1]),
-        pltpu.make_async_copy(tokens, packed.at[:, pl.ds(0, width)], arrived.at[2]),
+        pltpu.make_async_copy(tokens.at[:, pl.ds(0, main)], packed.at[:, pl.ds(0, main)], arrived.at[2]),
+        pltpu.make_async_copy(tokens.at[:, side], packed.at[:, pl.ds(main + LANES, width - main)], arrived.at[3]),
     ]
     for copy in copies:
         copy.start()
@@ -63,8 +71,9 @@
     coef = jnp.zeros(expert.shape, jnp.float32)
     for at in range(routes.shape[0]):
         coef += jnp.where(expert == named[at : at + 1, :], share[at : at + 1, :], 0.0)
-    packed[:, width:] = coef.T.astype(jnp.bfloat16)
+    packed[:, main : main + LANES] = coef.T.astype(jnp.bfloat16)
     copies[2].wait()
+    copies[3].wait()
 
 
 def pack(tokens, routes, route_weight):
@@ -75,24 +84,39 @@
         in_specs=[pl.BlockSpec(memory_space=pltpu.HBM)] * 3,
         out_specs=pl.BlockSpec(memory_space=pltpu.VMEM),
         out_shape=pltpu.VMEM((rows, width + LANES), jnp.bfloat16),
-        scratch_shapes=[pltpu.VMEM(a.shape, a.dtype) for a in arrays[1:]] + [pltpu.SemaphoreType.DMA((3,))],
+        scratch_shapes=[pltpu.VMEM(a.shape, a.dtype) for a in arrays[1:]] + [pltpu.SemaphoreType.DMA((4,))],
         compiler_params=pltpu.CompilerParams(vmem_limit_bytes=2 << 20),
     )(*arrays)
 
 
 def experts_kernel(ids, *refs, units, held):
-    blocks, weights, outs = refs[: 2 * units], refs[2 * units : -2 * units], refs[-2 * units :]
+    parts = 3 if SIDE_IN else 2
+    blocks, weights, outs = refs[: parts * units], refs[parts * units : -3 * units], refs[-3 * units :]
     width = weights[0].shape[0]
+    main = width - side_of(width)
     count = blocks[0].shape[0]
     lane = lax.broadcasted_iota(jnp.int32, (1, LANES), 1)
     repeat = max(1, LANES // (2 * units * count))
-    coefs = jnp.concatenate([block[:, width:] for block in blocks] * repeat, axis=0).astype(jnp.float32)
+    firsts = [blocks[parts * unit + at] for unit in range(units) for at in range(2)]
+    sides = [blocks[parts * unit + 2] for unit in range(units)] if SIDE_IN else None
+
+    def rows_of(start, size):
+        if start < main:
+            taken = [block[:, start : start + size] for block in firsts]
+        elif SIDE_IN:
+            taken = [block[:, start - main : start - main + size] for block in sides]
+        else:
+            taken = [block[:, start + LANES : start + LANES + size] for block in firsts]
+        return jnp.concatenate(taken * repeat, axis=0)
+
+    spans = pieces(0, main) + pieces(main, width)
+    coefs = jnp.concatenate([block[:, main : main + LANES] for block in firsts] * repeat, axis=0).astype(jnp.float32)
     hidden = []
     for at in range(held):
         w_gate, w_up, _ = weights[3 * at : 3 * at + 3]
         gate_vals = up_vals = None
-        for start, size in pieces(width):
-            rows = jnp.concatenate([block[:, start : start + size] for block in blocks] * repeat, axis=0)
+        for start, size in spans:
+            rows = rows_of(start, size)
             gate_part = jnp.dot(rows, w_gate[start : start + size, :], preferred_element_type=jnp.float32)
             up_part = jnp.dot(rows, w_up[start : start + size, :], preferred_element_type=jnp.float32)
             gate_vals = gate_part if gate_vals is None else gate_vals + gate_part
@@ -100,14 +124,20 @@
         mine = jnp.sum(jnp.where(lane == ids[at], coefs, 0.0), axis=1, keepdims=True)
         silu = gate_vals / (1.0 + jnp.exp(-gate_vals))
         hidden.append((silu * up_vals * mine).astype(jnp.bfloat16))
-    for start, size in pieces(width):
+    for start, size in spans:
         total = None
         for at, value in enumerate(hidden):
             w_down = weights[3 * at + 2]
             part = jnp.dot(value, w_down[:, start : start + size], preferred_element_type=jnp.float32)
             total = part if total is None else total + part
-        for at, out in enumerate(outs):
-            out[:, start : start + size] = total[at * count : (at + 1) * count].astype(out.dtype)
+        for unit in range(units):
+            kept, sent, side = outs[3 * unit : 3 * unit + 3]
+            own = total[2 * count * unit : 2 * count * (unit + 1)]
+            if start < main:
+                kept[:, start : start + size] = own[:count]
+                sent[:, start : start + size] = own[count:].astype(sent.dtype)
+            else:
+                side[:, start - main : start - main + size] = own.astype(side.dtype)
 
 
 def stage_kernel(*refs):
@@ -130,18 +160,24 @@
     )(*[pltpu.with_memory_space_constraint(w, pltpu.HBM) for w in weights])
 
 
-def run_experts(ids, blocks, weights):
+def run_experts(ids, units, blocks, weights):
     width = weights[0].shape[0]
+    side = side_of(width)
     rows = blocks[0].shape[0]
-    flops = 2 * rows * len(blocks) * sum(w.size for w in weights)
+    flops = 2 * 2 * rows * len(units) * sum(w.size for w in weights)
     whole = pl.BlockSpec(memory_space=pltpu.VMEM)
+    shapes = []
+    for unit in units:
+        shapes += [
+            jax.ShapeDtypeStruct((rows, width - side), jnp.float32),
+            jax.ShapeDtypeStruct((rows, width - side), jnp.bfloat16),
+            jax.ShapeDtypeStruct((2 * rows, side), jnp.bfloat16 if unit else jnp.float32),
+        ]
     return pl.pallas_call(
-        functools.partial(experts_kernel, units=len(blocks) // 2, held=len(weights) // 3),
+        functools.partial(experts_kernel, units=len(units), held=len(weights) // 3),
         in_specs=[pl.BlockSpec(memory_space=pltpu.SMEM)] + [whole] * (len(blocks) + len(weights)),
-        out_specs=(whole,) * len(blocks),
-        out_shape=tuple(
-            jax.ShapeDtypeStruct((rows, width), jnp.bfloat16 if at % 2 else jnp.float32) for at in range(len(blocks))
-        ),
+        out_specs=(whole,) * len(shapes),
+        out_shape=tuple(shapes),
         cost_estimate=pl.CostEstimate(flops=flops, bytes_accessed=0, transcendentals=0),
         compiler_params=pltpu.CompilerParams(vmem_limit_bytes=8 << 20),
     )(ids, *blocks, *weights)
@@ -157,7 +193,7 @@
 
 
 def layer(tokens, routes, route_weight, gate_weight, up_weight, down_weight):
-    row_count, _ = tokens.shape
+    row_count, model_width = tokens.shape
     nodes = lax.axis_size("node")
     layers = lax.axis_size("rail") // PLANE
     node = lax.axis_index("node")
@@ -169,26 +205,45 @@
     for count in range(nodes):
         held = (gate_weight[0, 0], up_weight[0, 0], down_weight[0, 0])
         weights += [send(w, node_shift(nodes, count)) for w in held] if count else held
-        weights[3 * count :] = stage(weights[3 * count :])
+        if count:
+            weights[3 * count :] = stage(weights[3 * count :])
     ids = jnp.stack([first_expert + (node - count) % nodes for count in range(nodes)])
 
     shifts = shifts_of(layers)
+    side = side_of(model_width)
+    main = model_width - side
     moved, blocks = {0: own}, {}
+    steps = {count: 1 if count <= layers // 2 else -1 for count in shifts}
     for count in shifts:
-        step = 1 if count <= layers // 2 else -1
-        moved[count] = send(moved[(count - step) % layers], layer_shift(layers, step))
+        source = moved[(count - steps[count]) % layers]
+        if SIDE_IN:
+            source = source[:, : main + LANES]
+        moved[count] = send(source, layer_shift(layers, steps[count]))
     for count, unit in moved.items():
         beside = send(unit, first_partner)
         near = jnp.concatenate([unit, beside], axis=0)
-        blocks[count] = (near, send(near, second_partner))
+        blocks[count] = [near, send(near, second_partner)]
+    if SIDE_IN:
+        blocks[0].append(jnp.concatenate([block[:, main + LANES :] for block in blocks[0]], axis=0))
+        for count in shifts:
+            source = blocks[(count - steps[count]) % layers][2]
+            blocks[count].append(send(source, layer_shift(layers, steps[count])))
     sums = {}
     for together in calls_of(layers):
-        outs = run_experts(ids, [block for unit in together for block in blocks[unit]], weights)
+        outs = run_experts(ids, together, [block for unit in together for block in blocks[unit]], weights)
         for at, unit in enumerate(together):
-            sums[unit] = outs[2 * at : 2 * at + 2]
+            sums[unit] = outs[3 * at : 3 * at + 3]
+    backs = [unit for call in calls_of(layers) for unit in call if unit]
+    arrived = [send(sums[count][2], layer_shift(layers, -count)) for count in backs]
     result = None
-    for count in [unit for call in calls_of(layers) for unit in call if unit] + [0]:
-        kept, sent = sums[count]
+    for count in backs + [0]:
+        kept, sent, own_side = sums[count]
+        if not count:
+            for piece in arrived:
+                own_side = own_side + piece.astype(jnp.float32)
+            kept = jnp.concatenate([kept, own_side[: kept.shape[0]]], axis=1)
+            sent = jnp.concatenate([sent, own_side[kept.shape[0] :].astype(jnp.bfloat16)], axis=1)
+            result = jnp.pad(result, ((0, 0), (0, side)))
         back = send(sent, second_partner)
         out = kept + back
         back = send(out[row_count:].astype(jnp.bfloat16), first_partner)

time: 113 us -> 112 us (level)
  waiting for transfers between devices: 61.5 us -> 51 us
  starting transfers between devices: 30.2 us -> 39.7 us
  Pallas kernels: 17 us -> 13.4 us
  local copies, waits for them, and re-layouts: 2.13 us -> 5.47 us
    ppermute x25 -> x28, waiting for transfers between devices: 61.5 us -> 51 us  [send(): return lax.ppermute(block, ('rail', 'node'), route)]
    ppermute x25 -> x28, starting transfers between devices: 30.2 us -> 39.7 us  [send(): return lax.ppermute(block, ('rail', 'node'), route)]
    pallas_call x2 -> x1, Pallas kernels: 8.45 us -> 4.36 us  [stage(): pl.pallas_call(stage_kernel, in_specs=[pl.BlockSpec(memory_space=pltpu.HB...]
    unnamed x5 -> x13, local copies, waits for them, and re-layouts: 1.96 us -> 5.29 us
  transfers between devices with their start and end apart: 25 -> 28, of which waited for: 14 -> 12; matrix products, arithmetic and copies ran while one was open for 1% -> 1% of each run, Pallas kernels for 14% -> 11%
where the time goes in v5:
time: 112 us; the launch traced here: 111 us
  waiting for transfers between devices  51 us (46%)
  starting transfers between devices  39.7 us (35%)
  Pallas kernels  13.4 us (12%)
  local copies, waits for them, and re-layouts  5.47 us (5%)
  other arithmetic  1.53 us (1%)
    ppermute x28, waiting for transfers between devices, send(): return lax.ppermute(block, ('rail', 'node'), route)  51 us
    ppermute x28, starting transfers between devices, send(): return lax.ppermute(block, ('rail', 'node'), route)  39.7 us
    pallas_call x2, Pallas kernels, run_experts(): pl.pallas_call(functools.partial(experts_kernel, units=len(units), held=l...  8.06 us
    unnamed x13, local copies, waits for them, and re-layouts  5.29 us
    pallas_call x1, Pallas kernels, stage(): pl.pallas_call(stage_kernel, in_specs=[pl.BlockSpec(memory_space=pltpu.HB...  4.36 us
  transfers between devices with their start and end apart: 28, of which 12 were waited for; matrix products, arithmetic and copies ran while one was open for 1% of the time, Pallas kernels for 11%

profile of v5, /device:TPU:0, one launch (start us, length us, event | category | flops | bytes accessed | tf_op | source)
XLA Modules:
  0.0 111.4 jit_solution(18305975952251335356)
XLA Ops:
  0.0 1.0 shard_map.64
  1.0 3.0 %collective-permute-start.3 = (bf16[16,7296]{1,0:T(8,128)(2,1)S(1)}, bf16[16,7296]{1,0:T(8,128)(2,1)S(1)}, u32[]{:S(2)}, u32[]{:S(2)}) collective-permute-start(bf16[16,7296]{1,0:T(8,128)(2,1)S(1)} %shard_map.64), channel_id=1, source_target_pairs={{0,2},{1,5},{2,0},{3,7},{4,6},{5,1},{6,4},{7,3},{8,10},{9,13},{10,... | collective-permute-start | bytes 700424 | tf_op jit(solution)/shard_map/ppermute | solution.py:25
  4.0 1.6 %collective-permute-start = (bf16[16,7296]{1,0:T(8,128)(2,1)S(1)}, bf16[16,7296]{1,0:T(8,128)(2,1)S(1)}, u32[]{:S(2)}, u32[]{:S(2)}) collective-permute-start(bf16[16,7296]{1,0:T(8,128)(2,1)S(1)} %shard_map.64), channel_id=1, source_target_pairs={{0,8},{1,9},{2,10},{3,11},{4,12},{5,13},{6,14},{7,15},{8,16},{9,17... | collective-permute-start | bytes 700424 | tf_op jit(solution)/shard_map/ppermute | solution.py:25
  5.6 2.2 %collective-permute-start.14 = (bf16[16,7296]{1,0:T(8,128)(2,1)S(1)}, bf16[16,7296]{1,0:T(8,128)(2,1)S(1)}, u32[]{:S(2)}, u32[]{:S(2)}) collective-permute-start(bf16[16,7296]{1,0:T(8,128)(2,1)S(1)} %shard_map.64), channel_id=1, source_target_pairs={{0,24},{1,25},{2,26},{3,27},{4,28},{5,29},{6,30},{7,31},{8,0},{9,1... | collective-permute-start | bytes 700424 | tf_op jit(solution)/shard_map/ppermute | solution.py:25
  7.9 0.0 collective-permute-start.5
  7.9 0.5 collective-permute-start.6
  8.4 0.0 collective-permute-start.7
  8.4 6.0 %collective-permute-done = bf16[16,7296]{1,0:T(8,128)(2,1)S(1)} collective-permute-done((bf16[16,7296]{1,0:T(8,128)(2,1)S(1)}, bf16[16,7296]{1,0:T(8,128)(2,1)S(1)}, u32[]{:S(2)}, u32[]{:S(2)}) %collective-permute-start) | collective-permute-done | bytes 233504 | tf_op jit(solution)/shard_map/ppermute | solution.py:25
  14.4 1.5 %collective-permute-start.4 = (bf16[32,7296]{1,0:T(8,128)(2,1)S(1)}, bf16[32,7296]{1,0:T(8,128)(2,1)S(1)}, u32[]{:S(2)}, u32[]{:S(2)}) collective-permute-start(bf16[32,7296]{1,0:T(8,128)(2,1)S(1)} %pad_maximum_fusion.refs_2_), channel_id=1, source_target_pairs={{0,4},{1,3},{2,6},{3,1},{4,0},{5,7},{6,2},{7,5},{8,12},{9,11},{10,... | collective-permute-start | bytes 1400840 | tf_op jit(solution)/shard_map/ppermute | solution.py:25
  15.9 1.6 %collective-permute-done.14 = bf16[16,7296]{1,0:T(8,128)(2,1)S(1)} collective-permute-done((bf16[16,7296]{1,0:T(8,128)(2,1)S(1)}, bf16[16,7296]{1,0:T(8,128)(2,1)S(1)}, u32[]{:S(2)}, u32[]{:S(2)}) %collective-permute-start.14) | collective-permute-done | bytes 233504 | tf_op jit(solution)/shard_map/ppermute | solution.py:25
  17.5 1.1 %collective-permute-start.11 = (bf16[16,7296]{1,0:T(8,128)(2,1)S(1)}, bf16[16,7296]{1,0:T(8,128)(2,1)S(1)}, u32[]{:S(2)}, u32[]{:S(2)}) collective-permute-start(bf16[16,7296]{1,0:T(8,128)(2,1)S(1)} %collective-permute-done), channel_id=1, source_target_pairs={{0,8},{1,9},{2,10},{3,11},{4,12},{5,13},{6,14},{7,15},{8,16},{9,17... | collective-permute-start | bytes 700424 | tf_op jit(solution)/shard_map/ppermute | solution.py:25
  18.7 7.7 %collective-permute-done.11 = bf16[16,7296]{1,0:T(8,128)(2,1)S(1)} collective-permute-done((bf16[16,7296]{1,0:T(8,128)(2,1)S(1)}, bf16[16,7296]{1,0:T(8,128)(2,1)S(1)}, u32[]{:S(2)}, u32[]{:S(2)}) %collective-permute-start.11) | collective-permute-done | bytes 233504 | tf_op jit(solution)/shard_map/ppermute | solution.py:25
  26.4 1.5 %collective-permute-start.1 = (bf16[16,7296]{1,0:T(8,128)(2,1)S(1)}, bf16[16,7296]{1,0:T(8,128)(2,1)S(1)}, u32[]{:S(2)}, u32[]{:S(2)}) collective-permute-start(bf16[16,7296]{1,0:T(8,128)(2,1)S(1)} %collective-permute-done), channel_id=1, source_target_pairs={{0,2},{1,5},{2,0},{3,7},{4,6},{5,1},{6,4},{7,3},{8,10},{9,13},{10,... | collective-permute-start | bytes 700424 | tf_op jit(solution)/shard_map/ppermute | solution.py:25
  27.9 4.6 %collective-permute-done.1 = bf16[16,7296]{1,0:T(8,128)(2,1)S(1)} collective-permute-done((bf16[16,7296]{1,0:T(8,128)(2,1)S(1)}, bf16[16,7296]{1,0:T(8,128)(2,1)S(1)}, u32[]{:S(2)}, u32[]{:S(2)}) %collective-permute-start.1) | collective-permute-done | bytes 233504 | tf_op jit(solution)/shard_map/ppermute | solution.py:25
  32.4 1.5 %collective-permute-start.15 = (bf16[16,7296]{1,0:T(8,128)(2,1)S(1)}, bf16[16,7296]{1,0:T(8,128)(2,1)S(1)}, u32[]{:S(2)}, u32[]{:S(2)}) collective-permute-start(bf16[16,7296]{1,0:T(8,128)(2,1)S(1)} %collective-permute-done.14), channel_id=1, source_target_pairs={{0,2},{1,5},{2,0},{3,7},{4,6},{5,1},{6,4},{7,3},{8,10},{9,13},{10,... | collective-permute-start | bytes 700424 | tf_op jit(solution)/shard_map/ppermute | solution.py:25
  33.9 4.6 %collective-permute-done.15 = bf16[16,7296]{1,0:T(8,128)(2,1)S(1)} collective-permute-done((bf16[16,7296]{1,0:T(8,128)(2,1)S(1)}, bf16[16,7296]{1,0:T(8,128)(2,1)S(1)}, u32[]{:S(2)}, u32[]{:S(2)}) %collective-permute-start.15) | collective-permute-done | bytes 233504 | tf_op jit(solution)/shard_map/ppermute | solution.py:25
  38.5 1.5 %collective-permute-start.12 = (bf16[16,7296]{1,0:T(8,128)(2,1)S(1)}, bf16[16,7296]{1,0:T(8,128)(2,1)S(1)}, u32[]{:S(2)}, u32[]{:S(2)}) collective-permute-start(bf16[16,7296]{1,0:T(8,128)(2,1)S(1)} %collective-permute-done.11), channel_id=1, source_target_pairs={{0,2},{1,5},{2,0},{3,7},{4,6},{5,1},{6,4},{7,3},{8,10},{9,13},{10,... | collective-permute-start | bytes 700424 | tf_op jit(solution)/shard_map/ppermute | solution.py:25
  40.0 6.5 %collective-permute-done.12 = bf16[16,7296]{1,0:T(8,128)(2,1)S(1)} collective-permute-done((bf16[16,7296]{1,0:T(8,128)(2,1)S(1)}, bf16[16,7296]{1,0:T(8,128)(2,1)S(1)}, u32[]{:S(2)}, u32[]{:S(2)}) %collective-permute-start.12) | collective-permute-done | bytes 233504 | tf_op jit(solution)/shard_map/ppermute | solution.py:25
  46.5 0.6 collective-permute-start.2
  47.1 0.0 collective-permute-done.5.refs_0_
  47.2 1.5 %collective-permute-start.16 = (bf16[32,7296]{1,0:T(8,128)(2,1)S(1)}, bf16[32,7296]{1,0:T(8,128)(2,1)S(1)}, u32[]{:S(2)}, u32[]{:S(2)}) collective-permute-start(bf16[32,7296]{1,0:T(8,128)(2,1)S(1)} %constant_dynamic-update-slice_fusion.4.refs_2_), channel_id=1, source_target_pairs={{0,4},{1,3},{2,6},{3,1},{4,0},{5,7},{6,2},{7,5},{8,12},{9,11},{10,... | collective-permute-start | bytes 1400840 | tf_op jit(solution)/shard_map/ppermute | solution.py:25
  48.7 0.3 copy-done.3
  49.0 0.0 collective-permute-done.6.refs_1_
  49.0 1.9 %copy-done.4 = bf16[7168,256]{1,0:T(8,128)(2,1)} copy-done((bf16[7168,256]{1,0:T(8,128)(2,1)}, bf16[7168,256]{1,0:T(8,128)(2,1)S(1)}, u32[]{:S(2)}) %copy-start.4) | copy-done | bytes 3670040
  50.9 1.4 %collective-permute-start.13 = (bf16[32,7296]{1,0:T(8,128)(2,1)S(1)}, bf16[32,7296]{1,0:T(8,128)(2,1)S(1)}, u32[]{:S(2)}, u32[]{:S(2)}) collective-permute-start(bf16[32,7296]{1,0:T(8,128)(2,1)S(1)} %constant_dynamic-update-slice_fusion.2.refs_0_), channel_id=1, source_target_pairs={{0,4},{1,3},{2,6},{3,1},{4,0},{5,7},{6,2},{7,5},{8,12},{9,11},{10,... | collective-permute-start | bytes 1400840 | tf_op jit(solution)/shard_map/ppermute | solution.py:25
  52.3 0.1 pad_add_fusion.ids
  52.4 0.0 collective-permute-done.7.refs_2_
  52.4 4.4 %shard_map.65 = (bf16[7168,256]{1,0:T(8,128)(2,1)S(1)}, bf16[7168,256]{1,0:T(8,128)(2,1)S(1)}, bf16[256,7168]{1,0:T(8,128)(2,1)S(1)}) custom-call(bf16[7168,256]{1,0:T(8,128)(2,1)} %copy-done.3, bf16[7168,256]{1,0:T(8,128)(2,1)} %copy-done.4, bf16[256,7168]{1,0:T(8,128)(2,1)} %collective-permute-done.7.refs_2_), custom_call_target="tpu_custom_call" | custom-call | tf_op jit(solution)/shard_map/pallas_call | solution.py:153
  56.8 0.0 collective-permute-done.2.refs_1_
  56.8 0.8 copy-done
  57.6 1.1 %copy-done.1 = bf16[1,1,7168,256]{3,2,1,0:T(8,128)(2,1)S(1)} copy-done((bf16[1,1,7168,256]{3,2,1,0:T(8,128)(2,1)S(1)}, bf16[1,1,7168,256]{3,2,1,0:T(8,128)(2,1)}, u32[]{:S(2)}) %copy-start.1) | copy-done | bytes 3670040
  58.8 1.0 copy-done.2
  59.8 4.3 %shard_map.66 = (f32[32,6144]{1,0:T(8,128)S(1)}, bf16[32,6144]{1,0:T(8,128)(2,1)S(1)}, bf16[64,1024]{1,0:T(8,128)(2,1)S(1)}, f32[32,6144]{1,0:T(8,128)S(1)}, bf1...) custom-call(s32[2]{0:T(128)S(1)} %pad_add_fusion.ids, bf16[32,7296]{1,0:T(8,128)(2,1)S(1)} %constant_dynamic-update-slice_fusion.refs_0_, ...), custom_call_target="tpu_custom_call" | custom-call | flops 2818572288 | tf_op jit(solution)/shard_map/pallas_call | solution.py:176
  64.1 0.5 collective-permute-start.23
  64.6 0.0 collective-permute-done.16.refs_3_
  64.6 0.5 collective-permute-done.13.refs_1_
  65.1 3.8 %shard_map.67 = (f32[32,6144]{1,0:T(8,128)S(1)}, bf16[32,6144]{1,0:T(8,128)(2,1)S(1)}, bf16[64,1024]{1,0:T(8,128)(2,1)S(1)}, f32[32,6144]{1,0:T(8,128)S(1)}, bf1...) custom-call(s32[2]{0:T(128)S(1)} %pad_add_fusion.ids, ...), custom_call_target="tpu_custom_call" | custom-call | flops 2818572288 | tf_op jit(solution)/shard_map/pallas_call | solution.py:176
  68.9 0.1 collective-permute-start.24
  69.0 1.1 %collective-permute-start.25 = (bf16[64,1024]{1,0:T(8,128)(2,1)S(1)}, bf16[64,1024]{1,0:T(8,128)(2,1)S(1)}, u32[]{:S(2)}, u32[]{:S(2)}) collective-permute-start(bf16[64,1024]{1,0:T(8,128)(2,1)S(1)} %get-tuple-element.33), channel_id=1, source_target_pairs={{0,8},{1,9},{2,10},{3,11},{4,12},{5,13},{6,14},{7,15},{8,16},{9,17... | collective-permute-start | bytes 393224 | tf_op jit(solution)/shard_map/ppermute | solution.py:25
  70.1 1.6 %collective-permute-start.8 = (bf16[32,6144]{1,0:T(8,128)(2,1)S(1)}, bf16[32,6144]{1,0:T(8,128)(2,1)S(1)}, u32[]{:S(2)}, u32[]{:S(2)}) collective-permute-start(bf16[32,6144]{1,0:T(8,128)(2,1)S(1)} %get-tuple-element.24), channel_id=1, source_target_pairs={{0,4},{1,3},{2,6},{3,1},{4,0},{5,7},{6,2},{7,5},{8,12},{9,11},{10,... | collective-permute-start | bytes 1179656 | tf_op jit(solution)/shard_map/ppermute | solution.py:25
  71.7 0.5 collective-permute-start.17
  72.1 1.6 %collective-permute-start.20 = (bf16[32,6144]{1,0:T(8,128)(2,1)S(1)}, bf16[32,6144]{1,0:T(8,128)(2,1)S(1)}, u32[]{:S(2)}, u32[]{:S(2)}) collective-permute-start(bf16[32,6144]{1,0:T(8,128)(2,1)S(1)} %get-tuple-element.28), channel_id=1, source_target_pairs={{0,4},{1,3},{2,6},{3,1},{4,0},{5,7},{6,2},{7,5},{8,12},{9,11},{10,... | collective-permute-start | bytes 1179656 | tf_op jit(solution)/shard_map/ppermute | solution.py:25
  73.7 3.9 %collective-permute-done.24 = bf16[64,1024]{1,0:T(8,128)(2,1)S(1)} collective-permute-done((bf16[64,1024]{1,0:T(8,128)(2,1)S(1)}, bf16[64,1024]{1,0:T(8,128)(2,1)S(1)}, u32[]{:S(2)}, u32[]{:S(2)}) %collective-permute-start.24) | collective-permute-done | bytes 131104 | tf_op jit(solution)/shard_map/ppermute | solution.py:25
  77.6 0.0 collective-permute-done.25
  77.6 0.1 convert_add_fusion.4
  77.8 1.2 %collective-permute-start.26 = (bf16[32,7168]{1,0:T(8,128)(2,1)S(1)}, bf16[32,7168]{1,0:T(8,128)(2,1)S(1)}, u32[]{:S(2)}, u32[]{:S(2)}) collective-permute-start(bf16[32,7168]{1,0:T(8,128)(2,1)S(1)} %pad_maximum_fusion.1), channel_id=1, source_target_pairs={{0,4},{1,3},{2,6},{3,1},{4,0},{5,7},{6,2},{7,5},{8,12},{9,11},{10,... | collective-permute-start | bytes 1376264 | tf_op jit(solution)/shard_map/ppermute | solution.py:25
  79.0 0.9 collective-permute-done.8
  79.9 0.1 convert_add_fusion.2
  80.0 2.7 %collective-permute-start.9 = (bf16[16,6144]{1,0:T(8,128)(2,1)S(1)}, bf16[16,6144]{1,0:T(8,128)(2,1)S(1)}, u32[]{:S(2)}, u32[]{:S(2)}) collective-permute-start(bf16[16,6144]{1,0:T(8,128)(2,1)S(1)} %slice.77), channel_id=1, source_target_pairs={{0,2},{1,5},{2,0},{3,7},{4,6},{5,1},{6,4},{7,3},{8,10},{9,13},{10,... | collective-permute-start | bytes 589832 | tf_op jit(solution)/shard_map/ppermute | solution.py:25
  82.6 5.5 %collective-permute-done.17 = bf16[32,6144]{1,0:T(8,128)(2,1)S(1)} collective-permute-done((bf16[32,6144]{1,0:T(8,128)(2,1)S(1)}, bf16[32,6144]{1,0:T(8,128)(2,1)S(1)}, u32[]{:S(2)}, u32[]{:S(2)}) %collective-permute-start.17) | collective-permute-done | bytes 393248 | tf_op jit(solution)/shard_map/ppermute | solution.py:25
  88.1 0.1 convert_add_fusion.1
  88.3 1.8 %collective-permute-start.18 = (bf16[16,6144]{1,0:T(8,128)(2,1)S(1)}, bf16[16,6144]{1,0:T(8,128)(2,1)S(1)}, u32[]{:S(2)}, u32[]{:S(2)}) collective-permute-start(bf16[16,6144]{1,0:T(8,128)(2,1)S(1)} %slice.76), channel_id=1, source_target_pairs={{0,2},{1,5},{2,0},{3,7},{4,6},{5,1},{6,4},{7,3},{8,10},{9,13},{10,... | collective-permute-start | bytes 589832 | tf_op jit(solution)/shard_map/ppermute | solution.py:25
  90.1 3.6 %collective-permute-done.20 = bf16[32,6144]{1,0:T(8,128)(2,1)S(1)} collective-permute-done((bf16[32,6144]{1,0:T(8,128)(2,1)S(1)}, bf16[32,6144]{1,0:T(8,128)(2,1)S(1)}, u32[]{:S(2)}, u32[]{:S(2)}) %collective-permute-start.20) | collective-permute-done | bytes 393248 | tf_op jit(solution)/shard_map/ppermute | solution.py:25
  93.7 0.1 convert_add_fusion
  93.8 1.7 %collective-permute-start.21 = (bf16[16,6144]{1,0:T(8,128)(2,1)S(1)}, bf16[16,6144]{1,0:T(8,128)(2,1)S(1)}, u32[]{:S(2)}, u32[]{:S(2)}) collective-permute-start(bf16[16,6144]{1,0:T(8,128)(2,1)S(1)} %slice.75), channel_id=1, source_target_pairs={{0,2},{1,5},{2,0},{3,7},{4,6},{5,1},{6,4},{7,3},{8,10},{9,13},{10,... | collective-permute-start | bytes 589832 | tf_op jit(solution)/shard_map/ppermute | solution.py:25
  95.5 0.0 collective-permute-done.9
  95.6 2.7 %collective-permute-start.10 = (bf16[16,6144]{1,0:T(8,128)(2,1)S(1)}, bf16[16,6144]{1,0:T(8,128)(2,1)S(1)}, u32[]{:S(2)}, u32[]{:S(2)}) collective-permute-start(bf16[16,6144]{1,0:T(8,128)(2,1)S(1)} %fusion.4), channel_id=1, source_target_pairs={{0,24},{1,25},{2,26},{3,27},{4,28},{5,29},{6,30},{7,31},{8,0},{9,1... | collective-permute-start | bytes 589832 | tf_op jit(solution)/shard_map/ppermute | solution.py:25
  98.3 2.3 %collective-permute-start.19 = (bf16[16,6144]{1,0:T(8,128)(2,1)S(1)}, bf16[16,6144]{1,0:T(8,128)(2,1)S(1)}, u32[]{:S(2)}, u32[]{:S(2)}) collective-permute-start(bf16[16,6144]{1,0:T(8,128)(2,1)S(1)} %fusion.3), channel_id=1, source_target_pairs={{0,16},{1,17},{2,18},{3,19},{4,20},{5,21},{6,22},{7,23},{8,24},{9,... | collective-permute-start | bytes 589832 | tf_op jit(solution)/shard_map/ppermute | solution.py:25
  100.7 2.5 %collective-permute-start.22 = (bf16[16,6144]{1,0:T(8,128)(2,1)S(1)}, bf16[16,6144]{1,0:T(8,128)(2,1)S(1)}, u32[]{:S(2)}, u32[]{:S(2)}) collective-permute-start(bf16[16,6144]{1,0:T(8,128)(2,1)S(1)} %fusion.2), channel_id=1, source_target_pairs={{0,8},{1,9},{2,10},{3,11},{4,12},{5,13},{6,14},{7,15},{8,16},{9,17... | collective-permute-start | bytes 589832 | tf_op jit(solution)/shard_map/ppermute | solution.py:25
  103.3 0.1 maximum_add_fusion
  103.4 1.6 %collective-permute-start.27 = (bf16[16,7168]{1,0:T(8,128)(2,1)S(1)}, bf16[16,7168]{1,0:T(8,128)(2,1)S(1)}, u32[]{:S(2)}, u32[]{:S(2)}) collective-permute-start(bf16[16,7168]{1,0:T(8,128)(2,1)S(1)} %slice.74), channel_id=1, source_target_pairs={{0,2},{1,5},{2,0},{3,7},{4,6},{5,1},{6,4},{7,3},{8,10},{9,13},{10,... | collective-permute-start | bytes 688136 | tf_op jit(solution)/shard_map/ppermute | solution.py:25
  104.9 5.6 %collective-permute-done.19 = bf16[16,6144]{1,0:T(8,128)(2,1)S(1)} collective-permute-done((bf16[16,6144]{1,0:T(8,128)(2,1)S(1)}, bf16[16,6144]{1,0:T(8,128)(2,1)S(1)}, u32[]{:S(2)}, u32[]{:S(2)}) %collective-permute-start.19) | collective-permute-done | bytes 196640 | tf_op jit(solution)/shard_map/ppermute | solution.py:25
  110.5 0.1 convert_add_fusion.3
  110.6 0.8 fusion.1
  (31 shorter events, 0.5 us)
Async XLA Ops:
  1.0 7.4 %collective-permute-start.3 = (bf16[16,7296]{1,0:T(8,128)(2,1)S(1)}, bf16[16,7296]{1,0:T(8,128)(2,1)S(1)}, u32[]{:S(2)}, u32[]{:S(2)}) collective-permute-start(bf16[16,7296]{1,0:T(8,128)(2,1)S(1)} %shard_map.64), channel_id=1, source_target_pairs={{0,2},{1,5},{2,0},{3,7},{4,6},{5,1},{6,4},{7,3},{8,10},{9,13},{10,... | collective-permute-start | bytes 700424 | tf_op jit(solution)/shard_map/ppermute | solution.py:25
  4.0 10.4 %collective-permute-start = (bf16[16,7296]{1,0:T(8,128)(2,1)S(1)}, bf16[16,7296]{1,0:T(8,128)(2,1)S(1)}, u32[]{:S(2)}, u32[]{:S(2)}) collective-permute-start(bf16[16,7296]{1,0:T(8,128)(2,1)S(1)} %shard_map.64), channel_id=1, source_target_pairs={{0,8},{1,9},{2,10},{3,11},{4,12},{5,13},{6,14},{7,15},{8,16},{9,17... | collective-permute-start | bytes 700424 | tf_op jit(solution)/shard_map/ppermute | solution.py:25
  5.6 11.9 %collective-permute-start.14 = (bf16[16,7296]{1,0:T(8,128)(2,1)S(1)}, bf16[16,7296]{1,0:T(8,128)(2,1)S(1)}, u32[]{:S(2)}, u32[]{:S(2)}) collective-permute-start(bf16[16,7296]{1,0:T(8,128)(2,1)S(1)} %shard_map.64), channel_id=1, source_target_pairs={{0,24},{1,25},{2,26},{3,27},{4,28},{5,29},{6,30},{7,31},{8,0},{9,1... | collective-permute-start | bytes 700424 | tf_op jit(solution)/shard_map/ppermute | solution.py:25
  7.9 39.3 %collective-permute-start.5 = (bf16[7168,256]{1,0:T(8,128)(2,1)}, bf16[7168,256]{1,0:T(8,128)(2,1)S(1)}, u32[]{:S(2)}, u32[]{:S(2)}) collective-permute-start(bf16[7168,256]{1,0:T(8,128)(2,1)} %bitcast.7), channel_id=1, source_target_pairs={{0,1},{1,0},{2,3},{3,2},{4,5},{5,4},{6,7},{7,6},{8,9},{9,8},{10,11... | collective-permute-start | bytes 11010056 | tf_op jit(solution)/shard_map/ppermute | solution.py:25
  7.9 41.1 %collective-permute-start.6 = (bf16[7168,256]{1,0:T(8,128)(2,1)}, bf16[7168,256]{1,0:T(8,128)(2,1)S(1)}, u32[]{:S(2)}, u32[]{:S(2)}) collective-permute-start(bf16[7168,256]{1,0:T(8,128)(2,1)} %bitcast.10), channel_id=1, source_target_pairs={{0,1},{1,0},{2,3},{3,2},{4,5},{5,4},{6,7},{7,6},{8,9},{9,8},{10,11... | collective-permute-start | bytes 11010056 | tf_op jit(solution)/shard_map/ppermute | solution.py:25
  8.4 44.0 %collective-permute-start.7 = (bf16[256,7168]{1,0:T(8,128)(2,1)}, bf16[256,7168]{1,0:T(8,128)(2,1)}, u32[]{:S(2)}, u32[]{:S(2)}) collective-permute-start(bf16[256,7168]{1,0:T(8,128)(2,1)} %bitcast.13), channel_id=1, source_target_pairs={{0,1},{1,0},{2,3},{3,2},{4,5},{5,4},{6,7},{7,6},{8,9},{9,8},{10,11... | collective-permute-start | bytes 11010056 | tf_op jit(solution)/shard_map/ppermute | solution.py:25
  14.4 42.4 %collective-permute-start.4 = (bf16[32,7296]{1,0:T(8,128)(2,1)S(1)}, bf16[32,7296]{1,0:T(8,128)(2,1)S(1)}, u32[]{:S(2)}, u32[]{:S(2)}) collective-permute-start(bf16[32,7296]{1,0:T(8,128)(2,1)S(1)} %pad_maximum_fusion.refs_2_), channel_id=1, source_target_pairs={{0,4},{1,3},{2,6},{3,1},{4,0},{5,7},{6,2},{7,5},{8,12},{9,11},{10,... | collective-permute-start | bytes 1400840 | tf_op jit(solution)/shard_map/ppermute | solution.py:25
  17.5 8.8 %collective-permute-start.11 = (bf16[16,7296]{1,0:T(8,128)(2,1)S(1)}, bf16[16,7296]{1,0:T(8,128)(2,1)S(1)}, u32[]{:S(2)}, u32[]{:S(2)}) collective-permute-start(bf16[16,7296]{1,0:T(8,128)(2,1)S(1)} %collective-permute-done), channel_id=1, source_target_pairs={{0,8},{1,9},{2,10},{3,11},{4,12},{5,13},{6,14},{7,15},{8,16},{9,17... | collective-permute-start | bytes 700424 | tf_op jit(solution)/shard_map/ppermute | solution.py:25
  26.4 6.1 %collective-permute-start.1 = (bf16[16,7296]{1,0:T(8,128)(2,1)S(1)}, bf16[16,7296]{1,0:T(8,128)(2,1)S(1)}, u32[]{:S(2)}, u32[]{:S(2)}) collective-permute-start(bf16[16,7296]{1,0:T(8,128)(2,1)S(1)} %collective-permute-done), channel_id=1, source_target_pairs={{0,2},{1,5},{2,0},{3,7},{4,6},{5,1},{6,4},{7,3},{8,10},{9,13},{10,... | collective-permute-start | bytes 700424 | tf_op jit(solution)/shard_map/ppermute | solution.py:25
  32.4 6.1 %collective-permute-start.15 = (bf16[16,7296]{1,0:T(8,128)(2,1)S(1)}, bf16[16,7296]{1,0:T(8,128)(2,1)S(1)}, u32[]{:S(2)}, u32[]{:S(2)}) collective-permute-start(bf16[16,7296]{1,0:T(8,128)(2,1)S(1)} %collective-permute-done.14), channel_id=1, source_target_pairs={{0,2},{1,5},{2,0},{3,7},{4,6},{5,1},{6,4},{7,3},{8,10},{9,13},{10,... | collective-permute-start | bytes 700424 | tf_op jit(solution)/shard_map/ppermute | solution.py:25
  38.5 8.0 %collective-permute-start.12 = (bf16[16,7296]{1,0:T(8,128)(2,1)S(1)}, bf16[16,7296]{1,0:T(8,128)(2,1)S(1)}, u32[]{:S(2)}, u32[]{:S(2)}) collective-permute-start(bf16[16,7296]{1,0:T(8,128)(2,1)S(1)} %collective-permute-done.11), channel_id=1, source_target_pairs={{0,2},{1,5},{2,0},{3,7},{4,6},{5,1},{6,4},{7,3},{8,10},{9,13},{10,... | collective-permute-start | bytes 700424 | tf_op jit(solution)/shard_map/ppermute | solution.py:25
  46.5 10.3 %collective-permute-start.2 = (bf16[32,7296]{1,0:T(8,128)(2,1)S(1)}, bf16[32,7296]{1,0:T(8,128)(2,1)}, u32[]{:S(2)}, u32[]{:S(2)}) collective-permute-start(bf16[32,7296]{1,0:T(8,128)(2,1)S(1)} %constant_dynamic-update-slice_fusion.refs_0_), channel_id=1, source_target_pairs={{0,4},{1,3},{2,6},{3,1},{4,0},{5,7},{6,2},{7,5},{8,12},{9,11},{10,... | collective-permute-start | bytes 1400840 | tf_op jit(solution)/shard_map/ppermute | solution.py:25
  47.2 1.8 %copy-start.3 = (bf16[7168,256]{1,0:T(8,128)(2,1)}, bf16[7168,256]{1,0:T(8,128)(2,1)S(1)}, u32[]{:S(2)}) copy-start(bf16[7168,256]{1,0:T(8,128)(2,1)S(1)} %collective-permute-done.5.refs_0_) | copy-start | bytes 11010052
  47.2 17.4 %collective-permute-start.16 = (bf16[32,7296]{1,0:T(8,128)(2,1)S(1)}, bf16[32,7296]{1,0:T(8,128)(2,1)S(1)}, u32[]{:S(2)}, u32[]{:S(2)}) collective-permute-start(bf16[32,7296]{1,0:T(8,128)(2,1)S(1)} %constant_dynamic-update-slice_fusion.4.refs_2_), channel_id=1, source_target_pairs={{0,4},{1,3},{2,6},{3,1},{4,0},{5,7},{6,2},{7,5},{8,12},{9,11},{10,... | collective-permute-start | bytes 1400840 | tf_op jit(solution)/shard_map/ppermute | solution.py:25
  49.0 1.9 %copy-start.4 = (bf16[7168,256]{1,0:T(8,128)(2,1)}, bf16[7168,256]{1,0:T(8,128)(2,1)S(1)}, u32[]{:S(2)}) copy-start(bf16[7168,256]{1,0:T(8,128)(2,1)S(1)} %collective-permute-done.6.refs_1_) | copy-start | bytes 11010052
  50.9 14.2 %collective-permute-start.13 = (bf16[32,7296]{1,0:T(8,128)(2,1)S(1)}, bf16[32,7296]{1,0:T(8,128)(2,1)S(1)}, u32[]{:S(2)}, u32[]{:S(2)}) collective-permute-start(bf16[32,7296]{1,0:T(8,128)(2,1)S(1)} %constant_dynamic-update-slice_fusion.2.refs_0_), channel_id=1, source_target_pairs={{0,4},{1,3},{2,6},{3,1},{4,0},{5,7},{6,2},{7,5},{8,12},{9,11},{10,... | collective-permute-start | bytes 1400840 | tf_op jit(solution)/shard_map/ppermute | solution.py:25
  52.4 5.2 %copy-start = (bf16[1,1,7168,256]{3,2,1,0:T(8,128)(2,1)S(1)}, bf16[1,1,7168,256]{3,2,1,0:T(8,128)(2,1)}, u32[]{:S(2)}) copy-start(bf16[1,1,7168,256]{3,2,1,0:T(8,128)(2,1)} %param.9) | copy-start | bytes 11010052
  52.4 6.3 %copy-start.1 = (bf16[1,1,7168,256]{3,2,1,0:T(8,128)(2,1)S(1)}, bf16[1,1,7168,256]{3,2,1,0:T(8,128)(2,1)}, u32[]{:S(2)}) copy-start(bf16[1,1,7168,256]{3,2,1,0:T(8,128)(2,1)} %param.10) | copy-start | bytes 11010052
  52.4 7.4 %copy-start.2 = (bf16[1,1,256,7168]{3,2,1,0:T(8,128)(2,1)S(1)}, bf16[1,1,256,7168]{3,2,1,0:T(8,128)(2,1)}, u32[]{:S(2)}) copy-start(bf16[1,1,256,7168]{3,2,1,0:T(8,128)(2,1)} %param.11) | copy-start | bytes 11010052
  64.1 8.0 %collective-permute-start.23 = (bf16[64,1024]{1,0:T(8,128)(2,1)S(1)}, bf16[64,1024]{1,0:T(8,128)(2,1)S(1)}, u32[]{:S(2)}, u32[]{:S(2)}) collective-permute-start(bf16[64,1024]{1,0:T(8,128)(2,1)S(1)} %get-tuple-element.31), channel_id=1, source_target_pairs={{0,24},{1,25},{2,26},{3,27},{4,28},{5,29},{6,30},{7,31},{8,0},{9,1... | collective-permute-start | bytes 393224 | tf_op jit(solution)/shard_map/ppermute | solution.py:25
  68.9 8.7 %collective-permute-start.24 = (bf16[64,1024]{1,0:T(8,128)(2,1)S(1)}, bf16[64,1024]{1,0:T(8,128)(2,1)S(1)}, u32[]{:S(2)}, u32[]{:S(2)}) collective-permute-start(bf16[64,1024]{1,0:T(8,128)(2,1)S(1)} %get-tuple-element.32), channel_id=1, source_target_pairs={{0,16},{1,17},{2,18},{3,19},{4,20},{5,21},{6,22},{7,23},{8,24},{9,... | collective-permute-start | bytes 393224 | tf_op jit(solution)/shard_map/ppermute | solution.py:25
  69.0 8.7 %collective-permute-start.25 = (bf16[64,1024]{1,0:T(8,128)(2,1)S(1)}, bf16[64,1024]{1,0:T(8,128)(2,1)S(1)}, u32[]{:S(2)}, u32[]{:S(2)}) collective-permute-start(bf16[64,1024]{1,0:T(8,128)(2,1)S(1)} %get-tuple-element.33), channel_id=1, source_target_pairs={{0,8},{1,9},{2,10},{3,11},{4,12},{5,13},{6,14},{7,15},{8,16},{9,17... | collective-permute-start | bytes 393224 | tf_op jit(solution)/shard_map/ppermute | solution.py:25
  70.1 9.8 %collective-permute-start.8 = (bf16[32,6144]{1,0:T(8,128)(2,1)S(1)}, bf16[32,6144]{1,0:T(8,128)(2,1)S(1)}, u32[]{:S(2)}, u32[]{:S(2)}) collective-permute-start(bf16[32,6144]{1,0:T(8,128)(2,1)S(1)} %get-tuple-element.24), channel_id=1, source_target_pairs={{0,4},{1,3},{2,6},{3,1},{4,0},{5,7},{6,2},{7,5},{8,12},{9,11},{10,... | collective-permute-start | bytes 1179656 | tf_op jit(solution)/shard_map/ppermute | solution.py:25
  71.7 16.5 %collective-permute-start.17 = (bf16[32,6144]{1,0:T(8,128)(2,1)S(1)}, bf16[32,6144]{1,0:T(8,128)(2,1)S(1)}, u32[]{:S(2)}, u32[]{:S(2)}) collective-permute-start(bf16[32,6144]{1,0:T(8,128)(2,1)S(1)} %get-tuple-element.26), channel_id=1, source_target_pairs={{0,4},{1,3},{2,6},{3,1},{4,0},{5,7},{6,2},{7,5},{8,12},{9,11},{10,... | collective-permute-start | bytes 1179656 | tf_op jit(solution)/shard_map/ppermute | solution.py:25
  72.1 21.6 %collective-permute-start.20 = (bf16[32,6144]{1,0:T(8,128)(2,1)S(1)}, bf16[32,6144]{1,0:T(8,128)(2,1)S(1)}, u32[]{:S(2)}, u32[]{:S(2)}) collective-permute-start(bf16[32,6144]{1,0:T(8,128)(2,1)S(1)} %get-tuple-element.28), channel_id=1, source_target_pairs={{0,4},{1,3},{2,6},{3,1},{4,0},{5,7},{6,2},{7,5},{8,12},{9,11},{10,... | collective-permute-start | bytes 1179656 | tf_op jit(solution)/shard_map/ppermute | solution.py:25
  77.8 25.5 %collective-permute-start.26 = (bf16[32,7168]{1,0:T(8,128)(2,1)S(1)}, bf16[32,7168]{1,0:T(8,128)(2,1)S(1)}, u32[]{:S(2)}, u32[]{:S(2)}) collective-permute-start(bf16[32,7168]{1,0:T(8,128)(2,1)S(1)} %pad_maximum_fusion.1), channel_id=1, source_target_pairs={{0,4},{1,3},{2,6},{3,1},{4,0},{5,7},{6,2},{7,5},{8,12},{9,11},{10,... | collective-permute-start | bytes 1376264 | tf_op jit(solution)/shard_map/ppermute | solution.py:25
  80.0 15.5 %collective-permute-start.9 = (bf16[16,6144]{1,0:T(8,128)(2,1)S(1)}, bf16[16,6144]{1,0:T(8,128)(2,1)S(1)}, u32[]{:S(2)}, u32[]{:S(2)}) collective-permute-start(bf16[16,6144]{1,0:T(8,128)(2,1)S(1)} %slice.77), channel_id=1, source_target_pairs={{0,2},{1,5},{2,0},{3,7},{4,6},{5,1},{6,4},{7,3},{8,10},{9,13},{10,... | collective-permute-start | bytes 589832 | tf_op jit(solution)/shard_map/ppermute | solution.py:25
  88.3 10.0 %collective-permute-start.18 = (bf16[16,6144]{1,0:T(8,128)(2,1)S(1)}, bf16[16,6144]{1,0:T(8,128)(2,1)S(1)}, u32[]{:S(2)}, u32[]{:S(2)}) collective-permute-start(bf16[16,6144]{1,0:T(8,128)(2,1)S(1)} %slice.76), channel_id=1, source_target_pairs={{0,2},{1,5},{2,0},{3,7},{4,6},{5,1},{6,4},{7,3},{8,10},{9,13},{10,... | collective-permute-start | bytes 589832 | tf_op jit(solution)/shard_map/ppermute | solution.py:25
  93.8 6.8 %collective-permute-start.21 = (bf16[16,6144]{1,0:T(8,128)(2,1)S(1)}, bf16[16,6144]{1,0:T(8,128)(2,1)S(1)}, u32[]{:S(2)}, u32[]{:S(2)}) collective-permute-start(bf16[16,6144]{1,0:T(8,128)(2,1)S(1)} %slice.75), channel_id=1, source_target_pairs={{0,2},{1,5},{2,0},{3,7},{4,6},{5,1},{6,4},{7,3},{8,10},{9,13},{10,... | collective-permute-start | bytes 589832 | tf_op jit(solution)/shard_map/ppermute | solution.py:25
  95.6 9.3 %collective-permute-start.10 = (bf16[16,6144]{1,0:T(8,128)(2,1)S(1)}, bf16[16,6144]{1,0:T(8,128)(2,1)S(1)}, u32[]{:S(2)}, u32[]{:S(2)}) collective-permute-start(bf16[16,6144]{1,0:T(8,128)(2,1)S(1)} %fusion.4), channel_id=1, source_target_pairs={{0,24},{1,25},{2,26},{3,27},{4,28},{5,29},{6,30},{7,31},{8,0},{9,1... | collective-permute-start | bytes 589832 | tf_op jit(solution)/shard_map/ppermute | solution.py:25
  98.3 12.2 %collective-permute-start.19 = (bf16[16,6144]{1,0:T(8,128)(2,1)S(1)}, bf16[16,6144]{1,0:T(8,128)(2,1)S(1)}, u32[]{:S(2)}, u32[]{:S(2)}) collective-permute-start(bf16[16,6144]{1,0:T(8,128)(2,1)S(1)} %fusion.3), channel_id=1, source_target_pairs={{0,16},{1,17},{2,18},{3,19},{4,20},{5,21},{6,22},{7,23},{8,24},{9,... | collective-permute-start | bytes 589832 | tf_op jit(solution)/shard_map/ppermute | solution.py:25
  100.7 9.8 %collective-permute-start.22 = (bf16[16,6144]{1,0:T(8,128)(2,1)S(1)}, bf16[16,6144]{1,0:T(8,128)(2,1)S(1)}, u32[]{:S(2)}, u32[]{:S(2)}) collective-permute-start(bf16[16,6144]{1,0:T(8,128)(2,1)S(1)} %fusion.2), channel_id=1, source_target_pairs={{0,8},{1,9},{2,10},{3,11},{4,12},{5,13},{6,14},{7,15},{8,16},{9,17... | collective-permute-start | bytes 589832 | tf_op jit(solution)/shard_map/ppermute | solution.py:25
  103.4 7.2 %collective-permute-start.27 = (bf16[16,7168]{1,0:T(8,128)(2,1)S(1)}, bf16[16,7168]{1,0:T(8,128)(2,1)S(1)}, u32[]{:S(2)}, u32[]{:S(2)}) collective-permute-start(bf16[16,7168]{1,0:T(8,128)(2,1)S(1)} %slice.74), channel_id=1, source_target_pairs={{0,2},{1,5},{2,0},{3,7},{4,6},{5,1},{6,4},{7,3},{8,10},{9,13},{10,... | collective-permute-start | bytes 688136 | tf_op jit(solution)/shard_map/ppermute | solution.py:25
